TPU v7x, 32 devices: a whole 2x2x4 slice. The times are simulated.
32 devices in a mesh: fsdp: 4 (over y, x), ctx: 2 (over core), tp: 4 (over z).
Axes of the slice: x: 2, y: 2, z: 4, core: 2. Of those that a mesh axis runs over, the one named last changes fastest.
Arguments:
- tokens: bfloat16 [4, 1024, 2048], P('fsdp', 'ctx'), may hold values from -6 to 6
- cotangent: bfloat16 [4, 1024, 2048], P('fsdp', 'ctx'), may hold values from -6 to 6
- block_ids: int32 [4, 1024], P('fsdp'), may hold values from 0 to 3, never falling along the last dimension, each value on 1 to 384 neighbouring positions
- live_count: int32 [4], P('fsdp'), may hold values from 0 to 1, as said below
- first_gain: bfloat16 [2048], P(('fsdp', 'ctx')), may hold values from 0.25 to 1.75
- first_shift: bfloat16 [2048], P(('fsdp', 'ctx')), may hold values from -1.796875 to 1.796875
- query_weight: bfloat16 [2048, 2048], P(('fsdp', 'ctx'), 'tp'), may hold values from -0.125 to 0.125
- query_bias: bfloat16 [16, 128], P('tp', ('fsdp', 'ctx')), may hold values from -3 to 3
- key_weight: bfloat16 [2048, 2048], P(('fsdp', 'ctx'), 'tp'), may hold values from -0.125 to 0.125
- value_weight: bfloat16 [2048, 2048], P(('fsdp', 'ctx'), 'tp'), may hold values from -0.125 to 0.125
- value_bias: bfloat16 [16, 128], P('tp', ('fsdp', 'ctx')), may hold values from -3 to 3
- output_weight: bfloat16 [2048, 2048], P('tp', ('fsdp', 'ctx')), may hold values from -0.5 to 0.5
- output_bias: bfloat16 [2048], P(('fsdp', 'ctx')), may hold values from -1.796875 to 1.796875
- second_gain: bfloat16 [2048], P(('fsdp', 'ctx')), may hold values from 0.25 to 1.75
- second_shift: bfloat16 [2048], P(('fsdp', 'ctx')), may hold values from -1.796875 to 1.796875
- expand_weight: bfloat16 [2048, 8192], P(('fsdp', 'ctx'), 'tp'), may hold values from -0.125 to 0.125
- expand_bias: bfloat16 [16, 512], P('tp', ('fsdp', 'ctx')), may hold values from -3 to 3
- reduce_weight: bfloat16 [8192, 2048], P('tp', ('fsdp', 'ctx')), may hold values from -0.0625 to 0.0625
- reduce_bias: bfloat16 [2048], P(('fsdp', 'ctx')), may hold values from -1.796875 to 1.796875
Outputs:
- layer_out: bfloat16 [4, 1024, 2048], P('fsdp', 'ctx')
- tokens_grad: bfloat16 [4, 1024, 2048], P('fsdp', 'ctx')
- first_gain_grad: float32 [2048], P(('fsdp', 'ctx'))
- first_shift_grad: float32 [2048], P(('fsdp', 'ctx'))
- query_weight_grad: float32 [2048, 2048], P(('fsdp', 'ctx'), 'tp')
- query_bias_grad: float32 [16, 128], P('tp', ('fsdp', 'ctx'))
- key_weight_grad: float32 [2048, 2048], P(('fsdp', 'ctx'), 'tp')
- value_weight_grad: float32 [2048, 2048], P(('fsdp', 'ctx'), 'tp')
- value_bias_grad: float32 [16, 128], P('tp', ('fsdp', 'ctx'))
- output_weight_grad: float32 [2048, 2048], P('tp', ('fsdp', 'ctx'))
- output_bias_grad: float32 [2048], P(('fsdp', 'ctx'))
- second_gain_grad: float32 [2048], P(('fsdp', 'ctx'))
- second_shift_grad: float32 [2048], P(('fsdp', 'ctx'))
- expand_weight_grad: float32 [2048, 8192], P(('fsdp', 'ctx'), 'tp')
- expand_bias_grad: float32 [16, 512], P('tp', ('fsdp', 'ctx'))
- reduce_weight_grad: float32 [8192, 2048], P('tp', ('fsdp', 'ctx'))
- reduce_bias_grad: float32 [2048], P(('fsdp', 'ctx'))
Inputs may be any that keep to these rules, and one draw needn't show every extreme that they name: Index r of fsdp holds one sequence in its single slot if live_count[r] = 1 and none if live_count[r] = 0; at least one index holds a sequence and at least one holds none. `block_ids`: block numbers never fall along a sequence; a block holds 1 to 384 positions.
All inputs are finite; a program needn't handle non-finite values.
Results may differ from a plain program's by a relative error of at most 0.015.
Values may be sent and summed in bfloat16 or wider, within the bound.
A program may use at most 192 MiB of HBM per device.

v0:
```python
import math

import jax
import jax.numpy as jnp
from jax import lax
from jax.sharding import PartitionSpec as P

HD = 128


epsilon = 1e-05


def shifted(block, axis, distance):
    devices = range(lax.axis_size(axis))
    route = [((i - distance) % len(devices), i) for i in devices]
    return lax.ppermute(block, axis, route)


def norm_parts(values):
    center = values - jnp.mean(values, axis=-1, keepdims=True)
    spread = lax.rsqrt(jnp.mean(center * center, axis=-1, keepdims=True) + epsilon)
    return (center * spread, spread)


def norm_back(grad_normed, scaled, spread, gain):
    weighted = grad_normed * gain
    inner = (
        weighted
        - jnp.mean(weighted, axis=-1, keepdims=True)
        - scaled * jnp.mean(weighted * scaled, axis=-1, keepdims=True)
    )
    return (inner * spread, jnp.sum(grad_normed * scaled, axis=0), jnp.sum(grad_normed, axis=0))


def gelu_exact(values):
    return 0.5 * values * (1.0 + lax.erf(values * (1.0 / math.sqrt(2.0))))


def masked_scores(queries, keys, query_ids, key_ids, scale):
    scores = jnp.einsum("qhd,khd->hqk", queries, keys, preferred_element_type=jnp.float32) * scale
    allowed = key_ids[None, None, :] <= query_ids[None, :, None]
    return jnp.where(allowed, scores, -1e30)


def attend_forward(queries, keys, values, query_ids, key_ids, scale):
    scores = masked_scores(queries, keys, query_ids, key_ids, scale)
    top = jnp.max(scores, axis=-1, keepdims=True)
    weights = jnp.exp(scores - top)
    total = jnp.sum(weights, axis=-1, keepdims=True)
    probs_low = (weights / total).astype(jnp.bfloat16)
    context = jnp.einsum("hqk,khd->qhd", probs_low, values, preferred_element_type=jnp.float32)
    return (context, top + jnp.log(total))


def attend_backward(queries, keys, values, query_ids, key_ids, log_total, grad_context, scale):
    scores = masked_scores(queries, keys, query_ids, key_ids, scale)
    probs = jnp.exp(scores - log_total)
    grad_probs = jnp.einsum(
        "qhd,khd->hqk", grad_context, values, preferred_element_type=jnp.float32
    )
    inner = jnp.sum(grad_probs * probs, axis=-1, keepdims=True)
    grad_scores = (probs * (grad_probs - inner)).astype(jnp.bfloat16)
    grad_queries = (
        jnp.einsum("hqk,khd->qhd", grad_scores, keys, preferred_element_type=jnp.float32) * scale
    )
    grad_keys = (
        jnp.einsum("hqk,qhd->khd", grad_scores, queries, preferred_element_type=jnp.float32) * scale
    )
    grad_values = jnp.einsum(
        "hqk,qhd->khd", probs.astype(jnp.bfloat16), grad_context, preferred_element_type=jnp.float32
    )
    return (grad_queries, grad_keys, grad_values)


def product(left, right):
    return jnp.dot(left, right, preferred_element_type=jnp.float32)


def head_total(term):
    return lax.psum(term, "tp")


def local(
    tokens,
    cotangent,
    block_ids,
    live_count,
    first_gain,
    first_shift,
    query_weight,
    query_bias,
    key_weight,
    value_weight,
    value_bias,
    output_weight,
    output_bias,
    second_gain,
    second_shift,
    expand_weight,
    expand_bias,
    reduce_weight,
    reduce_bias,
):
    slot_count, half_len, width = tokens.shape
    row_count = slot_count * half_len
    ctx_side = lax.axis_index("ctx")
    scale = 1.0 / math.sqrt(HD)
    gathered = (
        lax.all_gather(first_gain, ("fsdp", "ctx"), axis=0, tiled=True),
        lax.all_gather(first_shift, ("fsdp", "ctx"), axis=0, tiled=True),
        lax.all_gather(query_weight, ("fsdp", "ctx"), axis=0, tiled=True),
        lax.all_gather(query_bias, ("fsdp", "ctx"), axis=1, tiled=True),
        lax.all_gather(key_weight, ("fsdp", "ctx"), axis=0, tiled=True),
        lax.all_gather(value_weight, ("fsdp", "ctx"), axis=0, tiled=True),
        lax.all_gather(value_bias, ("fsdp", "ctx"), axis=1, tiled=True),
        lax.all_gather(output_weight, ("fsdp", "ctx"), axis=1, tiled=True),
        lax.all_gather(output_bias, ("fsdp", "ctx"), axis=0, tiled=True),
        lax.all_gather(second_gain, ("fsdp", "ctx"), axis=0, tiled=True),
        lax.all_gather(second_shift, ("fsdp", "ctx"), axis=0, tiled=True),
        lax.all_gather(expand_weight, ("fsdp", "ctx"), axis=0, tiled=True),
        lax.all_gather(expand_bias, ("fsdp", "ctx"), axis=1, tiled=True),
        lax.all_gather(reduce_weight, ("fsdp", "ctx"), axis=1, tiled=True),
        lax.all_gather(reduce_bias, ("fsdp", "ctx"), axis=0, tiled=True),
    )
    (
        full_gain_one,
        full_shift_one,
        full_query,
        full_query_bias,
        full_key,
        full_value,
        full_value_bias,
        full_output,
        full_output_bias,
        full_gain_two,
        full_shift_two,
        full_expand,
        full_expand_bias,
        full_reduce,
        full_reduce_bias,
    ) = gathered
    tp_width = full_query.shape[1]
    heads_local = tp_width // HD
    live = (jnp.arange(slot_count) < live_count[0]).astype(jnp.float32)
    row_live = jnp.repeat(live, half_len)[:, None]
    inputs = tokens.astype(jnp.float32).reshape(row_count, width)
    scaled_one, spread_one = norm_parts(inputs)
    normed_one = (
        scaled_one * full_gain_one.astype(jnp.float32) + full_shift_one.astype(jnp.float32)
    ).astype(jnp.bfloat16)
    queries = (
        product(normed_one, full_query) + full_query_bias.reshape(-1).astype(jnp.float32)
    ).astype(jnp.bfloat16)
    keys_local = product(normed_one, full_key).astype(jnp.bfloat16)
    values_local = (
        product(normed_one, full_value) + full_value_bias.reshape(-1).astype(jnp.float32)
    ).astype(jnp.bfloat16)
    shaped = (slot_count, half_len, tp_width)
    keys_local = keys_local.reshape(shaped)
    values_local = values_local.reshape(shaped)
    remote_keys, remote_values = shifted((keys_local, values_local), "ctx", 1)
    heads_shape = (slot_count, -1, heads_local, HD)
    all_keys = jnp.concatenate([keys_local, remote_keys], axis=1).reshape(heads_shape)
    all_values = jnp.concatenate([values_local, remote_values], axis=1).reshape(heads_shape)
    query_heads = queries.reshape(heads_shape)
    local_ids = lax.dynamic_slice_in_dim(block_ids, ctx_side * half_len, half_len, 1)
    remote_ids = lax.dynamic_slice_in_dim(block_ids, (1 - ctx_side) * half_len, half_len, 1)
    key_ids = jnp.concatenate([local_ids, remote_ids], axis=1)

    def forward_slot(element):
        return attend_forward(element[0], element[1], element[2], element[3], element[4], scale)

    context, log_total = lax.map(
        forward_slot, (query_heads, all_keys, all_values, local_ids, key_ids)
    )
    context_low = context.reshape(row_count, tp_width).astype(jnp.bfloat16)
    attn_term = product(context_low, full_output)
    gain_two = full_gain_two.astype(jnp.float32)
    shift_two = full_shift_two.astype(jnp.float32)
    middle = inputs + head_total(attn_term) + full_output_bias.astype(jnp.float32)
    scaled_two, spread_two = norm_parts(middle)
    normed_two = (scaled_two * gain_two + shift_two).astype(jnp.bfloat16)
    hidden = product(normed_two, full_expand) + full_expand_bias.reshape(-1).astype(jnp.float32)
    active, gelu_pull = jax.vjp(gelu_exact, hidden)
    active_low = active.astype(jnp.bfloat16)
    mlp_term = product(active_low, full_reduce)
    layer_out = (
        (middle + head_total(mlp_term) + full_reduce_bias.astype(jnp.float32)) * row_live
    ).astype(jnp.bfloat16)
    layer_out = layer_out.reshape(slot_count, half_len, width)
    backward_set = (
        lax.all_gather(first_gain, ("fsdp", "ctx"), axis=0, tiled=True),
        lax.all_gather(first_shift, ("fsdp", "ctx"), axis=0, tiled=True),
        lax.all_gather(query_weight, ("fsdp", "ctx"), axis=0, tiled=True),
        lax.all_gather(query_bias, ("fsdp", "ctx"), axis=1, tiled=True),
        lax.all_gather(key_weight, ("fsdp", "ctx"), axis=0, tiled=True),
        lax.all_gather(value_weight, ("fsdp", "ctx"), axis=0, tiled=True),
        lax.all_gather(value_bias, ("fsdp", "ctx"), axis=1, tiled=True),
        lax.all_gather(output_weight, ("fsdp", "ctx"), axis=1, tiled=True),
        lax.all_gather(output_bias, ("fsdp", "ctx"), axis=0, tiled=True),
        lax.all_gather(second_gain, ("fsdp", "ctx"), axis=0, tiled=True),
        lax.all_gather(second_shift, ("fsdp", "ctx"), axis=0, tiled=True),
        lax.all_gather(expand_weight, ("fsdp", "ctx"), axis=0, tiled=True),
        lax.all_gather(expand_bias, ("fsdp", "ctx"), axis=1, tiled=True),
        lax.all_gather(reduce_weight, ("fsdp", "ctx"), axis=1, tiled=True),
        lax.all_gather(reduce_bias, ("fsdp", "ctx"), axis=0, tiled=True),
    )
    (
        back_gain_one,
        back_shift_one,
        back_query,
        back_query_bias,
        back_key,
        back_value,
        back_value_bias,
        back_output,
        back_output_bias,
        back_gain_two,
        back_shift_two,
        back_expand,
        back_expand_bias,
        back_reduce,
        back_reduce_bias,
    ) = backward_set
    grad_out = cotangent.astype(jnp.float32).reshape(row_count, width) * row_live
    grad_low = grad_out.astype(jnp.bfloat16)
    reduce_bias_grad = jnp.sum(grad_out, axis=0)
    reduce_weight_grad = jnp.einsum(
        "rf,rd->fd", active_low, grad_low, preferred_element_type=jnp.float32
    )
    grad_active = jnp.einsum("rd,fd->rf", grad_low, back_reduce, preferred_element_type=jnp.float32)
    grad_hidden = gelu_pull(grad_active)[0].astype(jnp.bfloat16)
    expand_bias_grad = jnp.sum(grad_hidden.astype(jnp.float32), axis=0).reshape(
        full_expand_bias.shape
    )
    expand_weight_grad = jnp.einsum(
        "rd,rf->df", normed_two, grad_hidden, preferred_element_type=jnp.float32
    )
    normed_two_term = jnp.einsum(
        "rf,df->rd", grad_hidden, back_expand, preferred_element_type=jnp.float32
    )
    grad_normed_two = head_total(normed_two_term)
    norm_part_two, second_gain_grad, second_shift_grad = norm_back(
        grad_normed_two, scaled_two, spread_two, back_gain_two.astype(jnp.float32)
    )
    grad_middle = grad_out + norm_part_two
    grad_branch = grad_middle.astype(jnp.bfloat16)
    output_bias_grad = jnp.sum(grad_branch.astype(jnp.float32), axis=0)
    output_weight_grad = jnp.einsum(
        "rh,rd->hd", context_low, grad_branch, preferred_element_type=jnp.float32
    )
    grad_context = jnp.einsum(
        "rd,hd->rh", grad_branch, back_output, preferred_element_type=jnp.float32
    )
    grad_context = grad_context.astype(jnp.bfloat16).reshape(heads_shape)

    def backward_slot(element):
        return attend_backward(
            element[0],
            element[1],
            element[2],
            element[3],
            element[4],
            element[5],
            element[6],
            scale,
        )

    grad_queries, grad_keys, grad_values = lax.map(
        backward_slot,
        (query_heads, all_keys, all_values, local_ids, key_ids, log_total, grad_context),
    )
    returned_keys, returned_values = (
        shifted(grad_keys[:, half_len:].reshape(shaped).astype(jnp.bfloat16), "ctx", 1).astype(
            jnp.float32
        ),
        shifted(grad_values[:, half_len:].reshape(shaped).astype(jnp.bfloat16), "ctx", 1).astype(
            jnp.float32
        ),
    )
    keys_grad = (
        (grad_keys[:, :half_len].reshape(shaped) + returned_keys)
        .reshape(row_count, tp_width)
        .astype(jnp.bfloat16)
    )
    values_grad = (
        (grad_values[:, :half_len].reshape(shaped) + returned_values)
        .reshape(row_count, tp_width)
        .astype(jnp.bfloat16)
    )
    queries_grad = grad_queries.reshape(row_count, tp_width).astype(jnp.bfloat16)
    query_bias_grad = jnp.sum(queries_grad.astype(jnp.float32), axis=0).reshape(
        full_query_bias.shape
    )
    value_bias_grad = jnp.sum(values_grad.astype(jnp.float32), axis=0).reshape(
        full_value_bias.shape
    )
    query_weight_grad = jnp.einsum(
        "rd,rh->dh", normed_one, queries_grad, preferred_element_type=jnp.float32
    )
    key_weight_grad = jnp.einsum(
        "rd,rh->dh", normed_one, keys_grad, preferred_element_type=jnp.float32
    )
    value_weight_grad = jnp.einsum(
        "rd,rh->dh", normed_one, values_grad, preferred_element_type=jnp.float32
    )
    grad_normed_part = (
        jnp.einsum("rh,dh->rd", queries_grad, back_query, preferred_element_type=jnp.float32)
        + jnp.einsum("rh,dh->rd", keys_grad, back_key, preferred_element_type=jnp.float32)
        + jnp.einsum("rh,dh->rd", values_grad, back_value, preferred_element_type=jnp.float32)
    )
    gain_one = back_gain_one.astype(jnp.float32)
    grad_normed_one = head_total(grad_normed_part)
    norm_part_one, first_gain_grad, first_shift_grad = norm_back(
        grad_normed_one, scaled_one, spread_one, gain_one
    )
    tokens_grad = (grad_middle + norm_part_one).astype(jnp.bfloat16)
    tokens_grad = tokens_grad.reshape(slot_count, half_len, width)
    summed = (
        lax.psum_scatter(
            first_gain_grad.astype(jnp.bfloat16), ("fsdp", "ctx"), scatter_dimension=0, tiled=True
        ).astype(jnp.float32),
        lax.psum_scatter(
            first_shift_grad.astype(jnp.bfloat16), ("fsdp", "ctx"), scatter_dimension=0, tiled=True
        ).astype(jnp.float32),
        lax.psum_scatter(
            query_weight_grad.astype(jnp.bfloat16), ("fsdp", "ctx"), scatter_dimension=0, tiled=True
        ).astype(jnp.float32),
        lax.psum_scatter(
            query_bias_grad.astype(jnp.bfloat16), ("fsdp", "ctx"), scatter_dimension=1, tiled=True
        ).astype(jnp.float32),
        lax.psum_scatter(
            key_weight_grad.astype(jnp.bfloat16), ("fsdp", "ctx"), scatter_dimension=0, tiled=True
        ).astype(jnp.float32),
        lax.psum_scatter(
            value_weight_grad.astype(jnp.bfloat16), ("fsdp", "ctx"), scatter_dimension=0, tiled=True
        ).astype(jnp.float32),
        lax.psum_scatter(
            value_bias_grad.astype(jnp.bfloat16), ("fsdp", "ctx"), scatter_dimension=1, tiled=True
        ).astype(jnp.float32),
        lax.psum_scatter(
            output_weight_grad.astype(jnp.bfloat16),
            ("fsdp", "ctx"),
            scatter_dimension=1,
            tiled=True,
        ).astype(jnp.float32),
        lax.psum_scatter(
            output_bias_grad.astype(jnp.bfloat16), ("fsdp", "ctx"), scatter_dimension=0, tiled=True
        ).astype(jnp.float32),
        lax.psum_scatter(
            second_gain_grad.astype(jnp.bfloat16), ("fsdp", "ctx"), scatter_dimension=0, tiled=True
        ).astype(jnp.float32),
        lax.psum_scatter(
            second_shift_grad.astype(jnp.bfloat16), ("fsdp", "ctx"), scatter_dimension=0, tiled=True
        ).astype(jnp.float32),
        lax.psum_scatter(
            expand_weight_grad.astype(jnp.bfloat16),
            ("fsdp", "ctx"),
            scatter_dimension=0,
            tiled=True,
        ).astype(jnp.float32),
        lax.psum_scatter(
            expand_bias_grad.astype(jnp.bfloat16), ("fsdp", "ctx"), scatter_dimension=1, tiled=True
        ).astype(jnp.float32),
        lax.psum_scatter(
            reduce_weight_grad.astype(jnp.bfloat16),
            ("fsdp", "ctx"),
            scatter_dimension=1,
            tiled=True,
        ).astype(jnp.float32),
        lax.psum_scatter(
            reduce_bias_grad.astype(jnp.bfloat16), ("fsdp", "ctx"), scatter_dimension=0, tiled=True
        ).astype(jnp.float32),
    )
    return (layer_out, tokens_grad) + tuple(summed)


def solution(mesh):
    return jax.shard_map(
        local,
        mesh=mesh,
        in_specs=(
            P("fsdp", "ctx", None),
            P("fsdp", "ctx", None),
            P("fsdp", None),
            P("fsdp"),
            P(("fsdp", "ctx")),
            P(("fsdp", "ctx")),
            P(("fsdp", "ctx"), "tp"),
            P("tp", ("fsdp", "ctx")),
            P(("fsdp", "ctx"), "tp"),
            P(("fsdp", "ctx"), "tp"),
            P("tp", ("fsdp", "ctx")),
            P("tp", ("fsdp", "ctx")),
            P(("fsdp", "ctx")),
            P(("fsdp", "ctx")),
            P(("fsdp", "ctx")),
            P(("fsdp", "ctx"), "tp"),
            P("tp", ("fsdp", "ctx")),
            P("tp", ("fsdp", "ctx")),
            P(("fsdp", "ctx")),
        ),
        out_specs=(
            P("fsdp", "ctx", None),
            P("fsdp", "ctx", None),
            P(("fsdp", "ctx")),
            P(("fsdp", "ctx")),
            P(("fsdp", "ctx"), "tp"),
            P("tp", ("fsdp", "ctx")),
            P(("fsdp", "ctx"), "tp"),
            P(("fsdp", "ctx"), "tp"),
            P("tp", ("fsdp", "ctx")),
            P("tp", ("fsdp", "ctx")),
            P(("fsdp", "ctx")),
            P(("fsdp", "ctx")),
            P(("fsdp", "ctx")),
            P(("fsdp", "ctx"), "tp"),
            P("tp", ("fsdp", "ctx")),
            P("tp", ("fsdp", "ctx")),
            P(("fsdp", "ctx")),
        ),
        check_vma=False,
    )
```

profile of v0, /device:TPU:0, one launch (start us, length us, event | category | flops | bytes accessed | tf_op | source)
XLA Modules:
  0.0 1349.8 jit_solution(2311676599527489216)
XLA Ops:
  14.1 10.4 all-gather.1
  24.5 9.1 all-gather
  33.6 7.9 all-gather.3
  41.5 9.0 all-gather.2
  58.7 11.4 all-gather.16.cloned.1.call-done
  76.1 23.8 %all-gather.18.cloned.1.call-done = bf16[2048,512]{1,0:T(8,128)(2,1)} async-done(((bf16[256,512]{1,0:T(8,128)(2,1)}), bf16[2048,512]{1,0:T(8,128)(2,1)}) %all-gather.18.cloned.1.call-update) | async-done | bytes 2097168 | tf_op jit(solution)/shard_map/all_gather | solution.py:112
  115.5 14.3 %all-gather.22.cloned.1.call-done = bf16[512,2048]{1,0:T(8,128)(2,1)} async-done(((bf16[512,256]{1,0:T(8,128)(2,1)}), bf16[512,2048]{1,0:T(8,128)(2,1)}) %all-gather.22.cloned.1.call-update) | async-done | bytes 2097168 | tf_op jit(solution)/shard_map/all_gather | solution.py:117
  136.7 8.9 all-gather.6
  145.6 8.0 all-gather.5
  153.6 9.1 all-gather.4
  162.7 8.0 all-gather.7
  170.8 118.9 %all-reduce.12.cloned.1.call-done = f32[512,2048]{1,0:T(8,128)} async-done(((f32[512,2048]{1,0:T(8,128)}), f32[512,2048]{1,0:T(8,128)}) %all-reduce.12.cloned.1.call-update) | async-done | bytes 4194320 | tf_op jit(solution)/shard_map/psum | solution.py:81
  295.0 49.7 %all-gather.24.cloned.1.call-done = bf16[2048,2048]{1,0:T(8,128)(2,1)} async-done(((bf16[256,2048]{1,0:T(8,128)(2,1)}), bf16[2048,2048]{1,0:T(8,128)(2,1)}) %all-gather.24.cloned.1.call-update) | async-done | bytes 8388624 | tf_op jit(solution)/shard_map/all_gather | solution.py:121
  344.7 11.0 multiply_convert_fusion.2
  355.7 46.7 %all-gather.26.cloned.1.call-done = bf16[2048,2048]{1,0:T(8,128)(2,1)} async-done(((bf16[2048,256]{1,0:T(8,128)(2,1)}), bf16[2048,2048]{1,0:T(8,128)(2,1)}) %all-gather.26.cloned.1.call-update) | async-done | bytes 8388624 | tf_op jit(solution)/shard_map/all_gather | solution.py:123
  402.5 10.0 fusion.63
  413.8 6.2 fusion.66
  421.4 153.7 %all-reduce.14.cloned.1.call-done = f32[512,2048]{1,0:T(8,128)} async-done(((f32[512,2048]{1,0:T(8,128)}), f32[512,2048]{1,0:T(8,128)}) %all-reduce.14.cloned.1.call-update) | async-done | bytes 4194320 | tf_op jit(solution)/shard_map/psum | solution.py:81
  601.9 5.0 convolution_convert_fusion.2
  621.3 10.9 convolution_convert_fusion.1
  632.5 10.0 convolution_convert_fusion
  642.6 10.7 fusion.65
  660.6 9.2 all-gather.8
  681.2 43.0 %reduce-scatter.22.cloned.1.call-done = bf16[512,256]{1,0:T(8,128)(2,1)} async-done(((bf16[512,2048]{1,0:T(8,128)(2,1)}), bf16[512,256]{1,0:T(8,128)(2,1)}) %reduce-scatter.22.cloned.1.call-update) | async-done | bytes 262160 | tf_op jit(solution)/shard_map/reduce_scatter | solution.py:342
  726.0 43.2 %reduce-scatter.16.cloned.1.call-done = bf16[256,512]{1,0:T(8,128)(2,1)} async-done(((bf16[2048,512]{1,0:T(8,128)(2,1)}), bf16[256,512]{1,0:T(8,128)(2,1)}) %reduce-scatter.16.cloned.1.call-update) | async-done | bytes 262160 | tf_op jit(solution)/shard_map/reduce_scatter | solution.py:327
  771.0 43.1 %reduce-scatter.20.cloned.1.call-done = bf16[256,512]{1,0:T(8,128)(2,1)} async-done(((bf16[2048,512]{1,0:T(8,128)(2,1)}), bf16[256,512]{1,0:T(8,128)(2,1)}) %reduce-scatter.20.cloned.1.call-update) | async-done | bytes 262160 | tf_op jit(solution)/shard_map/reduce_scatter | solution.py:336
  815.9 43.1 %reduce-scatter.18.cloned.1.call-done = bf16[256,512]{1,0:T(8,128)(2,1)} async-done(((bf16[2048,512]{1,0:T(8,128)(2,1)}), bf16[256,512]{1,0:T(8,128)(2,1)}) %reduce-scatter.18.cloned.1.call-update) | async-done | bytes 262160 | tf_op jit(solution)/shard_map/reduce_scatter | solution.py:333
  860.8 73.0 %reduce-scatter.24.cloned.1.call-done = bf16[256,2048]{1,0:T(8,128)(2,1)} async-done(((bf16[2048,2048]{1,0:T(8,128)(2,1)}), bf16[256,2048]{1,0:T(8,128)(2,1)}) %reduce-scatter.24.cloned.1.call-update) | async-done | bytes 1048592 | tf_op jit(solution)/shard_map/reduce_scatter | solution.py:357
  936.6 71.8 %reduce-scatter.26.cloned.1.call-done = bf16[2048,256]{1,0:T(8,128)(2,1)} async-done(((bf16[2048,2048]{1,0:T(8,128)(2,1)}), bf16[2048,256]{1,0:T(8,128)(2,1)}) %reduce-scatter.26.cloned.1.call-update) | async-done | bytes 1048592 | tf_op jit(solution)/shard_map/reduce_scatter | solution.py:366
  1011.1 290.7 %all-reduce.16.cloned.1.call-done = (f32[512,2048]{1,0:T(8,128)}, f32[512,2048]{1,0:T(8,128)}) async-done(((f32[512,2048]{1,0:T(8,128)}, f32[512,2048]{1,0:T(8,128)}), (f32[512,2048]{1,0:T(8,128)}, f32[512,2048]{1,0:T(8,128)})) %all-reduce.16.cloned.1.call-update) | async-done | bytes 8388624 | tf_op jit(solution)/shard_map/psum | solution.py:81
  1305.4 23.8 %all-reduce.7 = (bf16[2048]{0:T(1024)(128)(2,1)S(1)}, bf16[2048]{0:T(1024)(128)(2,1)S(1)}, bf16[2048]{0:T(1024)(128)(2,1)S(1)}, bf16[2048]{0:T(1024)(128)(2,1)S(...) all-reduce(bf16[2048]{0:T(1024)(128)(2,1)S(1)} %get-tuple-element.7, ...), channel_id=2, replica_groups=mesh['fsdp'=4,'ctx'=2,'tp'=4] {'fsdp','ctx'}, use_global_device_ids=true, to_apply=%region_16.17.clone | all-reduce | flops 12288 | bytes 49152
  1333.1 6.0 fusion.29
  (203 shorter events, 133.5 us)
Async XLA Ops:
  7.2 26.4 %copy-start.20 = (bf16[4,16]{1,0:T(4,128)(2,1)S(1)}, bf16[4,16]{1,0:T(4,128)(2,1)}, u32[]{:S(2)}) copy-start(bf16[4,16]{1,0:T(4,128)(2,1)} %param.26) | copy-start | bytes 388
  7.2 34.3 %copy-start.21 = (bf16[4,16]{1,0:T(4,128)(2,1)S(1)}, bf16[4,16]{1,0:T(4,128)(2,1)}, u32[]{:S(2)}) copy-start(bf16[4,16]{1,0:T(4,128)(2,1)} %param.29) | copy-start | bytes 388
  7.2 43.3 %copy-start.19 = (s32[1,1024]{1,0:T(1,128)S(1)}, s32[1,1024]{1,0:T(1,128)}, u32[]{:S(2)}) copy-start(s32[1,1024]{1,0:T(1,128)} %param.21) | copy-start | bytes 12292
  7.2 46.8 %all-gather.20.cloned.1.call-start = ((), (), s32[]{:S(2)}) async-start(), calls=%async_computation.11 | async-start | bytes 2359296 | tf_op jit(solution)/shard_map/all_gather | solution.py:114
  8.0 62.2 %all-gather.16.cloned.1.call-start = ((), (), s32[]{:S(2)}) async-start(), calls=%async_computation.9 | async-start | bytes 2359296 | tf_op jit(solution)/shard_map/all_gather | solution.py:115
  8.7 91.2 %all-gather.18.cloned.1.call-start = ((), (), s32[]{:S(2)}) async-start(), calls=%async_computation.10 | async-start | bytes 2359296 | tf_op jit(solution)/shard_map/all_gather | solution.py:112
  9.4 120.3 %all-gather.22.cloned.1.call-start = ((), (), s32[]{:S(2)}) async-start(), calls=%async_computation.12 | async-start | bytes 2359296 | tf_op jit(solution)/shard_map/all_gather | solution.py:117
  10.0 279.7 %all-reduce.12.cloned.1.call-start = ((), (), s32[]{:S(2)}) async-start(), calls=%async_computation.13 | async-start | bytes 8388608 | tf_op jit(solution)/shard_map/psum | solution.py:81
  58.4 45.1 %collective-permute-start.1 = (bf16[1,512,512]{1,2,0:T(8,128)(2,1)}, bf16[1,512,512]{1,2,0:T(8,128)(2,1)}, u32[]{:S(2)}, u32[]{:S(2)}) collective-permute-start(bf16[1,512,512]{1,2,0:T(8,128)(2,1)} %bitcast.18), channel_id=1, source_target_pairs={{4,0},{0,4},{5,1},{1,5},{6,2},{2,6},{7,3},{3,7},{12,8},{8,12},{13,... | collective-permute-start | bytes 1572872 | tf_op jit(solution)/shard_map/ppermute | solution.py:17
  75.8 35.0 %collective-permute-start = (bf16[1,512,512]{1,2,0:T(8,128)(2,1)}, bf16[1,512,512]{1,2,0:T(8,128)(2,1)}, u32[]{:S(2)}, u32[]{:S(2)}) collective-permute-start(bf16[1,512,512]{1,2,0:T(8,128)(2,1)} %bitcast.8), channel_id=1, source_target_pairs={{4,0},{0,4},{5,1},{1,5},{6,2},{2,6},{7,3},{3,7},{12,8},{8,12},{13,... | collective-permute-start | bytes 1572872 | tf_op jit(solution)/shard_map/ppermute | solution.py:17
  115.4 19.1 %copy-start.18 = (bf16[4,128,512]{2,1,0:T(8,128)(2,1)}, bf16[4,128,512]{2,1,0:T(8,128)(2,1)S(1)}, u32[]{:S(2)}) copy-start(bf16[4,128,512]{2,1,0:T(8,128)(2,1)S(1)} %fusion.36) | copy-start | bytes 1572868
  134.5 28.1 %copy-start.22 = (bf16[4,64]{1,0:T(4,128)(2,1)S(1)}, bf16[4,64]{1,0:T(4,128)(2,1)}, u32[]{:S(2)}) copy-start(bf16[4,64]{1,0:T(4,128)(2,1)} %param.35) | copy-start | bytes 1540
  134.6 210.1 %all-gather.24.cloned.1.call-start = ((), (), s32[]{:S(2)}) async-start(), calls=%async_computation.14 | async-start | bytes 9437184 | tf_op jit(solution)/shard_map/all_gather | solution.py:121
  135.2 267.3 %all-gather.26.cloned.1.call-start = ((), (), s32[]{:S(2)}) async-start(), calls=%async_computation.15 | async-start | bytes 9437184 | tf_op jit(solution)/shard_map/all_gather | solution.py:123
  135.9 439.3 %all-reduce.14.cloned.1.call-start = ((), (), s32[]{:S(2)}) async-start(), calls=%async_computation.16 | async-start | bytes 8388608 | tf_op jit(solution)/shard_map/psum | solution.py:81
  402.5 11.3 copy-start.23
  420.1 253.0 %reduce-scatter.32.cloned.1.call-start = ((), (), s32[]{:S(2)}) async-start(), calls=%async_computation.25 | async-start | bytes 147456
  421.0 253.5 %reduce-scatter.28.cloned.1.call-start = ((), (), s32[]{:S(2)}) async-start(), calls=%async_computation.23 | async-start | bytes 36864
  575.2 10.8 slice-start
  592.2 7.0 collective-permute-start.3
  599.1 80.8 %reduce-scatter.30.cloned.1.call-start = ((), (), s32[]{:S(2)}) async-start(), calls=%async_computation.24 | async-start | bytes 36864
  601.9 122.4 %reduce-scatter.22.cloned.1.call-start = ((), (), s32[]{:S(2)}) async-start(), calls=%async_computation.20 | async-start | bytes 2359296 | tf_op jit(solution)/shard_map/reduce_scatter | solution.py:342
  606.9 162.3 %reduce-scatter.16.cloned.1.call-start = ((), (), s32[]{:S(2)}) async-start(), calls=%async_computation.17 | async-start | bytes 2359296 | tf_op jit(solution)/shard_map/reduce_scatter | solution.py:327
  609.9 204.2 %reduce-scatter.20.cloned.1.call-start = ((), (), s32[]{:S(2)}) async-start(), calls=%async_computation.19 | async-start | bytes 2359296 | tf_op jit(solution)/shard_map/reduce_scatter | solution.py:336
  612.8 246.1 %reduce-scatter.18.cloned.1.call-start = ((), (), s32[]{:S(2)}) async-start(), calls=%async_computation.18 | async-start | bytes 2359296 | tf_op jit(solution)/shard_map/reduce_scatter | solution.py:333
  616.1 2.1 collective-permute-start.2
  621.2 312.6 %reduce-scatter.24.cloned.1.call-start = ((), (), s32[]{:S(2)}) async-start(), calls=%async_computation.21 | async-start | bytes 9437184 | tf_op jit(solution)/shard_map/reduce_scatter | solution.py:357
  632.2 376.2 %reduce-scatter.26.cloned.1.call-start = ((), (), s32[]{:S(2)}) async-start(), calls=%async_computation.22 | async-start | bytes 9437184 | tf_op jit(solution)/shard_map/reduce_scatter | solution.py:366
  642.6 659.3 %all-reduce.16.cloned.1.call-start = ((), (), s32[]{:S(2)}) async-start(), calls=%async_computation.26 | async-start | bytes 16777216 | tf_op jit(solution)/shard_map/psum | solution.py:81
  642.6 10.8 copy-start.10
  642.6 10.8 copy-start.16
  659.9 9.8 copy-start.28
  (22 other events, 74.6 us)
Sparse Core Ops, SparseCore 0:
  9.9 30.5 all-gather.19
  42.4 27.7 all-gather.15
  72.1 27.7 all-gather.17
  101.6 28.0 all-gather.21
  134.7 154.9 all-reduce.11
  291.4 53.2 all-gather.23
  346.6 55.8 all-gather.25
  420.2 154.9 all-reduce.13
  578.2 32.5 reduce-scatter.31
  614.2 31.2 reduce-scatter.27
  648.5 31.3 reduce-scatter.29
  683.0 41.1 reduce-scatter.21
  728.1 41.1 reduce-scatter.15
  772.9 41.1 reduce-scatter.19
  817.8 41.1 reduce-scatter.17
  862.3 71.4 reduce-scatter.23
  937.1 71.2 reduce-scatter.25
  1010.9 290.8 all-reduce.15
where the time goes:
time: 1360 us; the launch traced here: 1350 us
  waiting for transfers between devices  1040 us (76%)
  matrix products  114 us (8%)
  blocking collectives  103 us (8%)
  other arithmetic  56.8 us (4%)
  local copies, waits for them, and re-layouts  20.5 us (2%)
  between operations  16.6 us (1%)
    psum x3, waiting for transfers between devices, head_total(): return lax.psum(term, 'tp')  563 us
    reduce_scatter x1, waiting for transfers between devices, local(): lax.psum_scatter(expand_weight_grad.astype(jnp.bfloat16), ('fsdp', 'ctx')...  73 us
    reduce_scatter x1, waiting for transfers between devices, local(): lax.psum_scatter(reduce_weight_grad.astype(jnp.bfloat16), ('fsdp', 'ctx')...  71.8 us
    all_gather x1, waiting for transfers between devices, local(): lax.all_gather(expand_weight, ('fsdp', 'ctx'), axis=0, tiled=True)  49.7 us
    all_gather x1, waiting for transfers between devices, local(): lax.all_gather(reduce_weight, ('fsdp', 'ctx'), axis=1, tiled=True)  46.7 us
    reduce_scatter x1, waiting for transfers between devices, local(): lax.psum_scatter(query_weight_grad.astype(jnp.bfloat16), ('fsdp', 'ctx'),...  43.2 us
    reduce_scatter x1, waiting for transfers between devices, local(): lax.psum_scatter(value_weight_grad.astype(jnp.bfloat16), ('fsdp', 'ctx'),...  43.1 us
    reduce_scatter x1, waiting for transfers between devices, local(): lax.psum_scatter(key_weight_grad.astype(jnp.bfloat16), ('fsdp', 'ctx'), s...  43.1 us
  transfers between devices with their start and end apart: 22, of which 16 were waited for; matrix products, arithmetic and copies ran while one was open for 11% of the time, Pallas kernels for 0%

commit v1 on v0

v1 whole, which is shorter than its diff:
```python
import functools
import math

import jax
import jax.numpy as jnp
from jax import lax
from jax.experimental import pallas as pl
from jax.experimental.pallas import tpu as pltpu
from jax.sharding import PartitionSpec as P

HD = 128
NEG = -1e30
MESH = pl.DeviceIdType.MESH
ANY = pl.BlockSpec(memory_space=pl.ANY)
VM = pl.BlockSpec(memory_space=pltpu.VMEM)
BF = jnp.bfloat16
F32 = jnp.float32
epsilon = 1e-05


def dot(left, right):
    return lax.dot_general(left, right, (((1,), (0,)), ((), ())), preferred_element_type=F32)


def dot_nt(left, right):
    return lax.dot_general(left, right, (((1,), (1,)), ((), ())), preferred_element_type=F32)


def dot_tn(left, right):
    return lax.dot_general(left, right, (((0,), (0,)), ((), ())), preferred_element_type=F32)


def al(value, step):
    return pl.multiple_of(value, step)


class Place:
    def __init__(self, n_f, n_t):
        self.n_f, self.n_t, self.m = n_f, n_t, n_f // 2
        self.f = lax.axis_index("fsdp")
        self.c = lax.axis_index("ctx")
        self.t = lax.axis_index("tp")
        self.p = self.spot(self.f)
        self.side = self.t // (n_t - 1)
        self.right = (self.owner(1), self.c, self.t)
        self.left = (self.owner(-1), self.c, self.t)
        self.sib = (self.f, 1 - self.c, self.t)

    def spot(self, g):
        a = g // self.m
        return (1 - a) * g + a * (self.n_f - 1 + self.m - g)

    def owner(self, k):
        return self.spot(lax.rem(self.p + k + self.n_f, self.n_f))

    def shard(self, k, other=False):
        c = 1 - self.c if other else self.c
        return 2 * self.owner(k) + c

    def tp(self, d):
        return (self.f, self.c, lax.rem(self.t + d + self.n_t, self.n_t))

    def plane(self, k):
        return (lax.rem(self.f + k, self.n_f), self.c, self.t)

    def greet(self):
        bar = pltpu.get_barrier_semaphore()
        others = [self.sib] + [self.plane(k) for k in range(1, self.n_f)]
        others += [self.tp(k) for k in range(1, self.n_t)]
        for other in others:
            pl.semaphore_signal(bar, 1, device_id=other, device_id_type=MESH)
        pl.semaphore_wait(bar, len(others))


def remote(src, dst, send, recv, to):
    return pltpu.make_async_remote_copy(
        src_ref=src, dst_ref=dst, send_sem=send, recv_sem=recv, device_id=to, device_id_type=MESH
    )


class Gather:
    def __init__(self, here, own, slot, send, recv):
        self.here, self.own, self.slot, self.send, self.recv = here, own, slot, send, recv
        self.m = here.m

    def half(self, way, s):
        return None if s < self.m else way

    def hop(self, way, s):
        here, sign = self.here, (-1, 1)[way]
        part = self.half(way, s)
        idx = here.shard(sign * (s - 1))
        src = self.own(part) if s == 1 else self.slot(idx, part)
        k = way * self.m + s - 1
        to = (here.right, here.left)[way]
        return remote(src, self.slot(idx, part), self.send.at[k], self.recv.at[k], to)

    def landing(self, way, s):
        here, sign = self.here, (-1, 1)[way]
        part = self.half(way, s)
        ref = self.slot(here.shard(sign * s), part)
        k = way * self.m + s - 1
        to = (here.right, here.left)[way]
        return remote(ref, ref, self.send.at[k], self.recv.at[k], to)

    def cross(self, k, offset, other=False):
        here = self.here
        ref = self.slot(here.shard(offset, other), None)
        src = self.own(None) if (offset == 0 and not other) else ref
        n = 2 * self.m + k
        return remote(src, ref, self.send.at[n], self.recv.at[n], here.sib)

    def crossings(self):
        found = [(0, 0)]
        for s in range(1, self.m):
            found += [(2 * s - 1, -s), (2 * s, s)]
        return found + [(2 * self.m - 1, self.m)]

    def start(self):
        self.hop(0, 1).start()
        self.hop(1, 1).start()
        self.cross(0, 0).start()

    def step(self, s):
        self.landing(0, s).wait_recv()
        self.landing(1, s).wait_recv()
        if s < self.m:
            self.hop(0, s + 1).start()
            self.hop(1, s + 1).start()
            self.cross(2 * s - 1, -s).start()
            self.cross(2 * s, s).start()
        else:
            self.cross(2 * self.m - 1, self.m).start()

    def arrive(self):
        for k, offset in self.crossings():
            self.cross(k, offset, True).wait_recv()

    def finish(self):
        for s in range(1, self.m + 1):
            self.hop(0, s).wait_send()
            self.hop(1, s).wait_send()
        for k, offset in self.crossings():
            self.cross(k, offset).wait_send()

    @staticmethod
    def sems(n_f):
        return 2 * n_f


class Line:
    def __init__(self, here, part, rbuf, norm, sems, chunks, lag):
        self.here, self.part, self.rbuf, self.norm = here, part, rbuf, norm
        self.s_send, self.s_recv, self.g_send, self.g_recv = sems
        self.half = part.shape[0] // 2
        self.nc, self.lag = chunks, lag
        self.cr = self.half // chunks

    def rows(self, d, j):
        return pl.ds(al(d * self.half + j * self.cr, self.cr), self.cr)

    def span(self, j):
        return pl.ds(al(j * self.cr, self.cr), self.cr)

    def s_copy(self, d, j):
        return remote(
            self.part.at[self.rows(d, j)],
            self.rbuf.at[d, self.span(j)],
            self.s_send.at[d, j],
            self.s_recv.at[d, j],
            self.here.tp(2 * d - 1),
        )

    def g_copy(self, d, j):
        ref = self.norm.at[self.rows(d, j)]
        to = self.here.tp(1 - 2 * d)
        return remote(ref, ref, self.g_send.at[d, j], self.g_recv.at[d, j], to)

    def depth(self, d):
        t, n = self.here.t, self.here.n_t
        return t if d == 1 else n - 1 - t

    def sum_step(self, d, tau):
        depth, n = self.depth(d), self.here.n_t
        j = tau - self.lag * depth
        valid = (j >= 0) & (j < self.nc)

        @pl.when(valid & (depth > 0))
        def _():
            self.s_copy(d, j).wait_recv()

        @pl.when(valid & (depth > 0) & (depth < n - 1))
        def _():
            own = self.part[self.rows(d, j), :].astype(F32)
            got = self.rbuf[d, self.span(j), :].astype(F32)
            self.part[self.rows(d, j), :] = (own + got).astype(BF)

        @pl.when(valid & (depth < n - 1))
        def _():
            self.s_copy(d, j).start()

    def owner_step(self, tau, final, back=True):
        here, n = self.here, self.here.n_t
        j = tau - self.lag * (n - 1)
        end = (here.t == 0) | (here.t == n - 1)

        @pl.when(end & (j >= 0) & (j < self.nc))
        def _():
            d = here.side
            rows = self.rows(d, j)
            total = self.part[rows, :].astype(F32) + self.rbuf[d, self.span(j), :].astype(F32)
            final(rows, self.span(j), total)
            if back:
                self.back_copy(j).start()

    def back_copy(self, j):
        here = self.here
        d = here.side
        ref = self.norm.at[self.rows(d, j)]
        return remote(
            ref, ref, self.g_send.at[d, j], self.g_recv.at[d, j], here.tp(1 - 2 * d)
        )

    def gather_step(self, d, tau, base):
        t, n = self.here.t, self.here.n_t
        depth = t if d == 0 else n - 1 - t
        j = tau - base - self.lag * depth
        valid = (j >= 0) & (j < self.nc) & (depth > 0)

        @pl.when(valid)
        def _():
            self.g_copy(d, j).wait_recv()

        @pl.when(valid & (depth < n - 1))
        def _():
            self.g_copy(d, j).start()

    def sum_ticks(self):
        return self.nc + self.lag * (self.here.n_t - 1)

    def ticks(self):
        return self.nc + 2 * self.lag * (self.here.n_t - 1)

    def tick(self, tau, final, back=True):
        self.sum_step(1, tau)
        self.sum_step(0, tau)
        self.owner_step(tau, final, back)
        if back:
            base = self.lag * (self.here.n_t - 1)
            self.gather_step(0, tau, base)
            self.gather_step(1, tau, base)

    def finish_sum(self):
        t, n = self.here.t, self.here.n_t

        def body(j, _):
            @pl.when(t > 0)
            def _():
                self.s_copy(0, j).wait_send()

            @pl.when(t < n - 1)
            def _():
                self.s_copy(1, j).wait_send()

            return 0

        lax.fori_loop(0, self.nc, body, 0)

    def finish_back(self):
        t, n = self.here.t, self.here.n_t

        def body(j, _):
            @pl.when(t < n - 1)
            def _():
                self.g_copy(0, j).wait_send()

            @pl.when(t > 0)
            def _():
                self.g_copy(1, j).wait_send()

            return 0

        lax.fori_loop(0, self.nc, body, 0)

    @staticmethod
    def sems(chunks):
        return [pltpu.SemaphoreType.DMA((2, chunks))] * 4


def norm_rows(values):
    mean = jnp.mean(values, axis=-1, keepdims=True)
    center = values - mean
    spread = lax.rsqrt(jnp.mean(center * center, axis=-1, keepdims=True) + epsilon)
    return center * spread, spread


class Outs:
    def __init__(self, sem):
        self.sem, self.made = sem, []

    def put(self, src, dst):
        copy = pltpu.make_async_copy(src, dst, self.sem.at[len(self.made)])
        copy.start()
        self.made.append(copy)

    def wait(self):
        for copy in self.made:
            copy.wait()


def row_slots(ref, size):
    def slot(idx, part):
        if part is None:
            return ref.at[pl.ds(al(idx * size, size), size)]
        return ref.at[pl.ds(al(idx * size + part * (size // 2), size // 2), size // 2)]

    return slot


def lead_slots(ref):
    size = ref.shape[1]

    def slot(idx, part):
        if part is None:
            return ref.at[idx]
        return ref.at[idx, pl.ds(part * (size // 2), size // 2)]

    return slot


def own_part(ref):
    size = ref.shape[0]

    def own(part):
        if part is None:
            return ref
        return ref.at[pl.ds(part * (size // 2), size // 2)]

    return own


def allowed_scores(q, k, col, row, scale):
    return jnp.where(row <= col, dot_nt(q, k) * scale, NEG)


def forward_kernel(
    n_f, n_t, chunks, lag,
    tok, col, row, small, wa, wo, we, wr,
    n1_o, q_o, kv_o, ctx_o, n2_o, mid_o, par_o, a_o, o_o, e_o, r_o,
    tokv, n1, full_a, full_o, stage_e, stage_r, q, kv, ctx, part, rbuf, norm, mid,
    sib_small, all_small, par,
    ga_s, ga_r, go_s, go_r, ge_s, ge_r, gr_s, gr_r,
    ls_s, ls_r, lg_s, lg_r, sm_s, sm_r, kv_s, kv_r, in_sem, out_sem,
):
    here = Place(n_f, n_t)
    width = wo.shape[0]
    shard = wa.shape[0]
    rows_all, model = n1.shape
    heads = width // HD
    scale = 1.0 / math.sqrt(HD)
    tok_in = pltpu.make_async_copy(tok, tokv, in_sem.at[0])
    tok_in.start()
    me = 2 * here.f + here.c
    a_slot, o_slot = row_slots(full_a, shard), lead_slots(full_o)
    e_slot, r_slot = row_slots(e_o, shard), lead_slots(r_o)
    loads = [
        pltpu.make_async_copy(wo, o_slot(me, None), in_sem.at[1]),
        pltpu.make_async_copy(wa, a_slot(me, None), in_sem.at[2]),
        pltpu.make_async_copy(we, stage_e, in_sem.at[3]),
        pltpu.make_async_copy(wr, stage_r, in_sem.at[4]),
    ]
    for load in loads:
        load.start()
    here.greet()
    ga = Gather(here, own_part(wa), a_slot, ga_s, ga_r)
    go = Gather(here, own_part(wo), o_slot, go_s, go_r)
    ge = Gather(here, own_part(we), e_slot, ge_s, ge_r)
    gr = Gather(here, own_part(wr), r_slot, gr_s, gr_r)
    outs = Outs(out_sem)
    to_sib = remote(small, sib_small, sm_s.at[0], sm_r.at[0], here.sib)
    to_sib.start()
    go.start()
    to_sib.wait_recv()
    all_small[here.f] = small[...] + sib_small[...]

    def small_copy(k):
        spot = all_small.at[here.f]
        return remote(spot, spot, sm_s.at[k], sm_r.at[k], here.plane(k))

    def small_landing(k):
        spot = all_small.at[lax.rem(here.f + n_f - k, n_f)]
        return remote(spot, spot, sm_s.at[k], sm_r.at[k], here.plane(k))

    for k in range(1, n_f):
        small_copy(k).start()
    ga.start()
    for load in loads[2:]:
        load.wait()
    outs.put(stage_e, e_slot(me, None))
    outs.put(stage_r, r_slot(me, None))
    for s in range(1, here.m):
        go.step(s)
    for k in range(1, n_f):
        small_landing(k).wait_recv()
    total = all_small[0]
    for k in range(1, n_f):
        total = total + all_small[k]
    par[...] = total
    outs.put(par, par_o)
    tok_in.wait()

    def norm_one(i, _):
        rows = pl.ds(al(i * 64, 64), 64)
        scaled, _spread = norm_rows(tokv[rows, :].astype(F32))
        n1[rows, :] = (scaled * par[0:1, :] + par[1:2, :]).astype(BF)
        return 0

    lax.fori_loop(0, rows_all // 64, norm_one, 0)
    outs.put(n1, n1_o)
    for s in range(1, here.m):
        ga.step(s)
    gr.start()
    ge.start()
    go.step(here.m)
    ga.step(here.m)
    for load in loads[:2]:
        load.wait()
    ga.arrive()
    q[...] = (dot(n1[...], full_a[:, 0:width]) + par[6:7, 0:width]).astype(BF)
    kv[0, :, 0:width] = dot(n1[...], full_a[:, width : 2 * width]).astype(BF)
    kv[0, :, width : 2 * width] = (
        dot(n1[...], full_a[:, 2 * width : 3 * width]) + par[6:7, width : 2 * width]
    ).astype(BF)
    swap = remote(kv.at[0], kv.at[1], kv_s.at[0], kv_r.at[0], here.sib)
    swap.start()
    outs.put(full_a, a_o)
    outs.put(q, q_o)
    go.arrive()
    outs.put(full_o, o_o)
    swap.wait_recv()
    outs.put(kv, kv_o)
    blk = rows_all // 2

    def head(i, _):
        h = i // 2
        rows = pl.ds(al((i - 2 * h) * blk, blk), blk)
        kc = pl.ds(al(h * HD, HD), HD)
        vc = pl.ds(al(width + h * HD, HD), HD)
        ids = col[rows, :]
        qh = q[rows, kc]
        near = allowed_scores(qh, kv[0, :, kc], ids, row[0:1, :], scale)
        far = allowed_scores(qh, kv[1, :, kc], ids, row[1:2, :], scale)
        top = jnp.maximum(
            jnp.max(near, axis=-1, keepdims=True), jnp.max(far, axis=-1, keepdims=True)
        )
        near = jnp.exp(near - top)
        far = jnp.exp(far - top)
        total = jnp.sum(near, axis=-1, keepdims=True) + jnp.sum(far, axis=-1, keepdims=True)
        inv = 1.0 / total
        out = dot((near * inv).astype(BF), kv[0, :, vc]) + dot((far * inv).astype(BF), kv[1, :, vc])
        ctx[rows, kc] = out.astype(BF)
        return 0

    lax.fori_loop(0, 2 * heads, head, 0)
    outs.put(ctx, ctx_o)

    def project(s, _):
        cols = pl.ds(al(s * shard, shard), shard)
        part[:, cols] = dot(ctx[...], full_o[s]).astype(BF)
        return 0

    lax.fori_loop(0, 2 * n_f, project, 0)
    line = Line(here, part, rbuf, norm, (ls_s, ls_r, lg_s, lg_r), chunks, lag)

    def final(rows, span, total):
        middle = tokv[rows, :].astype(F32) + total + par[2:3, :]
        mid[span, :] = middle
        scaled, _spread = norm_rows(middle)
        norm[rows, :] = (scaled * par[3:4, :] + par[4:5, :]).astype(BF)

    ticks = line.ticks()
    events = []
    for s in range(1, here.m):
        events += [functools.partial(gr.step, s), functools.partial(ge.step, s)]
    when = [1 + (ticks // 2) * i // max(1, len(events) - 1) for i in range(len(events))]
    events.append(functools.partial(gr.step, here.m))
    when.append(ticks - 2)

    def tick(tau, _):
        line.tick(tau, final)
        for at, event in zip(when, events):
            pl.when(tau == at)(event)
        return 0

    lax.fori_loop(0, ticks, tick, 0)
    outs.put(mid, mid_o)
    outs.put(norm, n2_o)
    ge.step(here.m)
    gr.arrive()
    ge.arrive()
    line.finish_sum()
    line.finish_back()
    for gather in (ga, go, gr, ge):
        gather.finish()
    to_sib.wait_send()
    for k in range(1, n_f):
        small_copy(k).wait_send()
    swap.wait_send()
    outs.wait()


def forward(n_f, n_t, tok, col, row, small, wa, wo, we, wr, chunks=16, lag=3):
    rows, model = tok.shape
    shard, width, ff = wa.shape[0], wo.shape[0], we.shape[1]
    n_s = 2 * n_f
    sds = jax.ShapeDtypeStruct
    dma = pltpu.SemaphoreType.DMA
    outs = (
        sds((rows, model), BF),
        sds((rows, width), BF),
        sds((2, rows, 2 * width), BF),
        sds((rows, width), BF),
        sds((rows, model), BF),
        sds((rows // 2, model), F32),
        sds((8, model), F32),
        sds((model, 3 * width), BF),
        sds((n_s, width, shard), BF),
        sds((model, ff), BF),
        sds((n_s, ff, shard), BF),
    )
    v = pltpu.VMEM
    return pl.pallas_call(
        functools.partial(forward_kernel, n_f, n_t, chunks, lag),
        out_shape=outs,
        in_specs=[ANY, VM, VM, VM, ANY, ANY, ANY, ANY],
        out_specs=(ANY,) * len(outs),
        scratch_shapes=[
            v((rows, model), BF), v((rows, model), BF), v((model, 3 * width), BF),
            v((n_s, width, shard), BF), v((shard, ff), BF), v((ff, shard), BF),
            v((rows, width), BF), v((2, rows, 2 * width), BF), v((rows, width), BF),
            v((rows, model), BF), v((2, rows // 2, model), BF), v((rows, model), BF),
            v((rows // 2, model), F32), v((8, model), F32), v((n_f, 8, model), F32),
            v((8, model), F32),
        ]
        + [dma((Gather.sems(n_f),))] * 8
        + Line.sems(chunks)
        + [dma((n_f,)), dma((n_f,)), dma((1,)), dma((1,)), dma((5,)), dma((16,))],
        compiler_params=pltpu.CompilerParams(
            collective_id=0, has_side_effects=True, vmem_limit_bytes=60 << 20
        ),
        cost_estimate=pl.CostEstimate(
            flops=8 * 10**9, bytes_accessed=60 * 10**6, transcendentals=10**6
        ),
        name="attention_forward",
    )(tok, col, row, small, wa, wo, we, wr)


def norm_back(grad_normed, scaled, spread, gain):
    weighted = grad_normed * gain
    inner = (
        weighted
        - jnp.mean(weighted, axis=-1, keepdims=True)
        - scaled * jnp.mean(weighted * scaled, axis=-1, keepdims=True)
    )
    return (inner * spread, jnp.sum(grad_normed * scaled, axis=0), jnp.sum(grad_normed, axis=0))


def gelu_exact(values):
    return 0.5 * values * (1.0 + lax.erf(values * (1.0 / math.sqrt(2.0))))


def masked_scores(queries, keys, query_ids, key_ids, scale):
    scores = jnp.einsum("qhd,khd->hqk", queries, keys, preferred_element_type=jnp.float32) * scale
    allowed = key_ids[None, None, :] <= query_ids[None, :, None]
    return jnp.where(allowed, scores, -1e30)


def attend_backward(queries, keys, values, query_ids, key_ids, grad_context, scale):
    scores = masked_scores(queries, keys, query_ids, key_ids, scale)
    probs = jax.nn.softmax(scores, axis=-1)
    grad_probs = jnp.einsum(
        "qhd,khd->hqk", grad_context, values, preferred_element_type=jnp.float32
    )
    inner = jnp.sum(grad_probs * probs, axis=-1, keepdims=True)
    grad_scores = (probs * (grad_probs - inner)).astype(jnp.bfloat16)
    grad_queries = (
        jnp.einsum("hqk,khd->qhd", grad_scores, keys, preferred_element_type=jnp.float32) * scale
    )
    grad_keys = (
        jnp.einsum("hqk,qhd->khd", grad_scores, queries, preferred_element_type=jnp.float32) * scale
    )
    grad_values = jnp.einsum(
        "hqk,qhd->khd", probs.astype(jnp.bfloat16), grad_context, preferred_element_type=jnp.float32
    )
    return (grad_queries, grad_keys, grad_values)


def shifted(block, axis, distance):
    devices = range(lax.axis_size(axis))
    route = [((i - distance) % len(devices), i) for i in devices]
    return lax.ppermute(block, axis, route)


def spread_out(piece, index, count):
    spots = (jnp.arange(count) == index).astype(F32)
    return (piece[:, None, :] * spots[None, :, None]).reshape(piece.shape[0], -1)


def local(
    tokens, cotangent, block_ids, live_count, first_gain, first_shift, query_weight, query_bias,
    key_weight, value_weight, value_bias, output_weight, output_bias, second_gain, second_shift,
    expand_weight, expand_bias, reduce_weight, reduce_bias,
):
    n_f, n_t = lax.axis_size("fsdp"), lax.axis_size("tp")
    n_s = 2 * n_f
    _, rows, model = tokens.shape
    c = lax.axis_index("ctx")
    index = 2 * lax.axis_index("fsdp") + c
    width, ff = query_weight.shape[1], expand_weight.shape[1]
    shard = query_weight.shape[0]
    heads = width // HD
    scale = 1.0 / math.sqrt(HD)
    vectors = jnp.stack(
        [first_gain, first_shift, output_bias, second_gain, second_shift, reduce_bias]
    ).astype(F32)

    def wide(bias):
        full = spread_out(bias.astype(F32), index, n_s)
        flat = full.reshape(1, -1)
        return jnp.pad(flat, ((0, 0), (0, model - flat.shape[1])))

    heads_bias = jnp.concatenate([query_bias, value_bias], axis=0)
    small = jnp.concatenate([spread_out(vectors, index, n_s), wide(heads_bias), wide(expand_bias)])
    ids = block_ids[0].reshape(2, rows)
    near, far = lax.dynamic_index_in_dim(ids, c, 0), lax.dynamic_index_in_dim(ids, 1 - c, 0)
    row = jnp.concatenate([near, far])
    col = near.reshape(rows, 1)
    wa = jnp.concatenate([query_weight, key_weight, value_weight], axis=1)
    tok = tokens.reshape(rows, model)
    n1, q, kv, context_low, n2, mid, par, full_a, full_o, full_e, full_r = forward(
        n_f, n_t, tok, col, row, small, wa, output_weight, expand_weight, reduce_weight
    )
    mids = lax.all_gather(mid, "tp")
    middle = jnp.concatenate([mids[0], mids[n_t - 1]])
    inputs = tok.astype(F32)
    scaled_one, spread_one = norm_rows(inputs)
    scaled_two, spread_two = norm_rows(middle)
    flat_r = full_r.transpose(1, 0, 2).reshape(ff, model)
    flat_o = full_o.transpose(1, 0, 2).reshape(width, model)
    row_live = live_count[0].astype(F32)
    hidden = dot(n2, full_e) + par[7:8, :ff]
    active, gelu_pull = jax.vjp(gelu_exact, hidden)
    active_low = active.astype(BF)
    mlp_term = dot(active_low, flat_r)
    layer_out = ((middle + lax.psum(mlp_term, "tp") + par[5:6]) * row_live).astype(BF)
    grad_out = cotangent.astype(F32).reshape(rows, model) * row_live
    grad_low = grad_out.astype(BF)
    reduce_bias_grad = jnp.sum(grad_out, axis=0)
    reduce_weight_grad = dot_tn(active_low, grad_low)
    grad_hidden = gelu_pull(dot_nt(grad_low, flat_r))[0].astype(BF)
    expand_bias_grad = jnp.sum(grad_hidden.astype(F32), axis=0)
    expand_weight_grad = dot_tn(n2, grad_hidden)
    grad_normed_two = lax.psum(dot_nt(grad_hidden, full_e), "tp")
    norm_part_two, second_gain_grad, second_shift_grad = norm_back(
        grad_normed_two, scaled_two, spread_two, par[3:4]
    )
    grad_middle = grad_out + norm_part_two
    grad_branch = grad_middle.astype(BF)
    output_bias_grad = jnp.sum(grad_branch.astype(F32), axis=0)
    output_weight_grad = dot_tn(context_low, grad_branch)
    grad_context = dot_nt(grad_branch, flat_o).astype(BF)
    hs = (rows, heads, HD)
    keys = kv[:, :, :width].reshape(2 * rows, heads, HD)
    values = kv[:, :, width:].reshape(2 * rows, heads, HD)
    gq, gk, gv = attend_backward(
        q.reshape(hs), keys, values, near[0], row.reshape(-1), grad_context.reshape(hs), scale
    )
    gk, gv = gk.reshape(2 * rows, width), gv.reshape(2 * rows, width)
    back_k = shifted(gk[rows:].astype(BF), "ctx", 1).astype(F32)
    back_v = shifted(gv[rows:].astype(BF), "ctx", 1).astype(F32)
    grads = jnp.concatenate(
        [gq.reshape(rows, width), gk[:rows] + back_k, gv[:rows] + back_v], axis=1
    ).astype(BF)
    sums = jnp.sum(grads.astype(F32), axis=0)
    query_bias_grad, value_bias_grad = sums[:width], sums[2 * width :]
    wa_grad = dot_tn(n1, grads)
    grad_normed_one = lax.psum(dot_nt(grads, full_a), "tp")
    norm_part_one, first_gain_grad, first_shift_grad = norm_back(
        grad_normed_one, scaled_one, spread_one, par[0:1]
    )
    tokens_grad = (grad_middle + norm_part_one).astype(BF)
    both = ("fsdp", "ctx")

    def scatter(value, dim):
        low = value.astype(BF)
        return lax.psum_scatter(low, both, scatter_dimension=dim, tiled=True).astype(F32)

    wa_mine = scatter(wa_grad, 0)
    return (
        layer_out.reshape(1, rows, model),
        tokens_grad.reshape(1, rows, model),
        scatter(first_gain_grad, 0),
        scatter(first_shift_grad, 0),
        wa_mine[:, :width],
        scatter(query_bias_grad.reshape(heads, HD), 1),
        wa_mine[:, width : 2 * width],
        wa_mine[:, 2 * width :],
        scatter(value_bias_grad.reshape(heads, HD), 1),
        scatter(output_weight_grad, 1),
        scatter(output_bias_grad, 0),
        scatter(second_gain_grad, 0),
        scatter(second_shift_grad, 0),
        scatter(expand_weight_grad, 0),
        scatter(expand_bias_grad.reshape(expand_bias.shape[0], -1), 1),
        scatter(reduce_weight_grad, 1),
        scatter(reduce_bias_grad, 0),
    )


def solution(mesh):
    tokens, vector = P("fsdp", "ctx", None), P(("fsdp", "ctx"))
    down, across = P(("fsdp", "ctx"), "tp"), P("tp", ("fsdp", "ctx"))
    return jax.shard_map(
        local,
        mesh=mesh,
        in_specs=(
            tokens, tokens, P("fsdp", None), P("fsdp"), vector, vector, down, across, down, down,
            across, across, vector, vector, vector, down, across, across, vector,
        ),
        out_specs=(
            tokens, tokens, vector, vector, down, across, down, down, across, across, vector,
            vector, vector, down, across, across, vector,
        ),
        check_vma=False,
    )
```

time: 1360 us -> 844 us (0.62)
  waiting for transfers between devices: 1040 us -> 490 us
  Pallas kernels: 0 us -> 128 us
  blocking collectives: 103 us -> 23.8 us
  matrix products: 114 us -> 86.4 us
  local copies, waits for them, and re-layouts: 20.5 us -> 41.5 us
    reduce_scatter x6 -> x4, waiting for transfers between devices: 317 us -> 43.6 us  [scatter(): lax.psum_scatter(low, both, scatter_dimension=dim, tiled=True).astype(F32)]
    psum x3 -> x2, waiting for transfers between devices: 563 us -> 354 us  [the longest x1 202 us: local(): lax.psum(mlp_term, 'tp')]
    pallas_call x0 -> x1, Pallas kernels: none -> 128 us  [forward(): pl.pallas_call(functools.partial(forward_kernel, n_f, n_t, chunks, lag),...]
    all_gather x9 -> x0, blocking collectives: 79.6 us -> none  [the longest x1 10.4 us: local(): lax.all_gather(first_shift, ('fsdp', 'ctx'), axis=0, tiled=True)]
    all_gather x6 -> x1, waiting for transfers between devices: 146 us -> 74.9 us  [local(): mids = lax.all_gather(mid, 'tp')]
    dot_general x20 -> x10, matrix products: 103 us -> 73 us  [the longest x4 31.4 us: dot_tn(): lax.dot_general(left, right, (((0,), (0,)), ((), ())), preferred_element_...]
    transpose x0 -> x2, local copies, waits for them, and re-layouts: none -> 14.2 us  [the longest x1 11.8 us: local(): flat_r = full_r.transpose(1, 0, 2).reshape(ff, model)]
  transfers between devices with their start and end apart: 22 -> 12, of which waited for: 16 -> 5; matrix products, arithmetic and copies ran while one was open for 11% -> 18% of each run, Pallas kernels for 0% -> 0%
where the time goes in v1:
time: 844 us; the launch traced here: 835 us
  waiting for transfers between devices  490 us (58%)
  Pallas kernels  128 us (15%)
  matrix products  86.4 us (10%)
  other arithmetic  46 us (5%)
  local copies, waits for them, and re-layouts  41.5 us (5%)
  blocking collectives  23.8 us (3%)
  between operations  17.6 us (2%)
    psum x1, waiting for transfers between devices, local(): lax.psum(mlp_term, 'tp')  202 us
    psum x1, waiting for transfers between devices, local(): grad_normed_two = lax.psum(dot_nt(grad_hidden, full_e), 'tp')  152 us
    pallas_call x1, Pallas kernels, forward(): pl.pallas_call(functools.partial(forward_kernel, n_f, n_t, chunks, lag),...  128 us
    all_gather x1, waiting for transfers between devices, local(): mids = lax.all_gather(mid, 'tp')  74.9 us
    reduce_scatter x4, waiting for transfers between devices, scatter(): lax.psum_scatter(low, both, scatter_dimension=dim, tiled=True).astype(F32)  43.6 us
    dot_general x4, matrix products, dot_tn(): lax.dot_general(left, right, (((0,), (0,)), ((), ())), preferred_element_...  31.4 us
    unnamed x1, blocking collectives  23.8 us
    dot_general x4, matrix products, dot_nt(): lax.dot_general(left, right, (((1,), (1,)), ((), ())), preferred_element_...  22 us
  transfers between devices with their start and end apart: 12, of which 5 were waited for; matrix products, arithmetic and copies ran while one was open for 18% of the time, Pallas kernels for 0%

profile of v1, /device:TPU:0, one launch (start us, length us, event | category | flops | bytes accessed | tf_op | source)
XLA Modules:
  0.0 835.3 jit_solution(4283858880914409595)
XLA Ops:
  17.9 2.0 pad_maximum_fusion.2.wa
  20.0 127.6 %attention_forward.1 = (bf16[512,2048]{1,0:T(8,128)(2,1)}, bf16[512,512]{1,0:T(8,128)(2,1)}, bf16[2,512,1024]{2,1,0:T(8,128)(2,1)}, bf16[512,512]{1,0:T(8,128)(2...) custom-call(bf16[512,2048]{1,0:T(8,128)(2,1)} %bitcast.96, ...), custom_call_target="tpu_custom_call" | custom-call | flops 8000000000 | bytes 60000000 | tf_op jit(solution)/shard_map/attention_forward/pallas_call | solution.py:532
  147.7 11.8 %copy.52 = bf16[2048,8,256]{0,2,1:T(8,128)(2,1)} copy(bf16[2048,8,256]{2,0,1:T(8,128)(2,1)} %bitcast.101) | data formatting | bytes 16777216 | tf_op jit(solution)/shard_map/transpose | solution.py:648
  160.3 9.1 %multiply_convert_fusion.2 = (bf16[512,2048]{1,0:T(8,128)(2,1)}, f32[512,2048]{1,0:T(8,128)S(1)}) fusion(f32[2048]{0:T(1024)S(1)} %bitcast.125, bf16[512,2048]{1,0:T(8,128)(2,1)} %get-tuple-element.29, bf16[2048,2048]{1,0:T(8,128)(2,1)} %get-tuple-element.30), kind=kOutput, calls=%fused_computation.39 | convolution fusion | flops 4301258752 | bytes 16785408 | tf_op jit(solution)/shard_map/dot_general | solution.py:22
  169.3 6.8 fusion.55
  177.4 6.1 fusion.57
  185.0 10.0 %convolution_convert_fusion.1 = bf16[2048,2048]{1,0:T(8,128)(2,1)} fusion(bf16[512,2048]{1,0:T(8,128)(2,1)} %get-tuple-element.29, bf16[512,2048]{1,0:T(8,128)(2,1)} %copy-done.21), kind=kOutput, calls=%fused_computation.6 | convolution fusion | flops 4299161600 | bytes 12582912 | tf_op jit(solution)/shard_map/dot_general | solution.py:30
  195.1 8.5 %convolution_convert_fusion = bf16[2048,2048]{1,0:T(8,128)(2,1)} fusion(bf16[512,2048]{1,0:T(8,128)(2,1)} %get-tuple-element.74, bf16[1,512,2048]{2,1,0:T(8,128)(2,1)S(1)} %copy-done.8, f32[]{:T(128)} %bitcast.6), kind=kOutput, calls=%fused_computation.5 | convolution fusion | flops 4302307328 | bytes 12582916 | tf_op jit(solution)/shard_map/dot_general | solution.py:30
  205.2 2.4 copy.55
  212.7 7.4 fusion.54
  220.1 74.9 %all-gather.3.cloned.1.call-done = f32[1024,2048]{1,0:T(8,128)} async-done(((f32[256,2048]{1,0:T(8,128)}), f32[1024,2048]{1,0:T(8,128)}) %all-gather.3.cloned.1.call-update) | async-done | bytes 8388624 | tf_op jit(solution)/shard_map/all_gather | solution.py:643
  295.0 2.5 fusion.50
  298.8 151.7 %all-reduce.12.cloned.1.call-done = f32[512,2048]{1,0:T(8,128)} async-done(((f32[512,2048]{1,0:T(8,128)}), f32[512,2048]{1,0:T(8,128)}) %all-reduce.12.cloned.1.call-update) | async-done | bytes 4194320 | tf_op jit(solution)/shard_map/psum | solution.py:663
  450.5 4.1 multiply_reduce_fusion.1
  455.8 2.5 convert_reduce_fusion.1
  461.1 2.6 multiply_reduce_fusion
  471.0 5.0 convolution_convert_fusion.3
  476.1 10.6 %fusion.56 = f32[512,2048]{1,0:T(8,128)} fusion(bf16[512,2048]{1,0:T(8,128)(2,1)} %get-tuple-element.74, bf16[2048,2048]{0,1:T(8,128)(2,1)} %bitcast.97), kind=kOutput, calls=%fused_computation.115 | convolution fusion | flops 4294967296 | bytes 14680064 | tf_op jit(solution)/shard_map/dot_general | solution.py:22
  486.7 7.8 fusion.49
  494.8 7.9 convolution_convert_fusion.2
  504.6 2.1 convert_reduce_fusion
  506.7 2.3 fusion.13
  510.9 2.8 convert_element_type.212
  513.7 2.7 convert_element_type.217
  517.8 17.8 %reduce-scatter.24.cloned.1.call-done = bf16[16,4]{1,0:T(8,128)(2,1)} async-done(((bf16[128,4]{1,0:T(8,128)(2,1)}), bf16[16,4]{1,0:T(8,128)(2,1)}) %reduce-scatter.24.cloned.1.call-update) | async-done | bytes 144
  536.9 43.5 %reduce-scatter.16.cloned.1.call-done = bf16[512,256]{1,0:T(8,128)(2,1)} async-done(((bf16[512,2048]{1,0:T(8,128)(2,1)}), bf16[512,256]{1,0:T(8,128)(2,1)}) %reduce-scatter.16.cloned.1.call-update) | async-done | bytes 262160 | tf_op jit(solution)/shard_map/reduce_scatter | solution.py:696
  582.3 202.2 %all-reduce.14.cloned.1.call-done = (f32[512,2048]{1,0:T(8,128)}, f32[512,2048]{1,0:T(8,128)}) async-done(((f32[512,2048]{1,0:T(8,128)}, f32[512,2048]{1,0:T(8,128)}), (f32[512,2048]{1,0:T(8,128)}, f32[512,2048]{1,0:T(8,128)})) %all-reduce.14.cloned.1.call-update) | async-done | bytes 8388624 | tf_op jit(solution)/shard_map/psum | solution.py:655
  784.5 3.8 fusion.12
  788.3 23.8 %all-reduce.8 = (bf16[2048]{0:T(1024)(128)(2,1)S(1)}, bf16[2048]{0:T(1024)(128)(2,1)S(1)}, bf16[2048]{0:T(1024)(128)(2,1)S(1)}, bf16[2048]{0:T(1024)(128)(2,1)S(...) all-reduce(bf16[2048]{0:T(1024)(128)(2,1)S(1)} %get-tuple-element.4, ...), channel_id=3, replica_groups=mesh['fsdp'=4,'ctx'=2,'tp'=4] {'fsdp','ctx'}, use_global_device_ids=true, to_apply=%region_15.16.clone | all-reduce | flops 12288 | bytes 49152
  816.0 5.4 fusion.21
  822.6 2.8 fusion.27
  825.4 2.3 fusion.52
  (160 shorter events, 44.8 us)
Async XLA Ops:
  8.0 286.9 %all-gather.3.cloned.1.call-start = ((), (), s32[]{:S(2)}) async-start(), calls=%async_computation.12 | async-start | bytes 10485760 | tf_op jit(solution)/shard_map/all_gather | solution.py:643
  147.6 302.9 %all-reduce.12.cloned.1.call-start = ((), (), s32[]{:S(2)}) async-start(), calls=%async_computation.7 | async-start | bytes 8388608 | tf_op jit(solution)/shard_map/psum | solution.py:663
  147.7 12.5 %copy-start.19 = (f32[8,2048]{1,0:T(8,128)S(1)}, f32[8,2048]{1,0:T(8,128)}, u32[]{:S(2)}) copy-start(f32[8,2048]{1,0:T(8,128)} %get-tuple-element.31) | copy-start | bytes 196612
  160.2 9.1 %copy-start.7 = (bf16[2048,8,256]{0,2,1:T(8,128)(2,1)S(1)}, bf16[2048,8,256]{0,2,1:T(8,128)(2,1)}, u32[]{:S(2)}) copy-start(bf16[2048,8,256]{0,2,1:T(8,128)(2,1)} %copy.52) | copy-start | bytes 25165828
  160.2 9.1 %copy-start.8 = (bf16[1,512,2048]{2,1,0:T(8,128)(2,1)S(1)}, bf16[1,512,2048]{2,1,0:T(8,128)(2,1)}, u32[]{:S(2)}) copy-start(bf16[1,512,2048]{2,1,0:T(8,128)(2,1)} %param.20) | copy-start | bytes 6291460
  160.2 17.2 %slice-start.3 = ((s8[8388608]{0:T(1024)(128)(4,1)}), s8[4194304]{0:T(1024)(128)(4,1)S(1)}, s32[]{:S(2)}) async-start(s8[8388608]{0:T(1024)(128)(4,1)} %bitcast.131), calls=%async_computation.20 | async-start | bytes 8388608
  169.3 8.1 slice-start.4
  183.5 326.0 %reduce-scatter.26.cloned.1.call-start = ((), (), s32[]{:S(2)}) async-start(), calls=%async_computation.15 | async-start | bytes 147456
  184.4 326.5 %reduce-scatter.18.cloned.1.call-start = ((), (), s32[]{:S(2)}) async-start(), calls=%async_computation.10 | async-start | bytes 9437184 | tf_op jit(solution)/shard_map/reduce_scatter | solution.py:696
  195.0 318.7 %reduce-scatter.20.cloned.1.call-start = ((), (), s32[]{:S(2)}) async-start(), calls=%async_computation.11 | async-start | bytes 9437184 | tf_op jit(solution)/shard_map/reduce_scatter | solution.py:696
  203.6 3.9 copy-start.18
  203.6 312.8 %reduce-scatter.22.cloned.1.call-start = ((), (), s32[]{:S(2)}) async-start(), calls=%async_computation.13 | async-start | bytes 36864
  450.5 4.2 copy-start.1
  450.5 4.7 copy-start.4
  450.5 5.3 copy-start.9
  454.7 5.0 slice-start
  455.8 2.5 copy-start.14
  455.8 3.9 slice-start.1
  458.4 2.5 copy-start.5
  460.9 5.1 copy-start.11
  461.0 7.3 collective-permute-start.1
  466.1 2.3 slice-start.2
  466.2 2.3 collective-permute-start
  470.2 65.4 %reduce-scatter.24.cloned.1.call-start = ((), (), s32[]{:S(2)}) async-start(), calls=%async_computation.14 | async-start | bytes 36864
  471.0 109.5 %reduce-scatter.16.cloned.1.call-start = ((), (), s32[]{:S(2)}) async-start(), calls=%async_computation.9 | async-start | bytes 2359296 | tf_op jit(solution)/shard_map/reduce_scatter | solution.py:696
  476.0 308.5 %all-reduce.14.cloned.1.call-start = ((), (), s32[]{:S(2)}) async-start(), calls=%async_computation.16 | async-start | bytes 16777216 | tf_op jit(solution)/shard_map/psum | solution.py:655
  476.1 10.6 %copy-start.16 = (bf16[4,128,512]{2,1,0:T(8,128)(2,1)S(1)}, bf16[4,128,512]{2,1,0:T(8,128)(2,1)}, u32[]{:S(2)}) copy-start(bf16[4,128,512]{2,1,0:T(8,128)(2,1)} %copy-done.15) | copy-start | bytes 1572868
  494.5 330.9 %reduce-scatter.14.cloned.1.call-start = ((), (), s32[]{:S(2)}) async-start(), calls=%async_computation.8 | async-start | bytes 7077888 | tf_op jit(solution)/shard_map/reduce_scatter | solution.py:696
  504.6 4.4 copy-start.10
  815.9 5.4 copy-start.2
  816.0 5.4 copy-start.3
  816.0 6.7 copy-start.6
  (7 other events, 8.6 us)
Sparse Core Ops, SparseCore 0:
  147.8 147.1 all-gather.2
  297.3 153.1 all-reduce.11
  494.6 289.7 all-reduce.13
Sparse Core Ops, SparseCore 1:
  187.6 31.4 reduce-scatter.25
  222.4 71.3 reduce-scatter.17
  297.1 71.1 reduce-scatter.19
  470.3 30.3 reduce-scatter.21
  504.2 31.3 reduce-scatter.23
  539.5 41.0 reduce-scatter.15
  583.7 61.5 reduce-scatter.13

commit v2 on v1

--- a/solution.py
+++ b/solution.py
@@ -63,13 +63,19 @@
     def plane(self, k):
         return (lax.rem(self.f + k, self.n_f), self.c, self.t)
 
-    def greet(self):
+    def greet_signal(self):
         bar = pltpu.get_barrier_semaphore()
         others = [self.sib] + [self.plane(k) for k in range(1, self.n_f)]
         others += [self.tp(k) for k in range(1, self.n_t)]
         for other in others:
             pl.semaphore_signal(bar, 1, device_id=other, device_id_type=MESH)
-        pl.semaphore_wait(bar, len(others))
+
+    def greet_wait(self):
+        pl.semaphore_wait(pltpu.get_barrier_semaphore(), self.n_f + self.n_t - 1)
+
+    def greet(self):
+        self.greet_signal()
+        self.greet_wait()
 
 
 def remote(src, dst, send, recv, to):
@@ -317,13 +323,14 @@
     return slot
 
 
-def lead_slots(ref):
-    size = ref.shape[1]
+def column_slots(ref, width):
+    size = ref.shape[0]
 
     def slot(idx, part):
+        cols = pl.ds(al(idx * width, width), width)
         if part is None:
-            return ref.at[idx]
-        return ref.at[idx, pl.ds(part * (size // 2), size // 2)]
+            return ref.at[:, cols]
+        return ref.at[pl.ds(part * (size // 2), size // 2), cols]
 
     return slot
 
@@ -361,8 +368,8 @@
     tok_in = pltpu.make_async_copy(tok, tokv, in_sem.at[0])
     tok_in.start()
     me = 2 * here.f + here.c
-    a_slot, o_slot = row_slots(full_a, shard), lead_slots(full_o)
-    e_slot, r_slot = row_slots(e_o, shard), lead_slots(r_o)
+    a_slot, o_slot = row_slots(full_a, shard), column_slots(full_o, shard)
+    e_slot, r_slot = row_slots(e_o, shard), column_slots(r_o, shard)
     loads = [
         pltpu.make_async_copy(wo, o_slot(me, None), in_sem.at[1]),
         pltpu.make_async_copy(wa, a_slot(me, None), in_sem.at[2]),
@@ -464,12 +471,14 @@
     lax.fori_loop(0, 2 * heads, head, 0)
     outs.put(ctx, ctx_o)
 
-    def project(s, _):
-        cols = pl.ds(al(s * shard, shard), shard)
-        part[:, cols] = dot(ctx[...], full_o[s]).astype(BF)
+    wide = model // 4
+
+    def project(i, _):
+        cols = pl.ds(al(i * wide, wide), wide)
+        part[:, cols] = dot(ctx[...], full_o[:, cols]).astype(BF)
         return 0
 
-    lax.fori_loop(0, 2 * n_f, project, 0)
+    lax.fori_loop(0, 4, project, 0)
     line = Line(here, part, rbuf, norm, (ls_s, ls_r, lg_s, lg_r), chunks, lag)
 
     def final(rows, span, total):
@@ -512,7 +521,6 @@
 def forward(n_f, n_t, tok, col, row, small, wa, wo, we, wr, chunks=16, lag=3):
     rows, model = tok.shape
     shard, width, ff = wa.shape[0], wo.shape[0], we.shape[1]
-    n_s = 2 * n_f
     sds = jax.ShapeDtypeStruct
     dma = pltpu.SemaphoreType.DMA
     outs = (
@@ -524,9 +532,9 @@
         sds((rows // 2, model), F32),
         sds((8, model), F32),
         sds((model, 3 * width), BF),
-        sds((n_s, width, shard), BF),
+        sds((width, model), BF),
         sds((model, ff), BF),
-        sds((n_s, ff, shard), BF),
+        sds((ff, model), BF),
     )
     v = pltpu.VMEM
     return pl.pallas_call(
@@ -536,7 +544,7 @@
         out_specs=(ANY,) * len(outs),
         scratch_shapes=[
             v((rows, model), BF), v((rows, model), BF), v((model, 3 * width), BF),
-            v((n_s, width, shard), BF), v((shard, ff), BF), v((ff, shard), BF),
+            v((width, model), BF), v((shard, ff), BF), v((ff, shard), BF),
             v((rows, width), BF), v((2, rows, 2 * width), BF), v((rows, width), BF),
             v((rows, model), BF), v((2, rows // 2, model), BF), v((rows, model), BF),
             v((rows // 2, model), F32), v((8, model), F32), v((n_f, 8, model), F32),
@@ -555,50 +563,657 @@
     )(tok, col, row, small, wa, wo, we, wr)
 
 
-def norm_back(grad_normed, scaled, spread, gain):
-    weighted = grad_normed * gain
+class Scatter:
+    def __init__(self, here, sums, stage, ring_half, ring_full, send, recv, block):
+        self.here, self.sums, self.stage = here, sums, stage
+        self.ring_half, self.ring_full = ring_half, ring_full
+        self.send, self.recv, self.block = send, recv, block
+        self.m, self.size = here.m, sums.shape[1]
+
+    def offset(self, i):
+        odd = lax.rem(i, 2)
+        return self.m + (1 - 2 * odd) * ((i + 1) // 2)
+
+    def shard(self, i, other):
+        return self.here.shard(self.offset(i), other)
+
+    def cross(self, i):
+        slot = self.sums.at[self.here.owner(self.offset(i))]
+        n = 2 * self.m + i
+        return remote(self.stage(i), slot, self.send.at[n], self.recv.at[n], self.here.sib)
+
+    def combine(self, i, own):
+        f = self.here.owner(self.offset(i))
+        self.sums[f] = (own + self.sums[f].astype(F32)).astype(BF)
+
+    def slot(self, k, half):
+        f = self.here.owner(k)
+        if half is None:
+            return self.sums.at[f]
+        return self.sums.at[f, pl.ds(half * (self.size // 2), self.size // 2)]
+
+    def hop(self, way, s):
+        here, sign = self.here, (1, -1)[way]
+        half = way if s == self.m else None
+        dst = self.ring_half.at[way] if s == self.m else self.ring_full.at[way, s - 1]
+        n = way * self.m + s - 1
+        to = (here.right, here.left)[way]
+        return remote(self.slot(sign * s, half), dst, self.send.at[n], self.recv.at[n], to)
+
+    def launch(self, s):
+        self.hop(0, s).start()
+        self.hop(1, s).start()
+
+    def absorb(self, s):
+        for way in (0, 1):
+            sign = (1, -1)[way]
+            self.hop(way, s).wait_recv()
+            f = self.here.owner(sign * (s - 1))
+            base = way * (self.size // 2) if s == self.m else 0
+            count = (self.size // 2 if s == self.m else self.size) // self.block
+
+            def body(i, _, way=way, f=f, base=base):
+                there = pl.ds(al(base + i * self.block, self.block), self.block)
+                here_rows = pl.ds(al(i * self.block, self.block), self.block)
+                if s == self.m:
+                    got = self.ring_half[way, here_rows, :]
+                else:
+                    got = self.ring_full[way, s - 1, here_rows, :]
+                self.sums[f, there, :] = (
+                    self.sums[f, there, :].astype(F32) + got.astype(F32)
+                ).astype(BF)
+                return 0
+
+            lax.fori_loop(0, count, body, 0)
+
+    def finish(self, crossed=True):
+        for s in range(1, self.m + 1):
+            self.hop(0, s).wait_send()
+            self.hop(1, s).wait_send()
+        if crossed:
+            for i in range(2 * self.m):
+                self.cross(i).wait_send()
+
+    @staticmethod
+    def buffers(n_f, rows, cols):
+        v = pltpu.VMEM
+        m = n_f // 2
+        return [
+            v((n_f, rows, cols), BF),
+            v((2, rows // 2, cols), BF),
+            v((2, max(1, m - 1), rows, cols), BF),
+        ]
+
+    @staticmethod
+    def sems(n_f):
+        return [pltpu.SemaphoreType.DMA((2 * n_f,))] * 2
+
+
+def norm_back_rows(total, scaled, spread, gain):
+    e = total * gain
     inner = (
-        weighted
-        - jnp.mean(weighted, axis=-1, keepdims=True)
-        - scaled * jnp.mean(weighted * scaled, axis=-1, keepdims=True)
+        e
+        - jnp.mean(e, axis=-1, keepdims=True)
+        - scaled * jnp.mean(e * scaled, axis=-1, keepdims=True)
     )
-    return (inner * spread, jnp.sum(grad_normed * scaled, axis=0), jnp.sum(grad_normed, axis=0))
-
-
-def gelu_exact(values):
-    return 0.5 * values * (1.0 + lax.erf(values * (1.0 / math.sqrt(2.0))))
-
-
-def masked_scores(queries, keys, query_ids, key_ids, scale):
-    scores = jnp.einsum("qhd,khd->hqk", queries, keys, preferred_element_type=jnp.float32) * scale
-    allowed = key_ids[None, None, :] <= query_ids[None, :, None]
-    return jnp.where(allowed, scores, -1e30)
-
-
-def attend_backward(queries, keys, values, query_ids, key_ids, grad_context, scale):
-    scores = masked_scores(queries, keys, query_ids, key_ids, scale)
-    probs = jax.nn.softmax(scores, axis=-1)
-    grad_probs = jnp.einsum(
-        "qhd,khd->hqk", grad_context, values, preferred_element_type=jnp.float32
+    return inner * spread
+
+
+def span_when(tau, start, stop, task):
+    @pl.when((tau >= start) & (tau < stop))
+    def _():
+        task(tau - start)
+
+
+def middle_kernel(
+    n_f, n_t, chunks, lag,
+    live, n2_i, cot, mid_i, par, full_e, full_r,
+    gb_o, lo_o, gm_o, eg_o, pr_o, sums_o,
+    ev, rv, n2, g, act, gh, part, part2, rbuf, rbuf2, gb, mid, gm, lo, sums,
+    e_sum, e_half, e_full, r_sum,
+    e_s, e_r, r_s, r_r,
+    ls_s, ls_r, lg_s, lg_r, ms_s, ms_r, in_sem, te_sem, tr_sem, out_sem,
+):
+    here = Place(n_f, n_t)
+    rows_all, model = n2.shape
+    ff = act.shape[1]
+    shard = e_sum.shape[1]
+    tiles = 4
+    ft = ff // tiles
+    here.greet_signal()
+
+    def e_load(i):
+        cols = pl.ds(i * ft, ft)
+        return pltpu.make_async_copy(full_e.at[:, cols], ev.at[:, cols], te_sem.at[i])
+
+    def r_load(i):
+        rows = pl.ds(i * ft, ft)
+        return pltpu.make_async_copy(full_r.at[rows], rv.at[rows], tr_sem.at[i])
+
+    loads = [
+        pltpu.make_async_copy(n2_i, n2, in_sem.at[0]),
+        pltpu.make_async_copy(cot, g, in_sem.at[1]),
+        pltpu.make_async_copy(mid_i, mid, in_sem.at[2]),
+    ]
+    loads[0].start()
+    e_load(0).start()
+    loads[1].start()
+    r_load(0).start()
+    for i in range(1, tiles):
+        e_load(i).start()
+        r_load(i).start()
+    loads[2].start()
+    alive = live[0].astype(F32)
+    loads[0].wait()
+    loads[1].wait()
+    sums[...] = jnp.zeros_like(sums)
+
+    def mask(i, total):
+        rows = pl.ds(al(i * 64, 64), 64)
+        value = g[rows, :].astype(F32) * alive
+        g[rows, :] = value.astype(BF)
+        return total + jnp.sum(value, axis=0, keepdims=True)
+
+    sums[0:1, :] = lax.fori_loop(0, rows_all // 64, mask, jnp.zeros((1, model), F32))
+
+    def hidden_tile(i):
+        cols = pl.ds(i * ft, ft)
+        e_load(i).wait()
+        h = dot(n2[...], ev[:, cols]) + par[7:8, cols]
+        r_load(i).wait()
+        ga = dot_nt(g[...], rv[cols, :])
+        bell = 0.5 * (1.0 + lax.erf(h * (1.0 / math.sqrt(2.0))))
+        act[:, cols] = (h * bell).astype(BF)
+        slope = bell + h * jnp.exp(-0.5 * h * h) * (1.0 / math.sqrt(2.0 * math.pi))
+        low = (ga * slope).astype(BF)
+        gh[:, cols] = low
+        sums[1:2, cols] = jnp.sum(low.astype(F32), axis=0, keepdims=True)
+
+    for i in range(tiles):
+        hidden_tile(i)
+    wide = model // 4
+
+    def back_tile(i, _):
+        cols = pl.ds(al(i * wide, wide), wide)
+        part[:, cols] = dot_nt(gh[...], ev[cols, :]).astype(BF)
+        return 0
+
+    lax.fori_loop(0, 4, back_tile, 0)
+    loads[2].wait()
+    here.greet_wait()
+    line = Line(here, part, rbuf, gb, (ls_s, ls_r, lg_s, lg_r), chunks, lag)
+    line2 = Line(here, part2, rbuf2, gb, (ms_s, ms_r, None, None), chunks, lag)
+    outs = Outs(out_sem)
+
+    def final(rows, span, total):
+        scaled, spread = norm_rows(mid[span, :])
+        grad = g[rows, :].astype(F32) + norm_back_rows(total, scaled, spread, par[3:4, :])
+        gm[span, :] = grad
+        gb[rows, :] = grad.astype(BF)
+        sums[4:5, :] += jnp.sum(total * scaled, axis=0, keepdims=True)
+        sums[5:6, :] += jnp.sum(total, axis=0, keepdims=True)
+
+    def final2(rows, span, total):
+        lo[span, :] = ((mid[span, :] + total + par[5:6, :]) * alive).astype(BF)
+
+    def e_stage(i):
+        return ev.at[pl.ds(al(i * shard, shard), shard)]
+
+    def r_stage(i):
+        return rv.at[:, pl.ds(al(i * shard, shard), shard)]
+
+    def cols_of(i):
+        return pl.ds(al(i * shard, shard), shard)
+
+    es = Scatter(here, e_sum, e_stage, e_half, e_full, e_s, e_r, 64)
+    rs = Scatter(here, r_sum, r_stage, None, None, r_s, r_r, 256)
+
+    def e_other(i):
+        value = dot_tn(n2[:, cols_of(es.shard(i, True))], gh[...])
+        ev[pl.ds(al(i * shard, shard), shard), :] = value.astype(BF)
+        es.cross(i).start()
+
+    def e_own(i):
+        value = dot_tn(n2[:, cols_of(es.shard(i, False))], gh[...])
+        es.cross(i).wait_recv()
+        es.combine(i, value)
+
+    def mlp(i):
+        part2[:, cols_of(i)] = dot(act[...], rv[:, cols_of(i)]).astype(BF)
+
+    def r_other(i):
+        value = dot_tn(act[...], g[:, cols_of(rs.shard(i, True))])
+        rv[:, cols_of(i)] = value.astype(BF)
+        rs.cross(i).start()
+
+    def r_own(i):
+        value = dot_tn(act[...], g[:, cols_of(rs.shard(i, False))])
+        rs.cross(i).wait_recv()
+        rs.combine(i, value)
+
+    n_s = 2 * n_f
+    a, b = n_f, 2 * n_f
+    d = b + n_s
+    ticks = max(line.ticks(), d + 2 * n_f, d + line2.sum_ticks())
+    gap = max(1, (ticks - b) // (n_f // 2 + 1))
+
+    def tick(tau, _):
+        line.tick(tau, final)
+        line2.tick(tau - d, final2, back=False)
+        span_when(tau, 0, a, e_other)
+        span_when(tau, a, b, e_own)
+        span_when(tau, b, d, mlp)
+        span_when(tau, d, d + n_f, r_other)
+        span_when(tau, d + n_f, d + 2 * n_f, r_own)
+
+        @pl.when(tau == a)
+        def _():
+            es.launch(here.m)
+
+        for s in range(here.m, 1, -1):
+
+            @pl.when(tau == b + gap * (here.m - s + 1) - 1)
+            def _(s=s):
+                es.absorb(s)
+                es.launch(s - 1)
+
+        return 0
+
+    lax.fori_loop(0, ticks, tick, 0)
+    outs.put(gb, gb_o)
+    outs.put(gm, gm_o)
+    outs.put(lo, lo_o)
+    outs.put(r_sum, pr_o)
+    outs.put(sums, sums_o)
+    es.absorb(1)
+    outs.put(e_sum.at[here.f], eg_o)
+    line.finish_sum()
+    line.finish_back()
+    line2.finish_sum()
+    es.finish()
+    for i in range(n_f):
+        rs.cross(i).wait_send()
+    outs.wait()
+
+
+def middle(n_f, n_t, live, n2, cot, mid, par, full_e, full_r, chunks=16, lag=3):
+    rows, model = n2.shape
+    ff = full_e.shape[1]
+    shard = model // (2 * n_f)
+    sds, dma, v = jax.ShapeDtypeStruct, pltpu.SemaphoreType.DMA, pltpu.VMEM
+    outs = (
+        sds((rows, model), BF),
+        sds((rows // 2, model), BF),
+        sds((rows // 2, model), F32),
+        sds((shard, ff), BF),
+        sds((n_f, ff, shard), BF),
+        sds((8, model), F32),
     )
-    inner = jnp.sum(grad_probs * probs, axis=-1, keepdims=True)
-    grad_scores = (probs * (grad_probs - inner)).astype(jnp.bfloat16)
-    grad_queries = (
-        jnp.einsum("hqk,khd->qhd", grad_scores, keys, preferred_element_type=jnp.float32) * scale
+    return pl.pallas_call(
+        functools.partial(middle_kernel, n_f, n_t, chunks, lag),
+        out_shape=outs,
+        in_specs=[pl.BlockSpec(memory_space=pltpu.SMEM), ANY, ANY, ANY, VM, ANY, ANY],
+        out_specs=(ANY,) * len(outs),
+        scratch_shapes=[
+            v((model, ff), BF), v((ff, model), BF), v((rows, model), BF), v((rows, model), BF),
+            v((rows, ff), BF), v((rows, ff), BF), v((rows, model), BF), v((rows, model), BF),
+            v((2, rows // 2, model), BF), v((2, rows // 2, model), BF), v((rows, model), BF),
+            v((rows // 2, model), F32), v((rows // 2, model), F32), v((rows // 2, model), BF),
+            v((8, model), F32),
+        ]
+        + Scatter.buffers(n_f, shard, ff)
+        + [v((n_f, ff, shard), BF)]
+        + Scatter.sems(n_f)
+        + Scatter.sems(n_f)
+        + Line.sems(chunks)
+        + Line.sems(chunks)[:2]
+        + [dma((3,)), dma((4,)), dma((4,)), dma((6,))],
+        compiler_params=pltpu.CompilerParams(
+            collective_id=1, has_side_effects=True, vmem_limit_bytes=63 << 20
+        ),
+        cost_estimate=pl.CostEstimate(
+            flops=26 * 10**9, bytes_accessed=40 * 10**6, transcendentals=4 * 10**6
+        ),
+        name="feed_forward",
+    )(live, n2, cot, mid, par, full_e, full_r)
+
+
+def backward_kernel(
+    n_f, n_t, chunks, lag, chunks2, lag2,
+    col, row, par, sums_i, tok, gm_i, lo_i, gb_i, ctx_i, q_i, kv_i, n1_i, full_a, full_o, pr_i,
+    lo_o, tg_o, rg_o, og_o, ag_o, small_o,
+    av, ov, gb, n1, tokh, gm, ctx, q, kv, gc, grads, near_g, far_g, got_g, lof, norm, part, rbuf,
+    sm, tp_small, sib_small, all_small,
+    r_sum, r_half, r_full, o_sum, o_half, o_full, a_sum, a_half, a_full,
+    r_s, r_r, o_s, o_r, a_s, a_r,
+    ls_s, ls_r, lg_s, lg_r, ms_s, ms_r, mg_s, mg_r,
+    kv_s, kv_r, tp_s, tp_r, sb_s, sb_r, pl_s, pl_r, in_sem, out_sem,
+):
+    here = Place(n_f, n_t)
+    rows_all, model = gb.shape
+    width = q.shape[1]
+    shard = a_sum.shape[1]
+    heads = width // HD
+    half = rows_all // 2
+    scale = 1.0 / math.sqrt(HD)
+    here.greet_signal()
+    mine = pl.ds(al(here.side * half, half), half)
+    pairs = [
+        (gb_i, gb), (full_o, ov), (pr_i, r_sum), (q_i, q), (kv_i, kv), (ctx_i, ctx),
+        (full_a, av), (n1_i, n1), (gm_i, gm), (tok.at[mine], tokh),
+    ]
+    loads = [pltpu.make_async_copy(s, d, in_sem.at[i]) for i, (s, d) in enumerate(pairs)]
+    for load in loads:
+        load.start()
+    end = (here.t == 0) | (here.t == n_t - 1)
+    lo_load = pltpu.make_async_copy(lo_i, lof.at[mine], in_sem.at[len(pairs)])
+    pl.when(end)(lo_load.start)
+    sm[...] = sums_i[...]
+    loads[0].wait()
+    loads[1].wait()
+    gc[...] = dot_nt(gb[...], ov[...]).astype(BF)
+    pl.when(end)(lo_load.wait)
+    loads[2].wait()
+    here.greet_wait()
+    outs = Outs(out_sem)
+    line = Line(here, part, rbuf, norm, (ls_s, ls_r, lg_s, lg_r), chunks, lag)
+    back = Line(here, lof, rbuf, lof, (ms_s, ms_r, mg_s, mg_r), chunks2, lag2)
+
+    @pl.when(end)
+    def _():
+        def send(j, _):
+            back.back_copy(j).start()
+            return 0
+
+        lax.fori_loop(0, chunks2, send, 0)
+
+    back_ticks = chunks2 + lag2 * (n_t - 1)
+
+    def back_tick(tau):
+        back.gather_step(0, tau, 0)
+        back.gather_step(1, tau, 0)
+
+    def cols_of(i):
+        return pl.ds(al(i * shard, shard), shard)
+
+    def rows_of(i):
+        return pl.ds(al(i * shard, shard), shard)
+
+    rs = Scatter(here, r_sum, None, r_half, r_full, r_s, r_r, 256)
+    os = Scatter(here, o_sum, lambda i: ov.at[:, cols_of(i)], o_half, o_full, o_s, o_r, 128)
+    sa = Scatter(here, a_sum, lambda i: av.at[rows_of(i)], a_half, a_full, a_s, a_r, 64)
+    rs.launch(here.m)
+    for load in loads[3:6]:
+        load.wait()
+
+    def head(h, _):
+        kc = pl.ds(al(h * HD, HD), HD)
+        vc = pl.ds(al(width + h * HD, HD), HD)
+        ids = col[...]
+        qh, gh = q[:, kc], gc[:, kc]
+        near = allowed_scores(qh, kv[0, :, kc], ids, row[0:1, :], scale)
+        far = allowed_scores(qh, kv[1, :, kc], ids, row[1:2, :], scale)
+        top = jnp.maximum(
+            jnp.max(near, axis=-1, keepdims=True), jnp.max(far, axis=-1, keepdims=True)
+        )
+        near = jnp.exp(near - top)
+        far = jnp.exp(far - top)
+        inv = 1.0 / (
+            jnp.sum(near, axis=-1, keepdims=True) + jnp.sum(far, axis=-1, keepdims=True)
+        )
+        near = near * inv
+        far = far * inv
+        near_gv = dot_tn(near.astype(BF), gh)
+        far_gv = dot_tn(far.astype(BF), gh)
+        gp_near = dot_nt(gh, kv[0, :, vc])
+        gp_far = dot_nt(gh, kv[1, :, vc])
+        inner = jnp.sum(gp_near * near, axis=-1, keepdims=True) + jnp.sum(
+            gp_far * far, axis=-1, keepdims=True
+        )
+        gs_near = (near * (gp_near - inner)).astype(BF)
+        gs_far = (far * (gp_far - inner)).astype(BF)
+        gq = (dot(gs_near, kv[0, :, kc]) + dot(gs_far, kv[1, :, kc])) * scale
+        grads[:, kc] = gq.astype(BF)
+        near_g[:, kc] = dot_tn(gs_near, qh) * scale
+        far_g[:, kc] = (dot_tn(gs_far, qh) * scale).astype(BF)
+        near_g[:, vc] = near_gv
+        far_g[:, vc] = far_gv.astype(BF)
+        back_tick(2 * h)
+        back_tick(2 * h + 1)
+
+        @pl.when(h == heads // 2)
+        def _():
+            rs.absorb(here.m)
+            rs.launch(here.m - 1)
+
+        return 0
+
+    lax.fori_loop(0, heads, head, 0)
+    swap = remote(far_g, got_g, kv_s.at[0], kv_r.at[0], here.sib)
+    swap.start()
+    for s in range(here.m - 1, 1, -1):
+        rs.absorb(s)
+        rs.launch(s - 1)
+
+    def out_task(i, _):
+        value = dot_tn(ctx[...], gb[:, cols_of(os.shard(i, True))])
+        ov[:, cols_of(i)] = value.astype(BF)
+        os.cross(i).start()
+        back_tick(2 * heads + i)
+        return 0
+
+    lax.fori_loop(0, n_f, out_task, 0)
+
+    def out_own(i, _):
+        value = dot_tn(ctx[...], gb[:, cols_of(os.shard(i, False))])
+        os.cross(i).wait_recv()
+        os.combine(i, value)
+        back_tick(2 * heads + n_f + i)
+        return 0
+
+    lax.fori_loop(0, n_f, out_own, 0)
+    os.launch(here.m)
+    swap.wait_recv()
+
+    def add_rows(i, total):
+        rows = pl.ds(al(i * 128, 128), 128)
+        low = (near_g[rows, :] + got_g[rows, :].astype(F32)).astype(BF)
+        grads[rows, width:] = low
+        both = jnp.concatenate([grads[rows, 0:width], low[:, width:]], axis=1).astype(F32)
+        return total + jnp.sum(both, axis=0, keepdims=True)
+
+    sm[3:4, 0 : 2 * width] = lax.fori_loop(
+        0, rows_all // 128, add_rows, jnp.zeros((1, 2 * width), F32)
     )
-    grad_keys = (
-        jnp.einsum("hqk,qhd->khd", grad_scores, queries, preferred_element_type=jnp.float32) * scale
+    loads[6].wait()
+    wide = model // 4
+
+    def back_part(i, _):
+        cols = pl.ds(al(i * wide, wide), wide)
+        part[:, cols] = dot_nt(grads[...], av[cols, :]).astype(BF)
+        return 0
+
+    lax.fori_loop(0, 4, back_part, 0)
+    for load in loads[7:]:
+        load.wait()
+
+    def final(rows, span, total):
+        scaled, spread = norm_rows(tokh[span, :].astype(F32))
+        grad = gm[span, :] + norm_back_rows(total, scaled, spread, par[0:1, :])
+        norm[rows, :] = grad.astype(BF)
+        sm[6:7, :] += jnp.sum(total * scaled, axis=0, keepdims=True)
+        sm[7:8, :] += jnp.sum(total, axis=0, keepdims=True)
+
+    def a_other(i):
+        value = dot_tn(n1[:, cols_of(sa.shard(i, True))], grads[...])
+        av[rows_of(i), :] = value.astype(BF)
+        sa.cross(i).start()
+
+    def a_own(i):
+        value = dot_tn(n1[:, cols_of(sa.shard(i, False))], grads[...])
+        sa.cross(i).wait_recv()
+        sa.combine(i, value)
+
+    def branch_sum(i):
+        rows = pl.ds(al(i * 64, 64), 64)
+        sm[2:3, :] += jnp.sum(gb[rows, :].astype(F32), axis=0, keepdims=True)
+
+    sm[2:3, :] = jnp.zeros((1, model), F32)
+    blocks = rows_all // 64
+    d = 2 * n_f
+    ticks = max(line.ticks(), d + blocks)
+    plan = [(d, lambda: rs.absorb(1))]
+    room = ticks - d
+    for s in range(here.m, 1, -1):
+        k = here.m - s
+        spots = here.m - 1
+        plan.append((d + 2 + (room * k) // (2 * spots), functools.partial(ring_step, os, s)))
+        plan.append((d + room // 4 + (room * k) // (2 * spots), functools.partial(ring_step, sa, s)))
+
+    def tick(tau, _):
+        line.tick(tau, final)
+        span_when(tau, 0, n_f, a_other)
+        span_when(tau, n_f, d, a_own)
+        span_when(tau, d, d + blocks, branch_sum)
+        pl.when(tau == n_f)(lambda: sa.launch(here.m))
+        for at, event in plan:
+            pl.when(tau == at)(event)
+        return 0
+
+    lax.fori_loop(0, ticks, tick, 0)
+    outs.put(norm, tg_o)
+    outs.put(r_sum.at[here.f], rg_o)
+
+    def rest(tau, _):
+        back_tick(tau)
+        return 0
+
+    lax.fori_loop(min(2 * heads + 2 * n_f, back_ticks), back_ticks, rest, 0)
+    outs.put(lof, lo_o)
+
+    def tp_copy(k):
+        spot = tp_small.at[here.side]
+        return remote(sm, spot, tp_s.at[k - 1], tp_r.at[here.side], here.tp(k))
+
+    @pl.when(end)
+    def _():
+        for k in range(1, n_t):
+            tp_copy(k).start()
+
+    def tp_landing(side):
+        spot = tp_small.at[side]
+        return remote(sm, spot, tp_s.at[0], tp_r.at[side], here.tp(1))
+
+    @pl.when(here.t != 0)
+    def _():
+        tp_landing(0).wait_recv()
+
+    @pl.when(here.t != n_t - 1)
+    def _():
+        tp_landing(1).wait_recv()
+
+    @pl.when(end)
+    def _():
+        tp_small[here.side] = sm[...]
+
+    top_rows = lax.broadcasted_iota(jnp.int32, (8, model), 0) < 4
+    all_small[here.f] = jnp.where(top_rows, sm[...], tp_small[0] + tp_small[1])
+    to_sib = remote(all_small.at[here.f], sib_small, sb_s.at[0], sb_r.at[0], here.sib)
+    to_sib.start()
+    to_sib.wait()
+    all_small[here.f] += sib_small[...]
+
+    def plane_copy(k):
+        spot = all_small.at[here.f]
+        return remote(spot, spot, pl_s.at[k], pl_r.at[k], here.plane(k))
+
+    def plane_landing(k):
+        spot = all_small.at[lax.rem(here.f + n_f - k, n_f)]
+        return remote(spot, spot, pl_s.at[k], pl_r.at[k], here.plane(k))
+
+    for k in range(1, n_f):
+        plane_copy(k).start()
+    os.absorb(1)
+    outs.put(o_sum.at[here.f], og_o)
+    sa.absorb(1)
+    outs.put(a_sum.at[here.f], ag_o)
+    for k in range(1, n_f):
+        plane_landing(k).wait_recv()
+    total = all_small[0]
+    for k in range(1, n_f):
+        total = total + all_small[k]
+    sib_small[...] = total
+    outs.put(sib_small, small_o)
+    line.finish_sum()
+    line.finish_back()
+    back.finish_back()
+    rs.finish(False)
+    os.finish()
+    sa.finish()
+    swap.wait_send()
+
+    @pl.when(end)
+    def _():
+        for k in range(1, n_t):
+            tp_copy(k).wait_send()
+
+    for k in range(1, n_f):
+        plane_copy(k).wait_send()
+    outs.wait()
+
+
+def ring_step(scatter, s):
+    scatter.absorb(s)
+    scatter.launch(s - 1)
+
+
+def backward(
+    n_f, n_t, col, row, par, sums, tok, gm, lo, gb, ctx, q, kv, n1, full_a, full_o, pr,
+    chunks=16, lag=3, chunks2=8, lag2=2,
+):
+    rows, model = gb.shape
+    width, ff = q.shape[1], pr.shape[1]
+    shard = model // (2 * n_f)
+    sds, dma, v = jax.ShapeDtypeStruct, pltpu.SemaphoreType.DMA, pltpu.VMEM
+    outs = (
+        sds((rows, model), BF),
+        sds((rows, model), BF),
+        sds((ff, shard), BF),
+        sds((width, shard), BF),
+        sds((shard, 3 * width), BF),
+        sds((8, model), F32),
     )
-    grad_values = jnp.einsum(
-        "hqk,qhd->khd", probs.astype(jnp.bfloat16), grad_context, preferred_element_type=jnp.float32
-    )
-    return (grad_queries, grad_keys, grad_values)
-
-
-def shifted(block, axis, distance):
-    devices = range(lax.axis_size(axis))
-    route = [((i - distance) % len(devices), i) for i in devices]
-    return lax.ppermute(block, axis, route)
+    return pl.pallas_call(
+        functools.partial(backward_kernel, n_f, n_t, chunks, lag, chunks2, lag2),
+        out_shape=outs,
+        in_specs=[VM] * 4 + [ANY] * 11,
+        out_specs=(ANY,) * len(outs),
+        scratch_shapes=[
+            v((model, 3 * width), BF), v((width, model), BF), v((rows, model), BF),
+            v((rows, model), BF), v((rows // 2, model), BF), v((rows // 2, model), F32),
+            v((rows, width), BF), v((rows, width), BF), v((2, rows, 2 * width), BF),
+            v((rows, width), BF), v((rows, 3 * width), BF), v((rows, 2 * width), F32),
+            v((rows, 2 * width), BF), v((rows, 2 * width), BF), v((rows, model), BF),
+            v((rows, model), BF), v((rows, model), BF), v((2, rows // 2, model), BF),
+            v((8, model), F32), v((2, 8, model), F32), v((8, model), F32),
+            v((n_f, 8, model), F32),
+        ]
+        + Scatter.buffers(n_f, ff, shard)
+        + Scatter.buffers(n_f, width, shard)
+        + Scatter.buffers(n_f, shard, 3 * width)
+        + Scatter.sems(n_f) * 3
+        + Line.sems(chunks)
+        + Line.sems(chunks2)
+        + [dma((1,)), dma((1,)), dma((n_t - 1,)), dma((2,)), dma((1,)), dma((1,))]
+        + [dma((n_f,)), dma((n_f,)), dma((11,)), dma((6,))],
+        compiler_params=pltpu.CompilerParams(
+            collective_id=2, has_side_effects=True, vmem_limit_bytes=63 << 20
+        ),
+        cost_estimate=pl.CostEstimate(
+            flops=14 * 10**9, bytes_accessed=40 * 10**6, transcendentals=4 * 10**6
+        ),
+        name="attention_backward",
+    )(col, row, par, sums, tok, gm, lo, gb, ctx, q, kv, n1, full_a, full_o, pr)
 
 
 def spread_out(piece, index, count):
@@ -618,8 +1233,6 @@
     index = 2 * lax.axis_index("fsdp") + c
     width, ff = query_weight.shape[1], expand_weight.shape[1]
     shard = query_weight.shape[0]
-    heads = width // HD
-    scale = 1.0 / math.sqrt(HD)
     vectors = jnp.stack(
         [first_gain, first_shift, output_bias, second_gain, second_shift, reduce_bias]
     ).astype(F32)
@@ -637,83 +1250,42 @@
     col = near.reshape(rows, 1)
     wa = jnp.concatenate([query_weight, key_weight, value_weight], axis=1)
     tok = tokens.reshape(rows, model)
-    n1, q, kv, context_low, n2, mid, par, full_a, full_o, full_e, full_r = forward(
+    n1, q, kv, ctx, n2, mid, par, full_a, full_o, full_e, full_r = forward(
         n_f, n_t, tok, col, row, small, wa, output_weight, expand_weight, reduce_weight
     )
-    mids = lax.all_gather(mid, "tp")
-    middle = jnp.concatenate([mids[0], mids[n_t - 1]])
-    inputs = tok.astype(F32)
-    scaled_one, spread_one = norm_rows(inputs)
-    scaled_two, spread_two = norm_rows(middle)
-    flat_r = full_r.transpose(1, 0, 2).reshape(ff, model)
-    flat_o = full_o.transpose(1, 0, 2).reshape(width, model)
-    row_live = live_count[0].astype(F32)
-    hidden = dot(n2, full_e) + par[7:8, :ff]
-    active, gelu_pull = jax.vjp(gelu_exact, hidden)
-    active_low = active.astype(BF)
-    mlp_term = dot(active_low, flat_r)
-    layer_out = ((middle + lax.psum(mlp_term, "tp") + par[5:6]) * row_live).astype(BF)
-    grad_out = cotangent.astype(F32).reshape(rows, model) * row_live
-    grad_low = grad_out.astype(BF)
-    reduce_bias_grad = jnp.sum(grad_out, axis=0)
-    reduce_weight_grad = dot_tn(active_low, grad_low)
-    grad_hidden = gelu_pull(dot_nt(grad_low, flat_r))[0].astype(BF)
-    expand_bias_grad = jnp.sum(grad_hidden.astype(F32), axis=0)
-    expand_weight_grad = dot_tn(n2, grad_hidden)
-    grad_normed_two = lax.psum(dot_nt(grad_hidden, full_e), "tp")
-    norm_part_two, second_gain_grad, second_shift_grad = norm_back(
-        grad_normed_two, scaled_two, spread_two, par[3:4]
+    gb, lo, gm, e_grad, r_part, sums = middle(
+        n_f, n_t, live_count, n2, cotangent.reshape(rows, model), mid, par, full_e, full_r
     )
-    grad_middle = grad_out + norm_part_two
-    grad_branch = grad_middle.astype(BF)
-    output_bias_grad = jnp.sum(grad_branch.astype(F32), axis=0)
-    output_weight_grad = dot_tn(context_low, grad_branch)
-    grad_context = dot_nt(grad_branch, flat_o).astype(BF)
-    hs = (rows, heads, HD)
-    keys = kv[:, :, :width].reshape(2 * rows, heads, HD)
-    values = kv[:, :, width:].reshape(2 * rows, heads, HD)
-    gq, gk, gv = attend_backward(
-        q.reshape(hs), keys, values, near[0], row.reshape(-1), grad_context.reshape(hs), scale
+    layer_out, tokens_grad, r_grad, o_grad, a_grad, total = backward(
+        n_f, n_t, col, row, par, sums, tok, gm, lo, gb, ctx, q, kv, n1, full_a, full_o, r_part
     )
-    gk, gv = gk.reshape(2 * rows, width), gv.reshape(2 * rows, width)
-    back_k = shifted(gk[rows:].astype(BF), "ctx", 1).astype(F32)
-    back_v = shifted(gv[rows:].astype(BF), "ctx", 1).astype(F32)
-    grads = jnp.concatenate(
-        [gq.reshape(rows, width), gk[:rows] + back_k, gv[:rows] + back_v], axis=1
-    ).astype(BF)
-    sums = jnp.sum(grads.astype(F32), axis=0)
-    query_bias_grad, value_bias_grad = sums[:width], sums[2 * width :]
-    wa_grad = dot_tn(n1, grads)
-    grad_normed_one = lax.psum(dot_nt(grads, full_a), "tp")
-    norm_part_one, first_gain_grad, first_shift_grad = norm_back(
-        grad_normed_one, scaled_one, spread_one, par[0:1]
-    )
-    tokens_grad = (grad_middle + norm_part_one).astype(BF)
-    both = ("fsdp", "ctx")
-
-    def scatter(value, dim):
-        low = value.astype(BF)
-        return lax.psum_scatter(low, both, scatter_dimension=dim, tiled=True).astype(F32)
-
-    wa_mine = scatter(wa_grad, 0)
+
+    def vector(k):
+        return lax.dynamic_slice_in_dim(total[k], index * shard, shard)
+
+    def across(flat, like):
+        whole = flat.reshape(like.shape[0], -1)
+        return lax.dynamic_slice_in_dim(whole, index * like.shape[1], like.shape[1], 1)
+
+    a_grad = a_grad.astype(F32)
     return (
         layer_out.reshape(1, rows, model),
         tokens_grad.reshape(1, rows, model),
-        scatter(first_gain_grad, 0),
-        scatter(first_shift_grad, 0),
-        wa_mine[:, :width],
-        scatter(query_bias_grad.reshape(heads, HD), 1),
-        wa_mine[:, width : 2 * width],
-        wa_mine[:, 2 * width :],
-        scatter(value_bias_grad.reshape(heads, HD), 1),
-        scatter(output_weight_grad, 1),
-        scatter(output_bias_grad, 0),
-        scatter(second_gain_grad, 0),
-        scatter(second_shift_grad, 0),
-        scatter(expand_weight_grad, 0),
-        scatter(expand_bias_grad.reshape(expand_bias.shape[0], -1), 1),
-        scatter(reduce_weight_grad, 1),
-        scatter(reduce_bias_grad, 0),
+        vector(6),
+        vector(7),
+        a_grad[:, :width],
+        across(total[3, :width], query_bias),
+        a_grad[:, width : 2 * width],
+        a_grad[:, 2 * width :],
+        across(total[3, width : 2 * width], value_bias),
+        o_grad.astype(F32),
+        vector(2),
+        vector(4),
+        vector(5),
+        e_grad.astype(F32),
+        across(total[1, :ff], expand_bias),
+        r_grad.astype(F32),
+        vector(0),
     )
 
 

time: 844 us -> 386 us (0.46)
  waiting for transfers between devices: 490 us -> 0 us
  Pallas kernels: 128 us -> 357 us
  matrix products: 86.4 us -> 0 us
  other arithmetic: 46 us -> 11.3 us
  local copies, waits for them, and re-layouts: 41.5 us -> 15.8 us
  blocking collectives: 23.8 us -> 0 us
  between operations: 17.6 us -> 1.4 us
    psum x2 -> x0, waiting for transfers between devices: 354 us -> none  [the longest x1 202 us: local(): lax.psum(mlp_term, 'tp')]
    pallas_call x0 -> x2, Pallas kernels: none -> 229 us  [the longest x1 118 us: backward(): pl.pallas_call(functools.partial(backward_kernel, n_f, n_t, chunks, lag,...]
    dot_general x14 -> x0, matrix products: 79 us -> none  [the longest x4 31.4 us: dot_tn(): lax.dot_general(left, right, (((0,), (0,)), ((), ())), preferred_element_...]
    all_gather x1 -> x0, waiting for transfers between devices: 74.9 us -> none  [local(): mids = lax.all_gather(mid, 'tp')]
    reduce_scatter x4 -> x0, waiting for transfers between devices: 43.6 us -> none  [scatter(): lax.psum_scatter(low, both, scatter_dimension=dim, tiled=True).astype(F32)]
    unnamed x1 -> x0, blocking collectives: 23.8 us -> none
    unnamed x13 -> x0, waiting for transfers between devices: 18 us -> none
    reduce_sum x9 -> x0, other arithmetic: 16.4 us -> none  [the longest x2 7.94 us: norm_back(): jnp.sum(grad_normed * scaled, axis=0)]
  transfers between devices with their start and end apart: 12 -> 0, of which waited for: 5 -> 0; matrix products, arithmetic and copies ran while one was open for 18% -> 0% of each run, Pallas kernels for 0% -> 0%
where the time goes in v2:
time: 386 us; the launch traced here: 385 us
  Pallas kernels  357 us (92%)
  local copies, waits for them, and re-layouts  15.8 us (4%)
  other arithmetic  11.3 us (3%)
    pallas_call x1, Pallas kernels, forward(): pl.pallas_call(functools.partial(forward_kernel, n_f, n_t, chunks, lag),...  128 us
    pallas_call x1, Pallas kernels, backward(): pl.pallas_call(functools.partial(backward_kernel, n_f, n_t, chunks, lag,...  118 us
    pallas_call x1, Pallas kernels, middle(): pl.pallas_call(functools.partial(middle_kernel, n_f, n_t, chunks, lag), o...  111 us

profile of v2, /device:TPU:0, one launch (start us, length us, event | category | flops | bytes accessed | tf_op | source)
XLA Modules:
  0.0 385.1 jit_solution(5402022693821161365)
XLA Ops:
  0.7 0.5 broadcast.30
  1.2 1.3 reduce.7
  2.6 0.6 pad_add_fusion.row
  3.2 0.9 copy.37.col
  4.1 0.7 stack.21
  4.8 0.7 stack.22
  5.4 0.7 stack.23
  6.1 0.7 stack.24
  6.7 0.7 stack.25
  7.4 0.7 stack.26
  8.1 0.7 maximum_convert_fusion
  8.9 0.1 mul.90
  9.0 0.7 convert_element_type.43
  9.9 0.7 fusion.small
  10.5 2.0 pad_maximum_fusion.wa
  12.5 127.6 %attention_forward.1 = (bf16[512,2048]{1,0:T(8,128)(2,1)}, bf16[512,512]{1,0:T(8,128)(2,1)}, bf16[2,512,1024]{2,1,0:T(8,128)(2,1)}, bf16[512,512]{1,0:T(8,128)(2...) custom-call(bf16[512,2048]{1,0:T(8,128)(2,1)} %bitcast.33, ...), custom_call_target="tpu_custom_call" | custom-call | flops 8000000000 | bytes 60000000 | tf_op jit(solution)/shard_map/attention_forward/pallas_call | solution.py:540
  140.8 111.3 %feed_forward.1 = (bf16[512,2048]{1,0:T(8,128)(2,1)}, bf16[256,2048]{1,0:T(8,128)(2,1)}, f32[256,2048]{1,0:T(8,128)}, bf16[256,2048]{1,0:T(8,128)(2,1)}, bf16[4,...) custom-call(s32[1]{0:T(128)S(6)} %copy.42.live, bf16[512,2048]{1,0:T(8,128)(2,1)} %get-tuple-element.41.n2_i, ...), custom_call_target="tpu_custom_call" | custom-call | flops 25999998976 | bytes 40000000 | tf_op jit(solution)/shard_map/feed_forward/pallas_call | solution.py:852
  252.1 117.8 %attention_backward.1 = (bf16[512,2048]{1,0:T(8,128)(2,1)}, bf16[512,2048]{1,0:T(8,128)(2,1)}, bf16[2048,256]{1,0:T(8,128)(2,1)}, bf16[512,256]{1,0:T(8,128)(2,1...) custom-call(s32[512,1]{1,0:T(8,128)} %copy.37.col, s32[2,512]{1,0:T(2,128)} %pad_add_fusion.row, ...), custom_call_target="tpu_custom_call" | custom-call | flops 14000000000 | bytes 40000000 | tf_op jit(solution)/shard_map/attention_backward/pallas_call | solution.py:1186
  369.9 1.5 fusion.3
  371.4 0.6 constant_dynamic-slice_fusion
  372.0 0.6 constant_dynamic-slice_fusion.3
  372.5 0.7 fusion.4
  373.3 0.7 constant_dynamic-slice_fusion.5
  373.9 0.6 constant_dynamic-slice_fusion.7
  374.5 2.7 convert_element_type.47
  377.2 1.2 fusion.2
  378.4 0.8 convert_element_type.45
  379.3 0.6 constant_dynamic-slice_fusion.1
  379.9 1.6 convert_element_type.46
  381.5 1.3 copy.43
  382.8 1.0 copy-done.1
  383.8 1.3 copy.44
  (23 shorter events, 0.4 us)
Async XLA Ops:
  369.9 7.3 %copy-start = (bf16[256,1536]{1,0:T(8,128)(2,1)S(1)}, bf16[256,1536]{1,0:T(8,128)(2,1)}, u32[]{:S(2)}) copy-start(bf16[256,1536]{1,0:T(8,128)(2,1)} %get-tuple-element.59) | copy-start | bytes 2359300
  377.2 1.2 copy-start.4
  377.2 2.7 copy-start.3
  378.4 3.1 copy-start.2
  381.5 2.3 copy-start.1

commit v3 on v2

--- a/solution.py
+++ b/solution.py
@@ -12,6 +12,7 @@
 NEG = -1e30
 MESH = pl.DeviceIdType.MESH
 ANY = pl.BlockSpec(memory_space=pl.ANY)
+HBM = pl.BlockSpec(memory_space=pltpu.HBM)
 VM = pl.BlockSpec(memory_space=pltpu.VMEM)
 BF = jnp.bfloat16
 F32 = jnp.float32
@@ -346,22 +347,44 @@
     return own
 
 
+def place_ids(ids, col, row, here):
+    rows = col.shape[0]
+    row[0:1, :] = ids[:, pl.ds(al(here.c * rows, rows), rows)].astype(F32)
+    row[1:2, :] = ids[:, pl.ds(al((1 - here.c) * rows, rows), rows)].astype(F32)
+    step = 128
+
+    def turn(i, _):
+        start = al(i * step, step)
+        down = lax.broadcasted_iota(jnp.int32, (step, rows), 0) + start
+        along = lax.broadcasted_iota(jnp.int32, (step, rows), 1)
+        kept = jnp.where(down == along, row[0:1, :], 0.0)
+        col[pl.ds(start, step), :] = jnp.sum(kept, axis=1, keepdims=True)
+        return 0
+
+    lax.fori_loop(0, rows // step, turn, 0)
+
+
+def picker(index, piece, count):
+    down = lax.broadcasted_iota(jnp.int32, (piece, piece * count), 0) + index * piece
+    return jnp.where(down == lax.broadcasted_iota(jnp.int32, (piece, piece * count), 1), 1.0, 0.0)
+
+
 def allowed_scores(q, k, col, row, scale):
     return jnp.where(row <= col, dot_nt(q, k) * scale, NEG)
 
 
 def forward_kernel(
     n_f, n_t, chunks, lag,
-    tok, col, row, small, wa, wo, we, wr,
+    tok, ids, g1, s1, b_o, g2, s2, b_r, b_q, b_v, b_e, wq, wk, wv, wo, we, wr,
     n1_o, q_o, kv_o, ctx_o, n2_o, mid_o, par_o, a_o, o_o, e_o, r_o,
     tokv, n1, full_a, full_o, stage_e, stage_r, q, kv, ctx, part, rbuf, norm, mid,
-    sib_small, all_small, par,
+    col, row, small, sib_small, all_small, par,
     ga_s, ga_r, go_s, go_r, ge_s, ge_r, gr_s, gr_r,
     ls_s, ls_r, lg_s, lg_r, sm_s, sm_r, kv_s, kv_r, in_sem, out_sem,
 ):
     here = Place(n_f, n_t)
     width = wo.shape[0]
-    shard = wa.shape[0]
+    shard = wq.shape[0]
     rows_all, model = n1.shape
     heads = width // HD
     scale = 1.0 / math.sqrt(HD)
@@ -372,14 +395,32 @@
     e_slot, r_slot = row_slots(e_o, shard), column_slots(r_o, shard)
     loads = [
         pltpu.make_async_copy(wo, o_slot(me, None), in_sem.at[1]),
-        pltpu.make_async_copy(wa, a_slot(me, None), in_sem.at[2]),
-        pltpu.make_async_copy(we, stage_e, in_sem.at[3]),
-        pltpu.make_async_copy(wr, stage_r, in_sem.at[4]),
+        pltpu.make_async_copy(we, stage_e, in_sem.at[2]),
+        pltpu.make_async_copy(wr, stage_r, in_sem.at[3]),
     ]
-    for load in loads:
+    mine = pl.ds(al(me * shard, shard), shard)
+    for k, w in enumerate((wq, wk, wv)):
+        spot = full_a.at[mine, pl.ds(k * width, width)]
+        loads.append(pltpu.make_async_copy(w, spot, in_sem.at[4 + k]))
+    for load in loads[3:] + loads[:3]:
         load.start()
-    here.greet()
-    ga = Gather(here, own_part(wa), a_slot, ga_s, ga_r)
+    here.greet_signal()
+    small[...] = jnp.zeros_like(small)
+    for k, vector in enumerate((g1, s1, b_o, g2, s2, b_r)):
+        small[k : k + 1, mine] = vector[...].astype(F32).reshape(1, shard)
+
+    def put_bias(bias, line, base):
+        count, piece = bias.shape
+        wide = dot(bias[...].astype(F32), picker(me, piece, 2 * n_f))
+        size = piece * 2 * n_f
+        for h in range(count):
+            small[line : line + 1, base + h * size : base + (h + 1) * size] = wide[h : h + 1, :]
+
+    put_bias(b_q, 6, 0)
+    put_bias(b_v, 6, width)
+    put_bias(b_e, 7, 0)
+    here.greet_wait()
+    ga = Gather(here, lambda part: a_slot(me, part), a_slot, ga_s, ga_r)
     go = Gather(here, own_part(wo), o_slot, go_s, go_r)
     ge = Gather(here, own_part(we), e_slot, ge_s, ge_r)
     gr = Gather(here, own_part(wr), r_slot, gr_s, gr_r)
@@ -400,8 +441,10 @@
 
     for k in range(1, n_f):
         small_copy(k).start()
+    for load in loads[3:]:
+        load.wait()
     ga.start()
-    for load in loads[2:]:
+    for load in loads[1:3]:
         load.wait()
     outs.put(stage_e, e_slot(me, None))
     outs.put(stage_r, r_slot(me, None))
@@ -424,14 +467,14 @@
 
     lax.fori_loop(0, rows_all // 64, norm_one, 0)
     outs.put(n1, n1_o)
+    place_ids(ids, col, row, here)
     for s in range(1, here.m):
         ga.step(s)
     gr.start()
     ge.start()
     go.step(here.m)
     ga.step(here.m)
-    for load in loads[:2]:
-        load.wait()
+    loads[0].wait()
     ga.arrive()
     q[...] = (dot(n1[...], full_a[:, 0:width]) + par[6:7, 0:width]).astype(BF)
     kv[0, :, 0:width] = dot(n1[...], full_a[:, width : 2 * width]).astype(BF)
@@ -518,9 +561,9 @@
     outs.wait()
 
 
-def forward(n_f, n_t, tok, col, row, small, wa, wo, we, wr, chunks=16, lag=3):
+def forward(n_f, n_t, tok, ids, vectors, biases, wq, wk, wv, wo, we, wr, chunks=16, lag=3):
     rows, model = tok.shape
-    shard, width, ff = wa.shape[0], wo.shape[0], we.shape[1]
+    shard, width, ff = wq.shape[0], wo.shape[0], we.shape[1]
     sds = jax.ShapeDtypeStruct
     dma = pltpu.SemaphoreType.DMA
     outs = (
@@ -540,19 +583,19 @@
     return pl.pallas_call(
         functools.partial(forward_kernel, n_f, n_t, chunks, lag),
         out_shape=outs,
-        in_specs=[ANY, VM, VM, VM, ANY, ANY, ANY, ANY],
+        in_specs=[ANY] + [VM] * 10 + [ANY] * 6,
         out_specs=(ANY,) * len(outs),
         scratch_shapes=[
             v((rows, model), BF), v((rows, model), BF), v((model, 3 * width), BF),
             v((width, model), BF), v((shard, ff), BF), v((ff, shard), BF),
             v((rows, width), BF), v((2, rows, 2 * width), BF), v((rows, width), BF),
             v((rows, model), BF), v((2, rows // 2, model), BF), v((rows, model), BF),
-            v((rows // 2, model), F32), v((8, model), F32), v((n_f, 8, model), F32),
-            v((8, model), F32),
+            v((rows // 2, model), F32), v((rows, 1), F32), v((2, rows), F32), v((8, model), F32),
+            v((8, model), F32), v((n_f, 8, model), F32), v((8, model), F32),
         ]
         + [dma((Gather.sems(n_f),))] * 8
         + Line.sems(chunks)
-        + [dma((n_f,)), dma((n_f,)), dma((1,)), dma((1,)), dma((5,)), dma((16,))],
+        + [dma((n_f,)), dma((n_f,)), dma((1,)), dma((1,)), dma((7,)), dma((16,))],
         compiler_params=pltpu.CompilerParams(
             collective_id=0, has_side_effects=True, vmem_limit_bytes=60 << 20
         ),
@@ -560,7 +603,7 @@
             flops=8 * 10**9, bytes_accessed=60 * 10**6, transcendentals=10**6
         ),
         name="attention_forward",
-    )(tok, col, row, small, wa, wo, we, wr)
+    )(tok, ids, *vectors, *biases, wq, wk, wv, wo, we, wr)
 
 
 class Scatter:
@@ -625,6 +668,20 @@
                 return 0
 
             lax.fori_loop(0, count, body, 0)
+
+    def last(self):
+        self.hop(0, 1).wait_recv()
+        self.hop(1, 1).wait_recv()
+        f = self.here.owner(0)
+
+        def body(i, _):
+            rows = pl.ds(al(i * self.block, self.block), self.block)
+            total = self.sums[f, rows, :].astype(F32) + self.ring_full[0, 0, rows, :].astype(F32)
+            total = total + self.ring_full[1, 0, rows, :].astype(F32)
+            self.sums[f, rows, :] = total.astype(BF)
+            return 0
+
+        lax.fori_loop(0, self.size // self.block, body, 0)
 
     def finish(self, crossed=True):
         for s in range(1, self.m + 1):
@@ -825,7 +882,7 @@
     outs.put(lo, lo_o)
     outs.put(r_sum, pr_o)
     outs.put(sums, sums_o)
-    es.absorb(1)
+    es.last()
     outs.put(e_sum.at[here.f], eg_o)
     line.finish_sum()
     line.finish_back()
@@ -880,10 +937,10 @@
 
 def backward_kernel(
     n_f, n_t, chunks, lag, chunks2, lag2,
-    col, row, par, sums_i, tok, gm_i, lo_i, gb_i, ctx_i, q_i, kv_i, n1_i, full_a, full_o, pr_i,
+    ids, par, sums_i, tok, gm_i, lo_i, gb_i, ctx_i, q_i, kv_i, n1_i, full_a, full_o, pr_i,
     lo_o, tg_o, rg_o, og_o, ag_o, small_o,
     av, ov, gb, n1, tokh, gm, ctx, q, kv, gc, grads, near_g, far_g, got_g, lof, norm, part, rbuf,
-    sm, tp_small, sib_small, all_small,
+    col, row, sm, tp_small, sib_small, all_small,
     r_sum, r_half, r_full, o_sum, o_half, o_full, a_sum, a_half, a_full,
     r_s, r_r, o_s, o_r, a_s, a_r,
     ls_s, ls_r, lg_s, lg_r, ms_s, ms_r, mg_s, mg_r,
@@ -909,6 +966,7 @@
     lo_load = pltpu.make_async_copy(lo_i, lof.at[mine], in_sem.at[len(pairs)])
     pl.when(end)(lo_load.start)
     sm[...] = sums_i[...]
+    place_ids(ids, col, row, here)
     loads[0].wait()
     loads[1].wait()
     gc[...] = dot_nt(gb[...], ov[...]).astype(BF)
@@ -1062,7 +1120,7 @@
     blocks = rows_all // 64
     d = 2 * n_f
     ticks = max(line.ticks(), d + blocks)
-    plan = [(d, lambda: rs.absorb(1))]
+    plan = [(d, rs.last)]
     room = ticks - d
     for s in range(here.m, 1, -1):
         k = here.m - s
@@ -1133,9 +1191,9 @@
 
     for k in range(1, n_f):
         plane_copy(k).start()
-    os.absorb(1)
+    os.last()
     outs.put(o_sum.at[here.f], og_o)
-    sa.absorb(1)
+    sa.last()
     outs.put(a_sum.at[here.f], ag_o)
     for k in range(1, n_f):
         plane_landing(k).wait_recv()
@@ -1168,7 +1226,7 @@
 
 
 def backward(
-    n_f, n_t, col, row, par, sums, tok, gm, lo, gb, ctx, q, kv, n1, full_a, full_o, pr,
+    n_f, n_t, ids, par, sums, tok, gm, lo, gb, ctx, q, kv, n1, full_a, full_o, pr,
     chunks=16, lag=3, chunks2=8, lag2=2,
 ):
     rows, model = gb.shape
@@ -1186,7 +1244,7 @@
     return pl.pallas_call(
         functools.partial(backward_kernel, n_f, n_t, chunks, lag, chunks2, lag2),
         out_shape=outs,
-        in_specs=[VM] * 4 + [ANY] * 11,
+        in_specs=[VM] * 3 + [ANY] * 11,
         out_specs=(ANY,) * len(outs),
         scratch_shapes=[
             v((model, 3 * width), BF), v((width, model), BF), v((rows, model), BF),
@@ -1195,6 +1253,7 @@
             v((rows, width), BF), v((rows, 3 * width), BF), v((rows, 2 * width), F32),
             v((rows, 2 * width), BF), v((rows, 2 * width), BF), v((rows, model), BF),
             v((rows, model), BF), v((rows, model), BF), v((2, rows // 2, model), BF),
+            v((rows, 1), F32), v((2, rows), F32),
             v((8, model), F32), v((2, 8, model), F32), v((8, model), F32),
             v((n_f, 8, model), F32),
         ]
@@ -1213,12 +1272,95 @@
             flops=14 * 10**9, bytes_accessed=40 * 10**6, transcendentals=4 * 10**6
         ),
         name="attention_backward",
-    )(col, row, par, sums, tok, gm, lo, gb, ctx, q, kv, n1, full_a, full_o, pr)
-
-
-def spread_out(piece, index, count):
-    spots = (jnp.arange(count) == index).astype(F32)
-    return (piece[:, None, :] * spots[None, :, None]).reshape(piece.shape[0], -1)
+    )(ids, par, sums, tok, gm, lo, gb, ctx, q, kv, n1, full_a, full_o, pr)
+
+
+def finish_kernel(
+    n_f, total, lo_i, tg_i, e_i, r_i, a_i, o_i,
+    lo_o, tg_o, e_o, r_o, q_o, k_o, v_o, o_o, g1_o, s1_o, bo_o, g2_o, s2_o, br_o, bq_o, bv_o, be_o,
+    lo, tg, e, r, a, o, e32, r32, a32, o32, in_sem, out_sem,
+):
+    me = 2 * lax.axis_index("fsdp") + lax.axis_index("ctx")
+    shard, width = q_o.shape
+    parts = 4
+
+    def slab(ref, i):
+        size = ref.shape[0] // parts
+        return ref.at[pl.ds(i * size, size)]
+
+    def load(n, src, dst):
+        found = [
+            pltpu.make_async_copy(slab(src, i), slab(dst, i), in_sem.at[n, i]) for i in range(parts)
+        ]
+        for copy in found:
+            copy.start()
+        return found
+
+    outs = Outs(out_sem)
+    loads = [load(n, *pair) for n, pair in enumerate(((e_i, e), (r_i, r), (lo_i, lo), (a_i, a), (o_i, o), (tg_i, tg)))]
+
+    def widen(found, src, dst, out):
+        size = src.shape[0] // parts
+        for i, copy in enumerate(found):
+            copy.wait()
+            rows = pl.ds(i * size, size)
+            dst[rows, :] = src[rows, :].astype(F32)
+            outs.put(slab(dst, i), slab(out, i))
+
+    def pass_on(found, src, out):
+        for i, copy in enumerate(found):
+            copy.wait()
+            outs.put(slab(src, i), slab(out, i))
+
+    widen(loads[0], e, e32, e_o)
+    widen(loads[1], r, r32, r_o)
+    pass_on(loads[2], lo, lo_o.at[0])
+    for copy in loads[3]:
+        copy.wait()
+    for k, out in enumerate((q_o, k_o, v_o)):
+        a32[k] = a[:, k * width : (k + 1) * width].astype(F32)
+        outs.put(a32.at[k], out)
+    widen(loads[4], o, o32, o_o)
+    pass_on(loads[5], tg, tg_o.at[0])
+    for k, out in ((0, br_o), (2, bo_o), (4, g2_o), (5, s2_o), (6, g1_o), (7, s1_o)):
+        out[...] = total[k : k + 1, pl.ds(al(me * shard, shard), shard)]
+
+    def take_bias(out, line, base):
+        count, piece = out.shape
+        size = piece * 2 * n_f
+        wide = jnp.concatenate(
+            [total[line : line + 1, base + h * size : base + (h + 1) * size] for h in range(count)]
+        )
+        out[...] = lax.dot_general(
+            wide, picker(me, piece, 2 * n_f), (((1,), (1,)), ((), ())),
+            precision=lax.Precision.HIGHEST, preferred_element_type=F32,
+        )
+
+    take_bias(bq_o, 3, 0)
+    take_bias(bv_o, 3, width)
+    take_bias(be_o, 1, 0)
+    outs.wait()
+
+
+def finish(n_f, total, lo, tg, e, r, a, o, bias, wide_bias):
+    (rows, model), (shard, ff), width = lo.shape, e.shape, o.shape[0]
+    sds, dma, v = jax.ShapeDtypeStruct, pltpu.SemaphoreType.DMA, pltpu.VMEM
+    big = [(1, rows, model)] * 2 + [(shard, ff), (ff, shard)] + [(shard, width)] * 3 + [(width, shard)]
+    outs = tuple(sds(shape, BF if i < 2 else F32) for i, shape in enumerate(big))
+    outs += (sds((1, shard), F32),) * 6
+    outs += (sds(bias.shape, F32),) * 2 + (sds(wide_bias.shape, F32),)
+    return pl.pallas_call(
+        functools.partial(finish_kernel, n_f),
+        out_shape=outs,
+        in_specs=[VM] + [HBM] * 6,
+        out_specs=(HBM,) * 8 + (VM,) * 9,
+        scratch_shapes=[v(x.shape, BF) for x in (lo, tg, e, r, a, o)]
+        + [v((shard, ff), F32), v((ff, shard), F32), v((3, shard, width), F32), v((width, shard), F32)]
+        + [dma((6, 4)), dma((24,))],
+        compiler_params=pltpu.CompilerParams(vmem_limit_bytes=60 << 20),
+        cost_estimate=pl.CostEstimate(flops=10**6, bytes_accessed=18 * 10**6, transcendentals=0),
+        name="finish",
+    )(total, lo, tg, e, r, a, o)
 
 
 def local(
@@ -1227,65 +1369,27 @@
     expand_weight, expand_bias, reduce_weight, reduce_bias,
 ):
     n_f, n_t = lax.axis_size("fsdp"), lax.axis_size("tp")
-    n_s = 2 * n_f
     _, rows, model = tokens.shape
-    c = lax.axis_index("ctx")
-    index = 2 * lax.axis_index("fsdp") + c
-    width, ff = query_weight.shape[1], expand_weight.shape[1]
-    shard = query_weight.shape[0]
-    vectors = jnp.stack(
-        [first_gain, first_shift, output_bias, second_gain, second_shift, reduce_bias]
-    ).astype(F32)
-
-    def wide(bias):
-        full = spread_out(bias.astype(F32), index, n_s)
-        flat = full.reshape(1, -1)
-        return jnp.pad(flat, ((0, 0), (0, model - flat.shape[1])))
-
-    heads_bias = jnp.concatenate([query_bias, value_bias], axis=0)
-    small = jnp.concatenate([spread_out(vectors, index, n_s), wide(heads_bias), wide(expand_bias)])
-    ids = block_ids[0].reshape(2, rows)
-    near, far = lax.dynamic_index_in_dim(ids, c, 0), lax.dynamic_index_in_dim(ids, 1 - c, 0)
-    row = jnp.concatenate([near, far])
-    col = near.reshape(rows, 1)
-    wa = jnp.concatenate([query_weight, key_weight, value_weight], axis=1)
     tok = tokens.reshape(rows, model)
+    vectors = (first_gain, first_shift, output_bias, second_gain, second_shift, reduce_bias)
     n1, q, kv, ctx, n2, mid, par, full_a, full_o, full_e, full_r = forward(
-        n_f, n_t, tok, col, row, small, wa, output_weight, expand_weight, reduce_weight
+        n_f, n_t, tok, block_ids, vectors, (query_bias, value_bias, expand_bias),
+        query_weight, key_weight, value_weight, output_weight, expand_weight, reduce_weight,
     )
     gb, lo, gm, e_grad, r_part, sums = middle(
         n_f, n_t, live_count, n2, cotangent.reshape(rows, model), mid, par, full_e, full_r
     )
-    layer_out, tokens_grad, r_grad, o_grad, a_grad, total = backward(
-        n_f, n_t, col, row, par, sums, tok, gm, lo, gb, ctx, q, kv, n1, full_a, full_o, r_part
+    lo, tg, r_grad, o_grad, a_grad, total = backward(
+        n_f, n_t, block_ids, par, sums, tok, gm, lo, gb, ctx, q, kv, n1, full_a, full_o, r_part
     )
-
-    def vector(k):
-        return lax.dynamic_slice_in_dim(total[k], index * shard, shard)
-
-    def across(flat, like):
-        whole = flat.reshape(like.shape[0], -1)
-        return lax.dynamic_slice_in_dim(whole, index * like.shape[1], like.shape[1], 1)
-
-    a_grad = a_grad.astype(F32)
+    (
+        layer_out, tokens_grad, e_grad, r_grad, q_grad, k_grad, v_grad, o_grad,
+        g1, s1, b_o, g2, s2, b_r, b_q, b_v, b_e,
+    ) = finish(n_f, total, lo, tg, e_grad, r_grad, a_grad, o_grad, query_bias, expand_bias)
+    flat = lambda vector: vector.reshape(-1)
     return (
-        layer_out.reshape(1, rows, model),
-        tokens_grad.reshape(1, rows, model),
-        vector(6),
-        vector(7),
-        a_grad[:, :width],
-        across(total[3, :width], query_bias),
-        a_grad[:, width : 2 * width],
-        a_grad[:, 2 * width :],
-        across(total[3, width : 2 * width], value_bias),
-        o_grad.astype(F32),
-        vector(2),
-        vector(4),
-        vector(5),
-        e_grad.astype(F32),
-        across(total[1, :ff], expand_bias),
-        r_grad.astype(F32),
-        vector(0),
+        layer_out, tokens_grad, flat(g1), flat(s1), q_grad, b_q, k_grad, v_grad, b_v, o_grad,
+        flat(b_o), flat(g2), flat(s2), e_grad, b_e, r_grad, flat(b_r),
     )
 
 

time: 386 us -> 368 us (0.953)
  local copies, waits for them, and re-layouts: 15.8 us -> 0 us
  other arithmetic: 11.3 us -> 0 us
  Pallas kernels: 357 us -> 365 us
    pallas_call x0 -> x1, Pallas kernels: none -> 8.61 us  [finish(): pl.pallas_call(functools.partial(finish_kernel, n_f), out_shape=outs, in_...]
    convert_element_type x7 -> x0, other arithmetic: 6.49 us -> none  [the longest x1 2.7 us: local(): r_grad.astype(F32)]
    unnamed x17 -> x0, local copies, waits for them, and re-layouts: 4.3 us -> none
    another operation x9 -> x0, local copies, waits for them, and re-layouts: 3.99 us -> none  [the longest x7 3.98 us: local(): jnp.stack([first_gain, first_shift, output_bias, second_gain, second_shif...]
where the time goes in v3:
time: 368 us; the launch traced here: 367 us
  Pallas kernels  365 us (99%)
    pallas_call x1, Pallas kernels, forward(): pl.pallas_call(functools.partial(forward_kernel, n_f, n_t, chunks, lag),...  128 us
    pallas_call x1, Pallas kernels, backward(): pl.pallas_call(functools.partial(backward_kernel, n_f, n_t, chunks, lag,...  118 us
    pallas_call x1, Pallas kernels, middle(): pl.pallas_call(functools.partial(middle_kernel, n_f, n_t, chunks, lag), o...  111 us
    pallas_call x1, Pallas kernels, finish(): pl.pallas_call(functools.partial(finish_kernel, n_f), out_shape=outs, in_...  8.61 us

profile of v3, /device:TPU:0, one launch (start us, length us, event | category | flops | bytes accessed | tf_op | source)
XLA Modules:
  0.0 366.6 jit_solution(16390581403444160956)
XLA Ops:
  1.3 127.6 %attention_forward.1 = (bf16[512,2048]{1,0:T(8,128)(2,1)}, bf16[512,512]{1,0:T(8,128)(2,1)}, bf16[2,512,1024]{2,1,0:T(8,128)(2,1)}, bf16[512,512]{1,0:T(8,128)(2...) custom-call(bf16[512,2048]{1,0:T(8,128)(2,1)} %bitcast.9, ...), custom_call_target="tpu_custom_call" | custom-call | flops 8000000000 | bytes 60000000 | tf_op jit(solution)/shard_map/attention_forward/pallas_call | solution.py:583
  128.9 111.3 %feed_forward.1 = (bf16[512,2048]{1,0:T(8,128)(2,1)}, bf16[256,2048]{1,0:T(8,128)(2,1)}, f32[256,2048]{1,0:T(8,128)}, bf16[256,2048]{1,0:T(8,128)(2,1)}, bf16[4,...) custom-call(s32[1]{0:T(128)S(6)} %copy.36.live, bf16[512,2048]{1,0:T(8,128)(2,1)} %get-tuple-element.58.n2_i, ...), custom_call_target="tpu_custom_call" | custom-call | flops 25999998976 | bytes 40000000 | tf_op jit(solution)/shard_map/feed_forward/pallas_call | solution.py:909
  240.1 117.7 %attention_backward.1 = (bf16[512,2048]{1,0:T(8,128)(2,1)}, bf16[512,2048]{1,0:T(8,128)(2,1)}, bf16[2048,256]{1,0:T(8,128)(2,1)}, bf16[512,256]{1,0:T(8,128)(2,1...) custom-call(s32[1,1024]{1,0:T(1,128)} %ids.3, f32[8,2048]{1,0:T(8,128)} %get-tuple-element.57.par, ...), custom_call_target="tpu_custom_call" | custom-call | flops 14000000000 | bytes 40000000 | tf_op jit(solution)/shard_map/attention_backward/pallas_call | solution.py:1244
  357.8 8.6 %finish.1 = (bf16[1,512,2048]{2,1,0:T(8,128)(2,1)}, bf16[1,512,2048]{2,1,0:T(8,128)(2,1)}, f32[256,2048]{1,0:T(8,128)}, f32[2048,256]{1,0:T(8,128)}, f32[256,512...) custom-call(f32[8,2048]{1,0:T(8,128)} %get-tuple-element.73.total, ...), custom_call_target="tpu_custom_call" | custom-call | flops 1000000 | bytes 18000000 | tf_op jit(solution)/shard_map/finish/pallas_call | solution.py:1352

commit v4 on v3

--- a/solution.py
+++ b/solution.py
@@ -17,6 +17,8 @@
 BF = jnp.bfloat16
 F32 = jnp.float32
 epsilon = 1e-05
+TILES = 4
+LATE = 1
 
 
 def dot(left, right):
@@ -376,9 +378,9 @@
 def forward_kernel(
     n_f, n_t, chunks, lag,
     tok, ids, g1, s1, b_o, g2, s2, b_r, b_q, b_v, b_e, wq, wk, wv, wo, we, wr,
-    n1_o, q_o, kv_o, ctx_o, n2_o, mid_o, par_o, a_o, o_o, e_o, r_o,
+    n1_o, q_o, kv_o, ctx_o, probs_o, n2_o, mid_o, par_o, a_o, o_o, e_o, r_o,
     tokv, n1, full_a, full_o, stage_e, stage_r, q, kv, ctx, part, rbuf, norm, mid,
-    col, row, small, sib_small, all_small, par,
+    probs, col, row, small, sib_small, all_small, par,
     ga_s, ga_r, go_s, go_r, ge_s, ge_r, gr_s, gr_r,
     ls_s, ls_r, lg_s, lg_r, sm_s, sm_r, kv_s, kv_r, in_sem, out_sem,
 ):
@@ -393,6 +395,7 @@
     me = 2 * here.f + here.c
     a_slot, o_slot = row_slots(full_a, shard), column_slots(full_o, shard)
     e_slot, r_slot = row_slots(e_o, shard), column_slots(r_o, shard)
+    wr = wr.at[pl.ds(0, r_o.shape[0])]
     loads = [
         pltpu.make_async_copy(wo, o_slot(me, None), in_sem.at[1]),
         pltpu.make_async_copy(we, stage_e, in_sem.at[2]),
@@ -507,12 +510,16 @@
         far = jnp.exp(far - top)
         total = jnp.sum(near, axis=-1, keepdims=True) + jnp.sum(far, axis=-1, keepdims=True)
         inv = 1.0 / total
-        out = dot((near * inv).astype(BF), kv[0, :, vc]) + dot((far * inv).astype(BF), kv[1, :, vc])
-        ctx[rows, kc] = out.astype(BF)
+        near = (near * inv).astype(BF)
+        far = (far * inv).astype(BF)
+        probs[h, rows, 0:rows_all] = near
+        probs[h, rows, rows_all:] = far
+        ctx[rows, kc] = (dot(near, kv[0, :, vc]) + dot(far, kv[1, :, vc])).astype(BF)
         return 0
 
     lax.fori_loop(0, 2 * heads, head, 0)
     outs.put(ctx, ctx_o)
+    outs.put(probs, probs_o)
 
     wide = model // 4
 
@@ -561,9 +568,10 @@
     outs.wait()
 
 
-def forward(n_f, n_t, tok, ids, vectors, biases, wq, wk, wv, wo, we, wr, chunks=16, lag=3):
+def forward(n_f, n_t, tok, ids, vectors, biases, wq, wk, wv, wo, we, wr, chunks=16, lag=2):
     rows, model = tok.shape
     shard, width, ff = wq.shape[0], wo.shape[0], we.shape[1]
+    early = ff - LATE * (ff // TILES)
     sds = jax.ShapeDtypeStruct
     dma = pltpu.SemaphoreType.DMA
     outs = (
@@ -571,13 +579,14 @@
         sds((rows, width), BF),
         sds((2, rows, 2 * width), BF),
         sds((rows, width), BF),
+        sds((width // HD, rows, 2 * rows), BF),
         sds((rows, model), BF),
         sds((rows // 2, model), F32),
         sds((8, model), F32),
         sds((model, 3 * width), BF),
         sds((width, model), BF),
         sds((model, ff), BF),
-        sds((ff, model), BF),
+        sds((early, model), BF),
     )
     v = pltpu.VMEM
     return pl.pallas_call(
@@ -587,10 +596,11 @@
         out_specs=(ANY,) * len(outs),
         scratch_shapes=[
             v((rows, model), BF), v((rows, model), BF), v((model, 3 * width), BF),
-            v((width, model), BF), v((shard, ff), BF), v((ff, shard), BF),
+            v((width, model), BF), v((shard, ff), BF), v((early, shard), BF),
             v((rows, width), BF), v((2, rows, 2 * width), BF), v((rows, width), BF),
             v((rows, model), BF), v((2, rows // 2, model), BF), v((rows, model), BF),
-            v((rows // 2, model), F32), v((rows, 1), F32), v((2, rows), F32), v((8, model), F32),
+            v((rows // 2, model), F32), v((width // HD, rows, 2 * rows), BF),
+            v((rows, 1), F32), v((2, rows), F32), v((8, model), F32),
             v((8, model), F32), v((n_f, 8, model), F32), v((8, model), F32),
         ]
         + [dma((Gather.sems(n_f),))] * 8
@@ -724,20 +734,25 @@
 
 def middle_kernel(
     n_f, n_t, chunks, lag,
-    live, n2_i, cot, mid_i, par, full_e, full_r,
+    live, n2_i, cot, mid_i, par, full_e, full_r, wr,
     gb_o, lo_o, gm_o, eg_o, pr_o, sums_o,
     ev, rv, n2, g, act, gh, part, part2, rbuf, rbuf2, gb, mid, gm, lo, sums,
     e_sum, e_half, e_full, r_sum,
-    e_s, e_r, r_s, r_r,
+    e_s, e_r, r_s, r_r, gl_s, gl_r,
     ls_s, ls_r, lg_s, lg_r, ms_s, ms_r, in_sem, te_sem, tr_sem, out_sem,
 ):
     here = Place(n_f, n_t)
     rows_all, model = n2.shape
     ff = act.shape[1]
     shard = e_sum.shape[1]
-    tiles = 4
+    tiles = TILES
     ft = ff // tiles
+    early = full_r.shape[0]
+    late = ff - early
     here.greet_signal()
+    late_own = wr.at[pl.ds(early, late)]
+    late_slot = column_slots(rv.at[pl.ds(early, late)], shard)
+    gl = Gather(here, own_part(late_own), late_slot, gl_s, gl_r)
 
     def e_load(i):
         cols = pl.ds(i * ft, ft)
@@ -751,15 +766,19 @@
         pltpu.make_async_copy(n2_i, n2, in_sem.at[0]),
         pltpu.make_async_copy(cot, g, in_sem.at[1]),
         pltpu.make_async_copy(mid_i, mid, in_sem.at[2]),
+        pltpu.make_async_copy(late_own, late_slot(2 * here.f + here.c, None), in_sem.at[3]),
     ]
     loads[0].start()
     e_load(0).start()
     loads[1].start()
-    r_load(0).start()
     for i in range(1, tiles):
         e_load(i).start()
+    for i in range(early // ft):
         r_load(i).start()
+    loads[3].start()
     loads[2].start()
+    here.greet_wait()
+    gl.start()
     alive = live[0].astype(F32)
     loads[0].wait()
     loads[1].wait()
@@ -777,27 +796,26 @@
         cols = pl.ds(i * ft, ft)
         e_load(i).wait()
         h = dot(n2[...], ev[:, cols]) + par[7:8, cols]
-        r_load(i).wait()
-        ga = dot_nt(g[...], rv[cols, :])
         bell = 0.5 * (1.0 + lax.erf(h * (1.0 / math.sqrt(2.0))))
         act[:, cols] = (h * bell).astype(BF)
         slope = bell + h * jnp.exp(-0.5 * h * h) * (1.0 / math.sqrt(2.0 * math.pi))
-        low = (ga * slope).astype(BF)
+        gh[:, cols] = slope.astype(BF)
+
+    def grad_piece(cols):
+        low = (dot_nt(g[...], rv[cols, :]) * gh[:, cols].astype(F32)).astype(BF)
         gh[:, cols] = low
         sums[1:2, cols] = jnp.sum(low.astype(F32), axis=0, keepdims=True)
 
     for i in range(tiles):
         hidden_tile(i)
-    wide = model // 4
-
-    def back_tile(i, _):
-        cols = pl.ds(al(i * wide, wide), wide)
-        part[:, cols] = dot_nt(gh[...], ev[cols, :]).astype(BF)
-        return 0
-
-    lax.fori_loop(0, 4, back_tile, 0)
-    loads[2].wait()
-    here.greet_wait()
+    for s in range(1, here.m):
+        gl.step(s)
+    for i in range(early // ft):
+        r_load(i).wait()
+        grad_piece(pl.ds(i * ft, ft))
+    gl.step(here.m)
+    loads[3].wait()
+    gl.arrive()
     line = Line(here, part, rbuf, gb, (ls_s, ls_r, lg_s, lg_r), chunks, lag)
     line2 = Line(here, part2, rbuf2, gb, (ms_s, ms_r, None, None), chunks, lag)
     outs = Outs(out_sem)
@@ -813,6 +831,32 @@
     def final2(rows, span, total):
         lo[span, :] = ((mid[span, :] + total + par[5:6, :]) * alive).astype(BF)
 
+    def mlp(i, _):
+        cols = pl.ds(al(i * shard, shard), shard)
+        part2[:, cols] = dot(act[...], rv[:, cols]).astype(BF)
+        return 0
+
+    lax.fori_loop(0, 2 * n_f, mlp, 0)
+    loads[2].wait()
+    piece = ft // 2
+    pieces, backs = late // piece, 8
+    wide = model // backs
+
+    def grad_step(i, _):
+        grad_piece(pl.ds(al(early + i * piece, piece), piece))
+        line2.tick(i, final2, back=False)
+        return 0
+
+    def back_step(i, _):
+        cols = pl.ds(al(i * wide, wide), wide)
+        part[:, cols] = dot_nt(gh[...], ev[cols, :]).astype(BF)
+        line2.tick(pieces + i, final2, back=False)
+        return 0
+
+    lax.fori_loop(0, pieces, grad_step, 0)
+    lax.fori_loop(0, backs, back_step, 0)
+    gl.finish()
+
     def e_stage(i):
         return ev.at[pl.ds(al(i * shard, shard), shard)]
 
@@ -835,9 +879,6 @@
         es.cross(i).wait_recv()
         es.combine(i, value)
 
-    def mlp(i):
-        part2[:, cols_of(i)] = dot(act[...], rv[:, cols_of(i)]).astype(BF)
-
     def r_other(i):
         value = dot_tn(act[...], g[:, cols_of(rs.shard(i, True))])
         rv[:, cols_of(i)] = value.astype(BF)
@@ -848,20 +889,18 @@
         rs.cross(i).wait_recv()
         rs.combine(i, value)
 
-    n_s = 2 * n_f
     a, b = n_f, 2 * n_f
-    d = b + n_s
-    ticks = max(line.ticks(), d + 2 * n_f, d + line2.sum_ticks())
+    ahead = pieces + backs
+    ticks = max(line.ticks(), b + 2 * n_f, line2.sum_ticks() - ahead)
     gap = max(1, (ticks - b) // (n_f // 2 + 1))
 
     def tick(tau, _):
         line.tick(tau, final)
-        line2.tick(tau - d, final2, back=False)
+        line2.tick(tau + ahead, final2, back=False)
         span_when(tau, 0, a, e_other)
         span_when(tau, a, b, e_own)
-        span_when(tau, b, d, mlp)
-        span_when(tau, d, d + n_f, r_other)
-        span_when(tau, d + n_f, d + 2 * n_f, r_own)
+        span_when(tau, b, b + n_f, r_other)
+        span_when(tau, b + n_f, b + 2 * n_f, r_own)
 
         @pl.when(tau == a)
         def _():
@@ -893,7 +932,7 @@
     outs.wait()
 
 
-def middle(n_f, n_t, live, n2, cot, mid, par, full_e, full_r, chunks=16, lag=3):
+def middle(n_f, n_t, live, n2, cot, mid, par, full_e, full_r, wr, chunks=16, lag=2):
     rows, model = n2.shape
     ff = full_e.shape[1]
     shard = model // (2 * n_f)
@@ -909,7 +948,7 @@
     return pl.pallas_call(
         functools.partial(middle_kernel, n_f, n_t, chunks, lag),
         out_shape=outs,
-        in_specs=[pl.BlockSpec(memory_space=pltpu.SMEM), ANY, ANY, ANY, VM, ANY, ANY],
+        in_specs=[pl.BlockSpec(memory_space=pltpu.SMEM), ANY, ANY, ANY, VM, ANY, ANY, ANY],
         out_specs=(ANY,) * len(outs),
         scratch_shapes=[
             v((model, ff), BF), v((ff, model), BF), v((rows, model), BF), v((rows, model), BF),
@@ -922,9 +961,10 @@
         + [v((n_f, ff, shard), BF)]
         + Scatter.sems(n_f)
         + Scatter.sems(n_f)
+        + [dma((Gather.sems(n_f),))] * 2
         + Line.sems(chunks)
         + Line.sems(chunks)[:2]
-        + [dma((3,)), dma((4,)), dma((4,)), dma((6,))],
+        + [dma((4,)), dma((4,)), dma((4,)), dma((6,))],
         compiler_params=pltpu.CompilerParams(
             collective_id=1, has_side_effects=True, vmem_limit_bytes=63 << 20
         ),
@@ -932,15 +972,15 @@
             flops=26 * 10**9, bytes_accessed=40 * 10**6, transcendentals=4 * 10**6
         ),
         name="feed_forward",
-    )(live, n2, cot, mid, par, full_e, full_r)
+    )(live, n2, cot, mid, par, full_e, full_r, wr)
 
 
 def backward_kernel(
     n_f, n_t, chunks, lag, chunks2, lag2,
-    ids, par, sums_i, tok, gm_i, lo_i, gb_i, ctx_i, q_i, kv_i, n1_i, full_a, full_o, pr_i,
+    par, sums_i, tok, gm_i, lo_i, gb_i, ctx_i, q_i, kv_i, probs_i, n1_i, full_a, full_o, pr_i,
     lo_o, tg_o, rg_o, og_o, ag_o, small_o,
-    av, ov, gb, n1, tokh, gm, ctx, q, kv, gc, grads, near_g, far_g, got_g, lof, norm, part, rbuf,
-    col, row, sm, tp_small, sib_small, all_small,
+    av, ov, gb, n1, tokh, gm, ctx, q, kv, probs, gc, grads, near_g, far_g, got_g, lof, norm, part, rbuf,
+    sm, tp_small, sib_small, all_small,
     r_sum, r_half, r_full, o_sum, o_half, o_full, a_sum, a_half, a_full,
     r_s, r_r, o_s, o_r, a_s, a_r,
     ls_s, ls_r, lg_s, lg_r, ms_s, ms_r, mg_s, mg_r,
@@ -956,7 +996,7 @@
     here.greet_signal()
     mine = pl.ds(al(here.side * half, half), half)
     pairs = [
-        (gb_i, gb), (full_o, ov), (pr_i, r_sum), (q_i, q), (kv_i, kv), (ctx_i, ctx),
+        (gb_i, gb), (full_o, ov), (pr_i, r_sum), (q_i, q), (kv_i, kv), (probs_i, probs), (ctx_i, ctx),
         (full_a, av), (n1_i, n1), (gm_i, gm), (tok.at[mine], tokh),
     ]
     loads = [pltpu.make_async_copy(s, d, in_sem.at[i]) for i, (s, d) in enumerate(pairs)]
@@ -966,7 +1006,6 @@
     lo_load = pltpu.make_async_copy(lo_i, lof.at[mine], in_sem.at[len(pairs)])
     pl.when(end)(lo_load.start)
     sm[...] = sums_i[...]
-    place_ids(ids, col, row, here)
     loads[0].wait()
     loads[1].wait()
     gc[...] = dot_nt(gb[...], ov[...]).astype(BF)
@@ -1001,28 +1040,16 @@
     os = Scatter(here, o_sum, lambda i: ov.at[:, cols_of(i)], o_half, o_full, o_s, o_r, 128)
     sa = Scatter(here, a_sum, lambda i: av.at[rows_of(i)], a_half, a_full, a_s, a_r, 64)
     rs.launch(here.m)
-    for load in loads[3:6]:
+    for load in loads[3:7]:
         load.wait()
 
     def head(h, _):
         kc = pl.ds(al(h * HD, HD), HD)
         vc = pl.ds(al(width + h * HD, HD), HD)
-        ids = col[...]
         qh, gh = q[:, kc], gc[:, kc]
-        near = allowed_scores(qh, kv[0, :, kc], ids, row[0:1, :], scale)
-        far = allowed_scores(qh, kv[1, :, kc], ids, row[1:2, :], scale)
-        top = jnp.maximum(
-            jnp.max(near, axis=-1, keepdims=True), jnp.max(far, axis=-1, keepdims=True)
-        )
-        near = jnp.exp(near - top)
-        far = jnp.exp(far - top)
-        inv = 1.0 / (
-            jnp.sum(near, axis=-1, keepdims=True) + jnp.sum(far, axis=-1, keepdims=True)
-        )
-        near = near * inv
-        far = far * inv
-        near_gv = dot_tn(near.astype(BF), gh)
-        far_gv = dot_tn(far.astype(BF), gh)
+        near_low, far_low = probs[h, :, 0:rows_all], probs[h, :, rows_all:]
+        near_gv, far_gv = dot_tn(near_low, gh), dot_tn(far_low, gh)
+        near, far = near_low.astype(F32), far_low.astype(F32)
         gp_near = dot_nt(gh, kv[0, :, vc])
         gp_far = dot_nt(gh, kv[1, :, vc])
         inner = jnp.sum(gp_near * near, axis=-1, keepdims=True) + jnp.sum(
@@ -1036,8 +1063,8 @@
         far_g[:, kc] = (dot_tn(gs_far, qh) * scale).astype(BF)
         near_g[:, vc] = near_gv
         far_g[:, vc] = far_gv.astype(BF)
-        back_tick(2 * h)
-        back_tick(2 * h + 1)
+        for k in range(3):
+            back_tick(3 * h + k)
 
         @pl.when(h == heads // 2)
         def _():
@@ -1053,24 +1080,16 @@
         rs.absorb(s)
         rs.launch(s - 1)
 
-    def out_task(i, _):
+    def out_other(i):
         value = dot_tn(ctx[...], gb[:, cols_of(os.shard(i, True))])
         ov[:, cols_of(i)] = value.astype(BF)
         os.cross(i).start()
-        back_tick(2 * heads + i)
-        return 0
-
-    lax.fori_loop(0, n_f, out_task, 0)
-
-    def out_own(i, _):
+
+    def out_own(i):
         value = dot_tn(ctx[...], gb[:, cols_of(os.shard(i, False))])
         os.cross(i).wait_recv()
         os.combine(i, value)
-        back_tick(2 * heads + n_f + i)
-        return 0
-
-    lax.fori_loop(0, n_f, out_own, 0)
-    os.launch(here.m)
+
     swap.wait_recv()
 
     def add_rows(i, total):
@@ -1083,7 +1102,7 @@
     sm[3:4, 0 : 2 * width] = lax.fori_loop(
         0, rows_all // 128, add_rows, jnp.zeros((1, 2 * width), F32)
     )
-    loads[6].wait()
+    loads[7].wait()
     wide = model // 4
 
     def back_part(i, _):
@@ -1092,7 +1111,7 @@
         return 0
 
     lax.fori_loop(0, 4, back_part, 0)
-    for load in loads[7:]:
+    for load in loads[8:]:
         load.wait()
 
     def final(rows, span, total):
@@ -1119,14 +1138,14 @@
     sm[2:3, :] = jnp.zeros((1, model), F32)
     blocks = rows_all // 64
     d = 2 * n_f
-    ticks = max(line.ticks(), d + blocks)
+    full = d + 2 * n_f
+    ticks = max(line.ticks(), d + blocks, full + 2 * here.m)
     plan = [(d, rs.last)]
-    room = ticks - d
+    room, spots = ticks - full, here.m - 1
     for s in range(here.m, 1, -1):
         k = here.m - s
-        spots = here.m - 1
-        plan.append((d + 2 + (room * k) // (2 * spots), functools.partial(ring_step, os, s)))
-        plan.append((d + room // 4 + (room * k) // (2 * spots), functools.partial(ring_step, sa, s)))
+        plan.append((full + 1 + (room * k) // (2 * spots), functools.partial(ring_step, os, s)))
+        plan.append((d + 3 + (ticks - d) // 4 + (room * k) // (2 * spots), functools.partial(ring_step, sa, s)))
 
     def tick(tau, _):
         line.tick(tau, final)
@@ -1134,6 +1153,10 @@
         span_when(tau, n_f, d, a_own)
         span_when(tau, d, d + blocks, branch_sum)
         pl.when(tau == n_f)(lambda: sa.launch(here.m))
+        span_when(tau, d, d + n_f, out_other)
+        span_when(tau, d + n_f, full, out_own)
+        pl.when(tau == d + n_f)(lambda: os.launch(here.m))
+        back_tick(3 * heads + tau)
         for at, event in plan:
             pl.when(tau == at)(event)
         return 0
@@ -1146,7 +1169,7 @@
         back_tick(tau)
         return 0
 
-    lax.fori_loop(min(2 * heads + 2 * n_f, back_ticks), back_ticks, rest, 0)
+    lax.fori_loop(min(3 * heads + ticks, back_ticks), back_ticks, rest, 0)
     outs.put(lof, lo_o)
 
     def tp_copy(k):
@@ -1226,8 +1249,8 @@
 
 
 def backward(
-    n_f, n_t, ids, par, sums, tok, gm, lo, gb, ctx, q, kv, n1, full_a, full_o, pr,
-    chunks=16, lag=3, chunks2=8, lag2=2,
+    n_f, n_t, par, sums, tok, gm, lo, gb, ctx, q, kv, probs, n1, full_a, full_o, pr,
+    chunks=16, lag=2, chunks2=8, lag2=2,
 ):
     rows, model = gb.shape
     width, ff = q.shape[1], pr.shape[1]
@@ -1244,16 +1267,16 @@
     return pl.pallas_call(
         functools.partial(backward_kernel, n_f, n_t, chunks, lag, chunks2, lag2),
         out_shape=outs,
-        in_specs=[VM] * 3 + [ANY] * 11,
+        in_specs=[VM] * 2 + [ANY] * 12,
         out_specs=(ANY,) * len(outs),
         scratch_shapes=[
             v((model, 3 * width), BF), v((width, model), BF), v((rows, model), BF),
             v((rows, model), BF), v((rows // 2, model), BF), v((rows // 2, model), F32),
             v((rows, width), BF), v((rows, width), BF), v((2, rows, 2 * width), BF),
+            v((width // HD, rows, 2 * rows), BF),
             v((rows, width), BF), v((rows, 3 * width), BF), v((rows, 2 * width), F32),
             v((rows, 2 * width), BF), v((rows, 2 * width), BF), v((rows, model), BF),
             v((rows, model), BF), v((rows, model), BF), v((2, rows // 2, model), BF),
-            v((rows, 1), F32), v((2, rows), F32),
             v((8, model), F32), v((2, 8, model), F32), v((8, model), F32),
             v((n_f, 8, model), F32),
         ]
@@ -1264,7 +1287,7 @@
         + Line.sems(chunks)
         + Line.sems(chunks2)
         + [dma((1,)), dma((1,)), dma((n_t - 1,)), dma((2,)), dma((1,)), dma((1,))]
-        + [dma((n_f,)), dma((n_f,)), dma((11,)), dma((6,))],
+        + [dma((n_f,)), dma((n_f,)), dma((12,)), dma((6,))],
         compiler_params=pltpu.CompilerParams(
             collective_id=2, has_side_effects=True, vmem_limit_bytes=63 << 20
         ),
@@ -1272,7 +1295,7 @@
             flops=14 * 10**9, bytes_accessed=40 * 10**6, transcendentals=4 * 10**6
         ),
         name="attention_backward",
-    )(ids, par, sums, tok, gm, lo, gb, ctx, q, kv, n1, full_a, full_o, pr)
+    )(par, sums, tok, gm, lo, gb, ctx, q, kv, probs, n1, full_a, full_o, pr)
 
 
 def finish_kernel(
@@ -1372,15 +1395,15 @@
     _, rows, model = tokens.shape
     tok = tokens.reshape(rows, model)
     vectors = (first_gain, first_shift, output_bias, second_gain, second_shift, reduce_bias)
-    n1, q, kv, ctx, n2, mid, par, full_a, full_o, full_e, full_r = forward(
+    n1, q, kv, ctx, probs, n2, mid, par, full_a, full_o, full_e, full_r = forward(
         n_f, n_t, tok, block_ids, vectors, (query_bias, value_bias, expand_bias),
         query_weight, key_weight, value_weight, output_weight, expand_weight, reduce_weight,
     )
     gb, lo, gm, e_grad, r_part, sums = middle(
-        n_f, n_t, live_count, n2, cotangent.reshape(rows, model), mid, par, full_e, full_r
+        n_f, n_t, live_count, n2, cotangent.reshape(rows, model), mid, par, full_e, full_r, reduce_weight
     )
     lo, tg, r_grad, o_grad, a_grad, total = backward(
-        n_f, n_t, block_ids, par, sums, tok, gm, lo, gb, ctx, q, kv, n1, full_a, full_o, r_part
+        n_f, n_t, par, sums, tok, gm, lo, gb, ctx, q, kv, probs, n1, full_a, full_o, r_part
     )
     (
         layer_out, tokens_grad, e_grad, r_grad, q_grad, k_grad, v_grad, o_grad,

time: 368 us -> 363 us (0.986)
  Pallas kernels: 365 us -> 361 us
    pallas_call x1, Pallas kernels: 118 us -> 113 us  [backward(): pl.pallas_call(functools.partial(backward_kernel, n_f, n_t, chunks, lag,...]
where the time goes in v4:
time: 363 us
  Pallas kernels  361 us (99%)
    pallas_call x1, Pallas kernels, forward(): pl.pallas_call(functools.partial(forward_kernel, n_f, n_t, chunks, lag),...  125 us
    pallas_call x1, Pallas kernels, middle(): pl.pallas_call(functools.partial(middle_kernel, n_f, n_t, chunks, lag), o...  115 us
    pallas_call x1, Pallas kernels, backward(): pl.pallas_call(functools.partial(backward_kernel, n_f, n_t, chunks, lag,...  113 us
    pallas_call x1, Pallas kernels, finish(): pl.pallas_call(functools.partial(finish_kernel, n_f), out_shape=outs, in_...  8.61 us

profile of v4, /device:TPU:0, one launch (start us, length us, event | category | flops | bytes accessed | tf_op | source)
XLA Modules:
  0.0 362.7 jit_solution(17988778216783481045)
XLA Ops:
  1.3 125.0 %attention_forward.1 = (bf16[512,2048]{1,0:T(8,128)(2,1)}, bf16[512,512]{1,0:T(8,128)(2,1)}, bf16[2,512,1024]{2,1,0:T(8,128)(2,1)}, bf16[512,512]{1,0:T(8,128)(2...) custom-call(bf16[512,2048]{1,0:T(8,128)(2,1)} %bitcast.9, ...), custom_call_target="tpu_custom_call" | custom-call | flops 8000000000 | bytes 60000000 | tf_op jit(solution)/shard_map/attention_forward/pallas_call | solution.py:592
  126.4 114.9 %feed_forward.1 = (bf16[512,2048]{1,0:T(8,128)(2,1)}, bf16[256,2048]{1,0:T(8,128)(2,1)}, f32[256,2048]{1,0:T(8,128)}, bf16[256,2048]{1,0:T(8,128)(2,1)}, bf16[4,...) custom-call(s32[1]{0:T(128)S(6)} %copy.36.live, bf16[512,2048]{1,0:T(8,128)(2,1)} %get-tuple-element.59.n2_i, ...), custom_call_target="tpu_custom_call" | custom-call | flops 25999998976 | bytes 40000000 | tf_op jit(solution)/shard_map/feed_forward/pallas_call | solution.py:948
  241.2 112.7 %attention_backward.1 = (bf16[512,2048]{1,0:T(8,128)(2,1)}, bf16[512,2048]{1,0:T(8,128)(2,1)}, bf16[2048,256]{1,0:T(8,128)(2,1)}, bf16[512,256]{1,0:T(8,128)(2,1...) custom-call(f32[8,2048]{1,0:T(8,128)} %get-tuple-element.58.par, f32[8,2048]{1,0:T(8,128)} %get-tuple-element.63.sums_i, ...), custom_call_target="tpu_custom_call" | custom-call | flops 14000000000 | bytes 40000000 | tf_op jit(solution)/shard_map/attention_backward/pallas_call | solution.py:1267
  354.0 8.6 %finish.1 = (bf16[1,512,2048]{2,1,0:T(8,128)(2,1)}, bf16[1,512,2048]{2,1,0:T(8,128)(2,1)}, f32[256,2048]{1,0:T(8,128)}, f32[2048,256]{1,0:T(8,128)}, f32[256,512...) custom-call(f32[8,2048]{1,0:T(8,128)} %get-tuple-element.75.total, ...), custom_call_target="tpu_custom_call" | custom-call | flops 1000000 | bytes 18000000 | tf_op jit(solution)/shard_map/finish/pallas_call | solution.py:1375

commit v5 on v4

--- a/solution.py
+++ b/solution.py
@@ -735,11 +735,11 @@
 def middle_kernel(
     n_f, n_t, chunks, lag,
     live, n2_i, cot, mid_i, par, full_e, full_r, wr,
-    gb_o, lo_o, gm_o, eg_o, pr_o, sums_o,
-    ev, rv, n2, g, act, gh, part, part2, rbuf, rbuf2, gb, mid, gm, lo, sums,
+    gb_o, p2_o, gm_o, eg_o, pr_o, sums_o,
+    ev, rv, n2, g, act, gh, part, part2, rbuf, gb, mid, gm, sums,
     e_sum, e_half, e_full, r_sum,
     e_s, e_r, r_s, r_r, gl_s, gl_r,
-    ls_s, ls_r, lg_s, lg_r, ms_s, ms_r, in_sem, te_sem, tr_sem, out_sem,
+    ls_s, ls_r, lg_s, lg_r, in_sem, te_sem, tr_sem, out_sem,
 ):
     here = Place(n_f, n_t)
     rows_all, model = n2.shape
@@ -817,7 +817,6 @@
     loads[3].wait()
     gl.arrive()
     line = Line(here, part, rbuf, gb, (ls_s, ls_r, lg_s, lg_r), chunks, lag)
-    line2 = Line(here, part2, rbuf2, gb, (ms_s, ms_r, None, None), chunks, lag)
     outs = Outs(out_sem)
 
     def final(rows, span, total):
@@ -828,15 +827,10 @@
         sums[4:5, :] += jnp.sum(total * scaled, axis=0, keepdims=True)
         sums[5:6, :] += jnp.sum(total, axis=0, keepdims=True)
 
-    def final2(rows, span, total):
-        lo[span, :] = ((mid[span, :] + total + par[5:6, :]) * alive).astype(BF)
-
-    def mlp(i, _):
+    def mlp(i):
         cols = pl.ds(al(i * shard, shard), shard)
         part2[:, cols] = dot(act[...], rv[:, cols]).astype(BF)
-        return 0
-
-    lax.fori_loop(0, 2 * n_f, mlp, 0)
+
     loads[2].wait()
     piece = ft // 2
     pieces, backs = late // piece, 8
@@ -844,13 +838,11 @@
 
     def grad_step(i, _):
         grad_piece(pl.ds(al(early + i * piece, piece), piece))
-        line2.tick(i, final2, back=False)
         return 0
 
     def back_step(i, _):
         cols = pl.ds(al(i * wide, wide), wide)
         part[:, cols] = dot_nt(gh[...], ev[cols, :]).astype(BF)
-        line2.tick(pieces + i, final2, back=False)
         return 0
 
     lax.fori_loop(0, pieces, grad_step, 0)
@@ -890,17 +882,17 @@
         rs.combine(i, value)
 
     a, b = n_f, 2 * n_f
-    ahead = pieces + backs
-    ticks = max(line.ticks(), b + 2 * n_f, line2.sum_ticks() - ahead)
+    d = b + 2 * n_f
+    ticks = max(line.ticks(), d + 2 * n_f)
     gap = max(1, (ticks - b) // (n_f // 2 + 1))
 
     def tick(tau, _):
         line.tick(tau, final)
-        line2.tick(tau + ahead, final2, back=False)
         span_when(tau, 0, a, e_other)
         span_when(tau, a, b, e_own)
-        span_when(tau, b, b + n_f, r_other)
-        span_when(tau, b + n_f, b + 2 * n_f, r_own)
+        span_when(tau, b, d, mlp)
+        span_when(tau, d, d + n_f, r_other)
+        span_when(tau, d + n_f, d + 2 * n_f, r_own)
 
         @pl.when(tau == a)
         def _():
@@ -918,14 +910,13 @@
     lax.fori_loop(0, ticks, tick, 0)
     outs.put(gb, gb_o)
     outs.put(gm, gm_o)
-    outs.put(lo, lo_o)
+    outs.put(part2, p2_o)
     outs.put(r_sum, pr_o)
     outs.put(sums, sums_o)
     es.last()
     outs.put(e_sum.at[here.f], eg_o)
     line.finish_sum()
     line.finish_back()
-    line2.finish_sum()
     es.finish()
     for i in range(n_f):
         rs.cross(i).wait_send()
@@ -939,7 +930,7 @@
     sds, dma, v = jax.ShapeDtypeStruct, pltpu.SemaphoreType.DMA, pltpu.VMEM
     outs = (
         sds((rows, model), BF),
-        sds((rows // 2, model), BF),
+        sds((rows, model), BF),
         sds((rows // 2, model), F32),
         sds((shard, ff), BF),
         sds((n_f, ff, shard), BF),
@@ -953,8 +944,8 @@
         scratch_shapes=[
             v((model, ff), BF), v((ff, model), BF), v((rows, model), BF), v((rows, model), BF),
             v((rows, ff), BF), v((rows, ff), BF), v((rows, model), BF), v((rows, model), BF),
-            v((2, rows // 2, model), BF), v((2, rows // 2, model), BF), v((rows, model), BF),
-            v((rows // 2, model), F32), v((rows // 2, model), F32), v((rows // 2, model), BF),
+            v((2, rows // 2, model), BF), v((rows, model), BF),
+            v((rows // 2, model), F32), v((rows // 2, model), F32),
             v((8, model), F32),
         ]
         + Scatter.buffers(n_f, shard, ff)
@@ -963,7 +954,6 @@
         + Scatter.sems(n_f)
         + [dma((Gather.sems(n_f),))] * 2
         + Line.sems(chunks)
-        + Line.sems(chunks)[:2]
         + [dma((4,)), dma((4,)), dma((4,)), dma((6,))],
         compiler_params=pltpu.CompilerParams(
             collective_id=1, has_side_effects=True, vmem_limit_bytes=63 << 20
@@ -977,9 +967,9 @@
 
 def backward_kernel(
     n_f, n_t, chunks, lag, chunks2, lag2,
-    par, sums_i, tok, gm_i, lo_i, gb_i, ctx_i, q_i, kv_i, probs_i, n1_i, full_a, full_o, pr_i,
+    live, par, sums_i, tok, gm_i, mid_i, p2_i, gb_i, ctx_i, q_i, kv_i, probs_i, n1_i, full_a, full_o, pr_i,
     lo_o, tg_o, rg_o, og_o, ag_o, small_o,
-    av, ov, gb, n1, tokh, gm, ctx, q, kv, probs, gc, grads, near_g, far_g, got_g, lof, norm, part, rbuf,
+    av, ov, gb, n1, tokh, gm, ctx, q, kv, probs, gc, grads, near_g, far_g, got_g, lof, p2, mid, rbuf2, norm, part, rbuf,
     sm, tp_small, sib_small, all_small,
     r_sum, r_half, r_full, o_sum, o_half, o_full, a_sum, a_half, a_full,
     r_s, r_r, o_s, o_r, a_s, a_r,
@@ -996,39 +986,32 @@
     here.greet_signal()
     mine = pl.ds(al(here.side * half, half), half)
     pairs = [
-        (gb_i, gb), (full_o, ov), (pr_i, r_sum), (q_i, q), (kv_i, kv), (probs_i, probs), (ctx_i, ctx),
+        (gb_i, gb), (full_o, ov), (p2_i, p2), (mid_i, mid), (pr_i, r_sum), (q_i, q), (kv_i, kv), (probs_i, probs), (ctx_i, ctx),
         (full_a, av), (n1_i, n1), (gm_i, gm), (tok.at[mine], tokh),
     ]
     loads = [pltpu.make_async_copy(s, d, in_sem.at[i]) for i, (s, d) in enumerate(pairs)]
     for load in loads:
         load.start()
     end = (here.t == 0) | (here.t == n_t - 1)
-    lo_load = pltpu.make_async_copy(lo_i, lof.at[mine], in_sem.at[len(pairs)])
-    pl.when(end)(lo_load.start)
     sm[...] = sums_i[...]
     loads[0].wait()
     loads[1].wait()
     gc[...] = dot_nt(gb[...], ov[...]).astype(BF)
-    pl.when(end)(lo_load.wait)
-    loads[2].wait()
+    for load in loads[2:5]:
+        load.wait()
     here.greet_wait()
+    alive = live[0].astype(F32)
     outs = Outs(out_sem)
     line = Line(here, part, rbuf, norm, (ls_s, ls_r, lg_s, lg_r), chunks, lag)
-    back = Line(here, lof, rbuf, lof, (ms_s, ms_r, mg_s, mg_r), chunks2, lag2)
-
-    @pl.when(end)
-    def _():
-        def send(j, _):
-            back.back_copy(j).start()
-            return 0
-
-        lax.fori_loop(0, chunks2, send, 0)
-
-    back_ticks = chunks2 + lag2 * (n_t - 1)
+    back = Line(here, p2, rbuf2, lof, (ms_s, ms_r, mg_s, mg_r), chunks2, lag2)
+
+    back_ticks = back.ticks()
+
+    def final2(rows, span, total):
+        lof[rows, :] = ((mid[span, :] + total + par[5:6, :]) * alive).astype(BF)
 
     def back_tick(tau):
-        back.gather_step(0, tau, 0)
-        back.gather_step(1, tau, 0)
+        back.tick(tau, final2)
 
     def cols_of(i):
         return pl.ds(al(i * shard, shard), shard)
@@ -1040,7 +1023,7 @@
     os = Scatter(here, o_sum, lambda i: ov.at[:, cols_of(i)], o_half, o_full, o_s, o_r, 128)
     sa = Scatter(here, a_sum, lambda i: av.at[rows_of(i)], a_half, a_full, a_s, a_r, 64)
     rs.launch(here.m)
-    for load in loads[3:7]:
+    for load in loads[5:9]:
         load.wait()
 
     def head(h, _):
@@ -1096,22 +1079,26 @@
         rows = pl.ds(al(i * 128, 128), 128)
         low = (near_g[rows, :] + got_g[rows, :].astype(F32)).astype(BF)
         grads[rows, width:] = low
+        back_tick(3 * heads + i)
         both = jnp.concatenate([grads[rows, 0:width], low[:, width:]], axis=1).astype(F32)
         return total + jnp.sum(both, axis=0, keepdims=True)
 
     sm[3:4, 0 : 2 * width] = lax.fori_loop(
         0, rows_all // 128, add_rows, jnp.zeros((1, 2 * width), F32)
     )
-    loads[7].wait()
+    loads[9].wait()
     wide = model // 4
 
     def back_part(i, _):
         cols = pl.ds(al(i * wide, wide), wide)
         part[:, cols] = dot_nt(grads[...], av[cols, :]).astype(BF)
+        back_tick(first + i)
         return 0
 
+    first = 3 * heads + rows_all // 128
+
     lax.fori_loop(0, 4, back_part, 0)
-    for load in loads[8:]:
+    for load in loads[10:]:
         load.wait()
 
     def final(rows, span, total):
@@ -1156,7 +1143,7 @@
         span_when(tau, d, d + n_f, out_other)
         span_when(tau, d + n_f, full, out_own)
         pl.when(tau == d + n_f)(lambda: os.launch(here.m))
-        back_tick(3 * heads + tau)
+        back_tick(first + 4 + tau)
         for at, event in plan:
             pl.when(tau == at)(event)
         return 0
@@ -1169,7 +1156,7 @@
         back_tick(tau)
         return 0
 
-    lax.fori_loop(min(3 * heads + ticks, back_ticks), back_ticks, rest, 0)
+    lax.fori_loop(min(first + 4 + ticks, back_ticks), back_ticks, rest, 0)
     outs.put(lof, lo_o)
 
     def tp_copy(k):
@@ -1227,6 +1214,7 @@
     outs.put(sib_small, small_o)
     line.finish_sum()
     line.finish_back()
+    back.finish_sum()
     back.finish_back()
     rs.finish(False)
     os.finish()
@@ -1249,8 +1237,8 @@
 
 
 def backward(
-    n_f, n_t, par, sums, tok, gm, lo, gb, ctx, q, kv, probs, n1, full_a, full_o, pr,
-    chunks=16, lag=2, chunks2=8, lag2=2,
+    n_f, n_t, live, par, sums, tok, gm, mid, p2, gb, ctx, q, kv, probs, n1, full_a, full_o, pr,
+    chunks=16, lag=2, chunks2=16, lag2=2,
 ):
     rows, model = gb.shape
     width, ff = q.shape[1], pr.shape[1]
@@ -1267,7 +1255,7 @@
     return pl.pallas_call(
         functools.partial(backward_kernel, n_f, n_t, chunks, lag, chunks2, lag2),
         out_shape=outs,
-        in_specs=[VM] * 2 + [ANY] * 12,
+        in_specs=[pl.BlockSpec(memory_space=pltpu.SMEM)] + [VM] * 2 + [ANY] * 13,
         out_specs=(ANY,) * len(outs),
         scratch_shapes=[
             v((model, 3 * width), BF), v((width, model), BF), v((rows, model), BF),
@@ -1276,6 +1264,7 @@
             v((width // HD, rows, 2 * rows), BF),
             v((rows, width), BF), v((rows, 3 * width), BF), v((rows, 2 * width), F32),
             v((rows, 2 * width), BF), v((rows, 2 * width), BF), v((rows, model), BF),
+            v((rows, model), BF), v((rows // 2, model), F32), v((2, rows // 2, model), BF),
             v((rows, model), BF), v((rows, model), BF), v((2, rows // 2, model), BF),
             v((8, model), F32), v((2, 8, model), F32), v((8, model), F32),
             v((n_f, 8, model), F32),
@@ -1287,7 +1276,7 @@
         + Line.sems(chunks)
         + Line.sems(chunks2)
         + [dma((1,)), dma((1,)), dma((n_t - 1,)), dma((2,)), dma((1,)), dma((1,))]
-        + [dma((n_f,)), dma((n_f,)), dma((12,)), dma((6,))],
+        + [dma((n_f,)), dma((n_f,)), dma((13,)), dma((6,))],
         compiler_params=pltpu.CompilerParams(
             collective_id=2, has_side_effects=True, vmem_limit_bytes=63 << 20
         ),
@@ -1295,7 +1284,7 @@
             flops=14 * 10**9, bytes_accessed=40 * 10**6, transcendentals=4 * 10**6
         ),
         name="attention_backward",
-    )(par, sums, tok, gm, lo, gb, ctx, q, kv, probs, n1, full_a, full_o, pr)
+    )(live, par, sums, tok, gm, mid, p2, gb, ctx, q, kv, probs, n1, full_a, full_o, pr)
 
 
 def finish_kernel(
@@ -1399,11 +1388,11 @@
         n_f, n_t, tok, block_ids, vectors, (query_bias, value_bias, expand_bias),
         query_weight, key_weight, value_weight, output_weight, expand_weight, reduce_weight,
     )
-    gb, lo, gm, e_grad, r_part, sums = middle(
+    gb, p2, gm, e_grad, r_part, sums = middle(
         n_f, n_t, live_count, n2, cotangent.reshape(rows, model), mid, par, full_e, full_r, reduce_weight
     )
     lo, tg, r_grad, o_grad, a_grad, total = backward(
-        n_f, n_t, par, sums, tok, gm, lo, gb, ctx, q, kv, probs, n1, full_a, full_o, r_part
+        n_f, n_t, live_count, par, sums, tok, gm, mid, p2, gb, ctx, q, kv, probs, n1, full_a, full_o, r_part
     )
     (
         layer_out, tokens_grad, e_grad, r_grad, q_grad, k_grad, v_grad, o_grad,

time: 363 us -> 352 us (0.970)
  Pallas kernels: 361 us -> 351 us
    pallas_call x1, Pallas kernels: 115 us -> 91.6 us  [middle(): pl.pallas_call(functools.partial(middle_kernel, n_f, n_t, chunks, lag), o...]
    pallas_call x1, Pallas kernels: 113 us -> 125 us  [backward(): pl.pallas_call(functools.partial(backward_kernel, n_f, n_t, chunks, lag,...]
where the time goes in v5:
time: 352 us
  Pallas kernels  351 us (100%)
    pallas_call x1, Pallas kernels, backward(): pl.pallas_call(functools.partial(backward_kernel, n_f, n_t, chunks, lag,...  125 us
    pallas_call x1, Pallas kernels, forward(): pl.pallas_call(functools.partial(forward_kernel, n_f, n_t, chunks, lag),...  125 us
    pallas_call x1, Pallas kernels, middle(): pl.pallas_call(functools.partial(middle_kernel, n_f, n_t, chunks, lag), o...  91.6 us
    pallas_call x1, Pallas kernels, finish(): pl.pallas_call(functools.partial(finish_kernel, n_f), out_shape=outs, in_...  8.61 us

profile of v5, /device:TPU:0, one launch (start us, length us, event | category | flops | bytes accessed | tf_op | source)
XLA Modules:
  0.0 352.0 jit_solution(10864996387081655211)
XLA Ops:
  1.3 125.0 %attention_forward.1 = (bf16[512,2048]{1,0:T(8,128)(2,1)}, bf16[512,512]{1,0:T(8,128)(2,1)}, bf16[2,512,1024]{2,1,0:T(8,128)(2,1)}, bf16[512,512]{1,0:T(8,128)(2...) custom-call(bf16[512,2048]{1,0:T(8,128)(2,1)} %bitcast.9, ...), custom_call_target="tpu_custom_call" | custom-call | flops 8000000000 | bytes 60000000 | tf_op jit(solution)/shard_map/attention_forward/pallas_call | solution.py:592
  126.3 91.6 %feed_forward.1 = (bf16[512,2048]{1,0:T(8,128)(2,1)}, bf16[512,2048]{1,0:T(8,128)(2,1)}, f32[256,2048]{1,0:T(8,128)}, bf16[256,2048]{1,0:T(8,128)(2,1)}, bf16[4,...) custom-call(s32[1]{0:T(128)S(6)} %copy.36.live, bf16[512,2048]{1,0:T(8,128)(2,1)} %get-tuple-element.59.n2_i, ...), custom_call_target="tpu_custom_call" | custom-call | flops 25999998976 | bytes 40000000 | tf_op jit(solution)/shard_map/feed_forward/pallas_call | solution.py:939
  217.9 125.3 %attention_backward.1 = (bf16[512,2048]{1,0:T(8,128)(2,1)}, bf16[512,2048]{1,0:T(8,128)(2,1)}, bf16[2048,256]{1,0:T(8,128)(2,1)}, bf16[512,256]{1,0:T(8,128)(2,1...) custom-call(s32[1]{0:T(128)S(6)} %copy.36.live, f32[8,2048]{1,0:T(8,128)} %get-tuple-element.58.par, ...), custom_call_target="tpu_custom_call" | custom-call | flops 14000000000 | bytes 40000000 | tf_op jit(solution)/shard_map/attention_backward/pallas_call | solution.py:1255
  343.2 8.6 %finish.1 = (bf16[1,512,2048]{2,1,0:T(8,128)(2,1)}, bf16[1,512,2048]{2,1,0:T(8,128)(2,1)}, f32[256,2048]{1,0:T(8,128)}, f32[2048,256]{1,0:T(8,128)}, f32[256,512...) custom-call(f32[8,2048]{1,0:T(8,128)} %get-tuple-element.75.total, ...), custom_call_target="tpu_custom_call" | custom-call | flops 1000000 | bytes 18000000 | tf_op jit(solution)/shard_map/finish/pallas_call | solution.py:1364

commit v6 on v5

--- a/solution.py
+++ b/solution.py
@@ -1046,8 +1046,8 @@
         far_g[:, kc] = (dot_tn(gs_far, qh) * scale).astype(BF)
         near_g[:, vc] = near_gv
         far_g[:, vc] = far_gv.astype(BF)
-        for k in range(3):
-            back_tick(3 * h + k)
+        for k in range(5):
+            back_tick(5 * h + k)
 
         @pl.when(h == heads // 2)
         def _():
@@ -1079,7 +1079,7 @@
         rows = pl.ds(al(i * 128, 128), 128)
         low = (near_g[rows, :] + got_g[rows, :].astype(F32)).astype(BF)
         grads[rows, width:] = low
-        back_tick(3 * heads + i)
+        back_tick(5 * heads + i)
         both = jnp.concatenate([grads[rows, 0:width], low[:, width:]], axis=1).astype(F32)
         return total + jnp.sum(both, axis=0, keepdims=True)
 
@@ -1095,7 +1095,7 @@
         back_tick(first + i)
         return 0
 
-    first = 3 * heads + rows_all // 128
+    first = 5 * heads + rows_all // 128
 
     lax.fori_loop(0, 4, back_part, 0)
     for load in loads[10:]:

time: 352 us -> 366 us (1.040)
  Pallas kernels: 351 us -> 364 us
    pallas_call x1, Pallas kernels: 125 us -> 139 us  [backward(): pl.pallas_call(functools.partial(backward_kernel, n_f, n_t, chunks, lag,...]
where the time goes in v6:
time: 366 us
  Pallas kernels  364 us (99%)
    pallas_call x1, Pallas kernels, backward(): pl.pallas_call(functools.partial(backward_kernel, n_f, n_t, chunks, lag,...  139 us
    pallas_call x1, Pallas kernels, forward(): pl.pallas_call(functools.partial(forward_kernel, n_f, n_t, chunks, lag),...  125 us
    pallas_call x1, Pallas kernels, middle(): pl.pallas_call(functools.partial(middle_kernel, n_f, n_t, chunks, lag), o...  91.6 us
    pallas_call x1, Pallas kernels, finish(): pl.pallas_call(functools.partial(finish_kernel, n_f), out_shape=outs, in_...  8.61 us

profile of v6, /device:TPU:0, one launch (start us, length us, event | category | flops | bytes accessed | tf_op | source)
XLA Modules:
  0.0 365.6 jit_solution(1153712362239746307)
XLA Ops:
  1.3 125.0 %attention_forward.1 = (bf16[512,2048]{1,0:T(8,128)(2,1)}, bf16[512,512]{1,0:T(8,128)(2,1)}, bf16[2,512,1024]{2,1,0:T(8,128)(2,1)}, bf16[512,512]{1,0:T(8,128)(2...) custom-call(bf16[512,2048]{1,0:T(8,128)(2,1)} %bitcast.9, ...), custom_call_target="tpu_custom_call" | custom-call | flops 8000000000 | bytes 60000000 | tf_op jit(solution)/shard_map/attention_forward/pallas_call | solution.py:592
  126.3 91.6 %feed_forward.1 = (bf16[512,2048]{1,0:T(8,128)(2,1)}, bf16[512,2048]{1,0:T(8,128)(2,1)}, f32[256,2048]{1,0:T(8,128)}, bf16[256,2048]{1,0:T(8,128)(2,1)}, bf16[4,...) custom-call(s32[1]{0:T(128)S(6)} %copy.36.live, bf16[512,2048]{1,0:T(8,128)(2,1)} %get-tuple-element.59.n2_i, ...), custom_call_target="tpu_custom_call" | custom-call | flops 25999998976 | bytes 40000000 | tf_op jit(solution)/shard_map/feed_forward/pallas_call | solution.py:939
  217.9 138.9 %attention_backward.1 = (bf16[512,2048]{1,0:T(8,128)(2,1)}, bf16[512,2048]{1,0:T(8,128)(2,1)}, bf16[2048,256]{1,0:T(8,128)(2,1)}, bf16[512,256]{1,0:T(8,128)(2,1...) custom-call(s32[1]{0:T(128)S(6)} %copy.36.live, f32[8,2048]{1,0:T(8,128)} %get-tuple-element.58.par, ...), custom_call_target="tpu_custom_call" | custom-call | flops 14000000000 | bytes 40000000 | tf_op jit(solution)/shard_map/attention_backward/pallas_call | solution.py:1255
  356.8 8.6 %finish.1 = (bf16[1,512,2048]{2,1,0:T(8,128)(2,1)}, bf16[1,512,2048]{2,1,0:T(8,128)(2,1)}, f32[256,2048]{1,0:T(8,128)}, f32[2048,256]{1,0:T(8,128)}, f32[256,512...) custom-call(f32[8,2048]{1,0:T(8,128)} %get-tuple-element.75.total, ...), custom_call_target="tpu_custom_call" | custom-call | flops 1000000 | bytes 18000000 | tf_op jit(solution)/shard_map/finish/pallas_call | solution.py:1364
